TPU v7x, 32 devices: a whole 2x2x4 slice. The times are simulated.
32 devices in a mesh: section: 4 (over y, core), rep: 2 (over x), tp: 4 (over z).
Axes of the slice: x: 2, y: 2, z: 4, core: 2. Of those that a mesh axis runs over, the one named last changes fastest.
Arguments:
- token_ids: int32 [2, 8, 128], P('rep', None, 'tp'), may hold values from 0 to 16383
- embed: bfloat16 [16384, 1024], P('section'), may hold values from -6 to 6
- w_in: bfloat16 [2, 4, 2, 1024, 2816], P('rep', 'section', None, None, 'tp'), may hold values from -0.1875 to 0.1875
- w_down: bfloat16 [2, 4, 2816, 1024], P('rep', 'section', 'tp'), may hold values from -0.109375 to 0.109375
- outer_in: float32 [4, 2, 1024, 2816], P('section', None, None, 'tp'), may hold values from -0.1875 to 0.1875
- outer_down: float32 [4, 2816, 1024], P('section', 'tp'), may hold values from -0.109375 to 0.109375
- moment_in: float32 [4, 2, 1024, 2816], P('section', None, None, 'tp'), may hold values from -0.12 to 0.12
- moment_down: float32 [4, 2816, 1024], P('section', 'tp'), may hold values from -0.12 to 0.12
- cotangent: bfloat16 [2, 8, 128, 1024], P('rep', None, 'tp'), may hold values from -6 to 6
- fragment: int32 [4], replicated, may hold values 0 or 1
Outputs:
- new_in: bfloat16 [2, 4, 2, 1024, 2816], P('rep', 'section', None, None, 'tp')
- new_down: bfloat16 [2, 4, 2816, 1024], P('rep', 'section', 'tp')
- next_outer_in: float32 [4, 2, 1024, 2816], P('section', None, None, 'tp')
- next_outer_down: float32 [4, 2816, 1024], P('section', 'tp')
- next_moment_in: float32 [4, 2, 1024, 2816], P('section', None, None, 'tp')
- next_moment_down: float32 [4, 2816, 1024], P('section', 'tp')
All inputs are finite; a program needn't handle non-finite values.
Results may differ from a plain program's by a relative error of at most 0.03.
Values may be sent and summed in bfloat16 or wider, within the bound.
No kernel may reach another device: no remote copies, remote signals or barrier semaphores. Data moves between devices by JAX's collectives and lax.ppermute only.
A program may use at most 128 MiB of HBM per device.

v0:
```python
import jax
import jax.numpy as jnp
from jax import lax
from jax.sharding import PartitionSpec as P

EPS = 1e-05
INNER_LR = 0.001
OUTER_LR = 0.7
MOMENTUM = 0.9


def from_behind(value, axis, steps):
    count = lax.axis_size(axis)
    initial, last = (max(0, -steps), min(count, count - steps))
    return lax.ppermute(value, axis, [(source, source + steps) for source in range(initial, last)])


def scale_rows(values):
    return lax.rsqrt(jnp.mean(values * values, axis=-1, keepdims=True) + EPS)


def gather_rows(values):
    return lax.all_gather(values, "tp", axis=0, tiled=True)


def pass_along(values, step):
    return from_behind(values, "section", step)


def reduce_rows(left, right, form):
    return lax.psum_scatter(
        jnp.einsum(form, left, right, preferred_element_type=jnp.float32),
        "tp",
        scatter_dimension=0,
        tiled=True,
    )


def layer_forward(x_own, pair, down):
    full = gather_rows(x_own).astype(jnp.float32)
    normed = (full * scale_rows(full)).astype(jnp.bfloat16)
    gate_up = jnp.einsum("td,kdf->tkf", normed, pair, preferred_element_type=jnp.float32)
    hidden = (jax.nn.silu(gate_up[:, 0]) * gate_up[:, 1]).astype(jnp.bfloat16)
    out = reduce_rows(hidden, down, "tf,fd->td")
    return ((x_own.astype(jnp.float32) + out).astype(jnp.bfloat16), normed, gate_up)


def layer_backward(grad_own, x_own, pair, down, normed, gate_up):
    grad_full = gather_rows(grad_own)
    d_hidden = jnp.einsum("td,fd->tf", grad_full, down, preferred_element_type=jnp.float32)
    gate = gate_up[:, 0]
    upper = gate_up[:, 1]
    sig = jax.nn.sigmoid(gate)
    active = jax.nn.silu(gate)
    hidden = (active * upper).astype(jnp.bfloat16)
    d_both = jnp.stack(
        [d_hidden * upper * sig * (1.0 + gate * (1.0 - sig)), d_hidden * active], axis=1
    ).astype(jnp.bfloat16)
    g_down = jnp.einsum("tf,td->fd", hidden, grad_full, preferred_element_type=jnp.float32)
    g_pair = jnp.einsum("td,tkf->kdf", normed, d_both, preferred_element_type=jnp.float32)
    d_norm = reduce_rows(d_both, pair, "tkf,kdf->td")
    xf = x_own.astype(jnp.float32)
    rinv = scale_rows(xf)
    d_x = (
        grad_own.astype(jnp.float32)
        + rinv * d_norm
        - xf * (rinv * rinv * rinv) * jnp.mean(d_norm * xf, axis=-1, keepdims=True)
    )
    return (d_x.astype(jnp.bfloat16), g_pair, g_down)


def shards(
    token_ids,
    embed,
    w_in,
    w_down,
    outer_in,
    outer_down,
    moment_in,
    moment_down,
    cotangent,
    fragment,
):
    sections = lax.axis_size("section")
    section = lax.axis_index("section")
    replicas = lax.axis_size("rep")
    ids = token_ids[0]
    batches, own_rows = ids.shape
    vocab_part, width = embed.shape
    local_ids = ids - section * vocab_part
    inside = (local_ids >= 0) & (local_ids < vocab_part)
    looked = jnp.take(embed, jnp.clip(local_ids, 0, vocab_part - 1), axis=0).astype(jnp.float32)
    looked = jnp.where(inside[:, :, None], looked, 0.0)
    start_rows = lax.psum(looked.astype(jnp.bfloat16), "section")
    pairs = w_in[0]
    downs = w_down[0]
    depth = pairs.shape[0]
    hidden_width = pairs.shape[-1]
    total_rows = own_rows * lax.axis_size("tp")
    ticks = batches + sections - 1
    first = section == 0
    final = section == sections - 1

    def forward_tick(tick, carry):
        inbox, x_store, normed_store, gate_store = carry
        micro = tick - section
        valid = (micro >= 0) & (micro < batches)
        slot = jnp.where(valid, micro, batches)
        feed = lax.dynamic_index_in_dim(
            start_rows, jnp.clip(tick, 0, batches - 1).astype(jnp.int32), 0, keepdims=False
        )
        current = jnp.where(first, feed, inbox)
        zero = jnp.zeros((), jnp.int32)
        x_store = lax.dynamic_update_slice(
            x_store, current[None, None], (slot, zero + 0, zero, zero)
        )
        current, normed, gate_up = layer_forward(current, pairs[0], downs[0])
        normed_store = lax.dynamic_update_slice(
            normed_store, normed[None, None], (slot, zero + 0, zero, zero)
        )
        gate_store = lax.dynamic_update_slice(
            gate_store, gate_up[None, None], (slot, zero + 0, zero, zero, zero)
        )
        return (pass_along(current, 1), x_store, normed_store, gate_store)

    start_carry = (
        jnp.zeros((own_rows, width), jnp.bfloat16),
        jnp.zeros((batches + 1, depth, own_rows, width), jnp.bfloat16),
        jnp.zeros((batches + 1, depth, total_rows, width), jnp.bfloat16),
        jnp.zeros((batches + 1, depth, total_rows, 2, hidden_width), jnp.float32),
    )
    _, x_store, normed_store, gate_store = lax.fori_loop(0, ticks, forward_tick, start_carry)
    seeds = cotangent[0]

    def backward_tick(tick, carry):
        inbox, acc_pair, acc_down = carry
        micro = tick - (sections - 1 - section)
        valid = (micro >= 0) & (micro < batches)
        index = jnp.clip(micro, 0, batches - 1)
        feed = lax.dynamic_index_in_dim(seeds, index, 0, keepdims=False)
        grad = jnp.where(final, feed, inbox)
        grad = jnp.where(valid, grad, jnp.zeros_like(grad))
        zero = jnp.zeros((), jnp.int32)
        for layer in reversed(range(depth)):
            x_own = lax.dynamic_slice(
                x_store, (index, zero + layer, zero, zero), (1, 1, own_rows, width)
            )[0, 0]
            normed = lax.dynamic_slice(
                normed_store, (index, zero + layer, zero, zero), (1, 1, total_rows, width)
            )[0, 0]
            gate_up = lax.dynamic_slice(
                gate_store,
                (index, zero + layer, zero, zero, zero),
                (1, 1, total_rows, 2, hidden_width),
            )[0, 0]
            grad, g_pair, g_down = layer_backward(
                grad, x_own, pairs[layer], downs[layer], normed, gate_up
            )
            acc_pair = acc_pair.at[layer].add(g_pair)
            acc_down = acc_down.at[layer].add(g_down)
        return (pass_along(grad, -1), acc_pair, acc_down)

    back_carry = (
        jnp.zeros((own_rows, width), jnp.bfloat16),
        jnp.zeros(pairs.shape, jnp.float32),
        jnp.zeros(downs.shape, jnp.float32),
    )
    _, acc_pair, acc_down = lax.fori_loop(0, ticks, backward_tick, back_carry)
    new_pair = (pairs.astype(jnp.float32) - INNER_LR * acc_pair).astype(jnp.bfloat16)
    new_out = (downs.astype(jnp.float32) - INNER_LR * acc_down).astype(jnp.bfloat16)
    every_pair, every_down = (
        lax.all_gather(new_pair[None], "rep", axis=0, tiled=True),
        lax.all_gather(new_out[None], "rep", axis=0, tiled=True),
    )
    sum_pair = jnp.sum(every_pair.astype(jnp.float32), axis=0)
    sum_down = jnp.sum(every_down.astype(jnp.float32), axis=0)
    mean_pair = outer_in - sum_pair / replicas
    mean_down = outer_down - sum_down / replicas
    flag = lax.dynamic_index_in_dim(fragment, section, 0, keepdims=False)
    chosen = flag == 1
    moment_pair = MOMENTUM * moment_in + mean_pair
    moment_out = MOMENTUM * moment_down + mean_down
    outer_pair = outer_in - OUTER_LR * (mean_pair + MOMENTUM * moment_pair)
    outer_out = outer_down - OUTER_LR * (mean_down + MOMENTUM * moment_out)
    result_pair = jnp.where(chosen, outer_pair.astype(jnp.bfloat16), new_pair)
    result_down = jnp.where(chosen, outer_out.astype(jnp.bfloat16), new_out)
    return (
        result_pair[None],
        result_down[None],
        jnp.where(chosen, outer_pair, outer_in),
        jnp.where(chosen, outer_out, outer_down),
        jnp.where(chosen, moment_pair, moment_in),
        jnp.where(chosen, moment_out, moment_down),
    )


def solution(mesh):
    return jax.shard_map(
        shards,
        mesh=mesh,
        in_specs=(
            P("rep", None, "tp"),
            P("section", None),
            P("rep", "section", None, None, "tp"),
            P("rep", "section", "tp", None),
            P("section", None, None, "tp"),
            P("section", "tp", None),
            P("section", None, None, "tp"),
            P("section", "tp", None),
            P("rep", None, "tp", None),
            P(),
        ),
        out_specs=(
            P("rep", "section", None, None, "tp"),
            P("rep", "section", "tp", None),
            P("section", None, None, "tp"),
            P("section", "tp", None),
            P("section", None, None, "tp"),
            P("section", "tp", None),
        ),
        check_vma=False,
    )
```

profile of v0, /device:TPU:0, one launch (start us, length us, event | category | flops | bytes accessed | tf_op | source)
XLA Modules:
  0.0 1249.5 jit_solution(3856151392380230476)
XLA Ops:
  16.5 36.3 %all-reduce.2.cloned.1.call-done = bf16[8,32,1024]{2,1,0:T(8,128)(2,1)} async-done(((bf16[8,32,1024]{2,1,0:T(8,128)(2,1)}), bf16[8,32,1024]{2,1,0:T(8,128)(2,1)}) %all-reduce.2.cloned.1.call-update) | async-done | bytes 524304 | tf_op jit(solution)/shard_map/psum | solution.py:94
  58.9 500.8 %while.42 = (s32[]{:T(128)}, bf16[32,1024]{1,0:T(8,128)(2,1)S(1)}, bf16[9,1,32,1024]{3,2,1,0:T(8,128)(2,1)}, bf16[9,1,128,1024]{3,2,1,0:T(8,128)(2,1)}, f32[9,1,...) while((s32[]{:T(128)}, bf16[32,1024]{1,0:T(8,128)(2,1)S(1)}, ...), condition=%wide.region_4.5_spmd, body=%wide.region_1.4_spmd.sunk | while | flops 555499648 | bytes 16911728 | solution.py:132
  77.7 22.5 %reduce-scatter.3.cloned.1.call-done = f32[32,1024]{1,0:T(8,128)} async-done(((f32[128,1024]{1,0:T(8,128)}), f32[32,1024]{1,0:T(8,128)}) %reduce-scatter.3.cloned.1.call-update) | async-done | bytes 131088 | tf_op jit(solution)/shard_map/while/body/eval_jaxpr/reduce_scatter | solution.py:31
  104.8 14.5 %all_gather.29 = bf16[128,1024]{1,0:T(8,128)(2,1)S(1)} all-gather(bf16[32,1024]{1,0:T(8,128)(2,1)S(1)} %get-tuple-element.782), channel_id=1, replica_groups=mesh['section'=4,'rep'=2,'tp'=4] {'tp'}, dimensions={0}, use_global_device_ids=true | all-gather | bytes 327680 | tf_op jit(solution)/shard_map/while/body/eval_jaxpr/all_gather | solution.py:23
  122.6 23.1 %reduce-scatter.3.cloned.1.call-done = f32[32,1024]{1,0:T(8,128)} async-done(((f32[128,1024]{1,0:T(8,128)}), f32[32,1024]{1,0:T(8,128)}) %reduce-scatter.3.cloned.1.call-update) | async-done | bytes 131088 | tf_op jit(solution)/shard_map/while/body/eval_jaxpr/reduce_scatter | solution.py:31
  150.5 14.5 %all_gather.29 = bf16[128,1024]{1,0:T(8,128)(2,1)S(1)} all-gather(bf16[32,1024]{1,0:T(8,128)(2,1)S(1)} %get-tuple-element.782), channel_id=1, replica_groups=mesh['section'=4,'rep'=2,'tp'=4] {'tp'}, dimensions={0}, use_global_device_ids=true | all-gather | bytes 327680 | tf_op jit(solution)/shard_map/while/body/eval_jaxpr/all_gather | solution.py:23
  168.2 23.2 %reduce-scatter.3.cloned.1.call-done = f32[32,1024]{1,0:T(8,128)} async-done(((f32[128,1024]{1,0:T(8,128)}), f32[32,1024]{1,0:T(8,128)}) %reduce-scatter.3.cloned.1.call-update) | async-done | bytes 131088 | tf_op jit(solution)/shard_map/while/body/eval_jaxpr/reduce_scatter | solution.py:31
  196.1 14.5 %all_gather.29 = bf16[128,1024]{1,0:T(8,128)(2,1)S(1)} all-gather(bf16[32,1024]{1,0:T(8,128)(2,1)S(1)} %get-tuple-element.782), channel_id=1, replica_groups=mesh['section'=4,'rep'=2,'tp'=4] {'tp'}, dimensions={0}, use_global_device_ids=true | all-gather | bytes 327680 | tf_op jit(solution)/shard_map/while/body/eval_jaxpr/all_gather | solution.py:23
  213.9 23.2 %reduce-scatter.3.cloned.1.call-done = f32[32,1024]{1,0:T(8,128)} async-done(((f32[128,1024]{1,0:T(8,128)}), f32[32,1024]{1,0:T(8,128)}) %reduce-scatter.3.cloned.1.call-update) | async-done | bytes 131088 | tf_op jit(solution)/shard_map/while/body/eval_jaxpr/reduce_scatter | solution.py:31
  241.8 14.5 %all_gather.29 = bf16[128,1024]{1,0:T(8,128)(2,1)S(1)} all-gather(bf16[32,1024]{1,0:T(8,128)(2,1)S(1)} %get-tuple-element.782), channel_id=1, replica_groups=mesh['section'=4,'rep'=2,'tp'=4] {'tp'}, dimensions={0}, use_global_device_ids=true | all-gather | bytes 327680 | tf_op jit(solution)/shard_map/while/body/eval_jaxpr/all_gather | solution.py:23
  259.6 23.2 %reduce-scatter.3.cloned.1.call-done = f32[32,1024]{1,0:T(8,128)} async-done(((f32[128,1024]{1,0:T(8,128)}), f32[32,1024]{1,0:T(8,128)}) %reduce-scatter.3.cloned.1.call-update) | async-done | bytes 131088 | tf_op jit(solution)/shard_map/while/body/eval_jaxpr/reduce_scatter | solution.py:31
  287.5 14.5 %all_gather.29 = bf16[128,1024]{1,0:T(8,128)(2,1)S(1)} all-gather(bf16[32,1024]{1,0:T(8,128)(2,1)S(1)} %get-tuple-element.782), channel_id=1, replica_groups=mesh['section'=4,'rep'=2,'tp'=4] {'tp'}, dimensions={0}, use_global_device_ids=true | all-gather | bytes 327680 | tf_op jit(solution)/shard_map/while/body/eval_jaxpr/all_gather | solution.py:23
  305.2 23.2 %reduce-scatter.3.cloned.1.call-done = f32[32,1024]{1,0:T(8,128)} async-done(((f32[128,1024]{1,0:T(8,128)}), f32[32,1024]{1,0:T(8,128)}) %reduce-scatter.3.cloned.1.call-update) | async-done | bytes 131088 | tf_op jit(solution)/shard_map/while/body/eval_jaxpr/reduce_scatter | solution.py:31
  333.2 14.5 %all_gather.29 = bf16[128,1024]{1,0:T(8,128)(2,1)S(1)} all-gather(bf16[32,1024]{1,0:T(8,128)(2,1)S(1)} %get-tuple-element.782), channel_id=1, replica_groups=mesh['section'=4,'rep'=2,'tp'=4] {'tp'}, dimensions={0}, use_global_device_ids=true | all-gather | bytes 327680 | tf_op jit(solution)/shard_map/while/body/eval_jaxpr/all_gather | solution.py:23
  350.9 23.1 %reduce-scatter.3.cloned.1.call-done = f32[32,1024]{1,0:T(8,128)} async-done(((f32[128,1024]{1,0:T(8,128)}), f32[32,1024]{1,0:T(8,128)}) %reduce-scatter.3.cloned.1.call-update) | async-done | bytes 131088 | tf_op jit(solution)/shard_map/while/body/eval_jaxpr/reduce_scatter | solution.py:31
  378.7 14.5 %all_gather.29 = bf16[128,1024]{1,0:T(8,128)(2,1)S(1)} all-gather(bf16[32,1024]{1,0:T(8,128)(2,1)S(1)} %get-tuple-element.782), channel_id=1, replica_groups=mesh['section'=4,'rep'=2,'tp'=4] {'tp'}, dimensions={0}, use_global_device_ids=true | all-gather | bytes 327680 | tf_op jit(solution)/shard_map/while/body/eval_jaxpr/all_gather | solution.py:23
  396.5 23.1 %reduce-scatter.3.cloned.1.call-done = f32[32,1024]{1,0:T(8,128)} async-done(((f32[128,1024]{1,0:T(8,128)}), f32[32,1024]{1,0:T(8,128)}) %reduce-scatter.3.cloned.1.call-update) | async-done | bytes 131088 | tf_op jit(solution)/shard_map/while/body/eval_jaxpr/reduce_scatter | solution.py:31
  424.3 14.5 %all_gather.29 = bf16[128,1024]{1,0:T(8,128)(2,1)S(1)} all-gather(bf16[32,1024]{1,0:T(8,128)(2,1)S(1)} %get-tuple-element.782), channel_id=1, replica_groups=mesh['section'=4,'rep'=2,'tp'=4] {'tp'}, dimensions={0}, use_global_device_ids=true | all-gather | bytes 327680 | tf_op jit(solution)/shard_map/while/body/eval_jaxpr/all_gather | solution.py:23
  442.1 23.1 %reduce-scatter.3.cloned.1.call-done = f32[32,1024]{1,0:T(8,128)} async-done(((f32[128,1024]{1,0:T(8,128)}), f32[32,1024]{1,0:T(8,128)}) %reduce-scatter.3.cloned.1.call-update) | async-done | bytes 131088 | tf_op jit(solution)/shard_map/while/body/eval_jaxpr/reduce_scatter | solution.py:31
  470.0 14.4 %all_gather.29 = bf16[128,1024]{1,0:T(8,128)(2,1)S(1)} all-gather(bf16[32,1024]{1,0:T(8,128)(2,1)S(1)} %get-tuple-element.782), channel_id=1, replica_groups=mesh['section'=4,'rep'=2,'tp'=4] {'tp'}, dimensions={0}, use_global_device_ids=true | all-gather | bytes 327680 | tf_op jit(solution)/shard_map/while/body/eval_jaxpr/all_gather | solution.py:23
  487.7 23.2 %reduce-scatter.3.cloned.1.call-done = f32[32,1024]{1,0:T(8,128)} async-done(((f32[128,1024]{1,0:T(8,128)}), f32[32,1024]{1,0:T(8,128)}) %reduce-scatter.3.cloned.1.call-update) | async-done | bytes 131088 | tf_op jit(solution)/shard_map/while/body/eval_jaxpr/reduce_scatter | solution.py:31
  515.6 14.5 %all_gather.29 = bf16[128,1024]{1,0:T(8,128)(2,1)S(1)} all-gather(bf16[32,1024]{1,0:T(8,128)(2,1)S(1)} %get-tuple-element.782), channel_id=1, replica_groups=mesh['section'=4,'rep'=2,'tp'=4] {'tp'}, dimensions={0}, use_global_device_ids=true | all-gather | bytes 327680 | tf_op jit(solution)/shard_map/while/body/eval_jaxpr/all_gather | solution.py:23
  533.4 23.2 %reduce-scatter.3.cloned.1.call-done = f32[32,1024]{1,0:T(8,128)} async-done(((f32[128,1024]{1,0:T(8,128)}), f32[32,1024]{1,0:T(8,128)}) %reduce-scatter.3.cloned.1.call-update) | async-done | bytes 131088 | tf_op jit(solution)/shard_map/while/body/eval_jaxpr/reduce_scatter | solution.py:31
  560.3 542.4 %while.43 = (s32[]{:T(128)}, bf16[32,1024]{1,0:T(8,128)(2,1)}, f32[1,2,1024,704]{2,3,1,0:T(8,128)}, f32[1,704,1024]{2,1,0:T(8,128)}, s32[]{:T(128)}, /*index=5*/...) while((s32[]{:T(128)}, bf16[32,1024]{1,0:T(8,128)(2,1)}, ...), condition=%wide.region_9.10_spmd.clone, body=%wide.region_5.9_spmd.clone.sunk | while | flops 1114185856 | bytes 33326708 | solution.py:168
  561.2 14.5 %all_gather.30 = bf16[128,1024]{1,0:T(8,128)(2,1)S(1)} all-gather(bf16[32,1024]{1,0:T(8,128)(2,1)S(1)} %fusion.66), channel_id=1, replica_groups=mesh['section'=4,'rep'=2,'tp'=4] {'tp'}, dimensions={0}, use_global_device_ids=true | all-gather | bytes 327680 | tf_op jit(solution)/shard_map/while/body/eval_jaxpr/all_gather | solution.py:23
  585.4 18.8 %reduce-scatter.5.cloned.1.call-done = f32[32,1024]{1,0:T(8,128)} async-done(((f32[128,1024]{1,0:T(8,128)}), f32[32,1024]{1,0:T(8,128)}) %reduce-scatter.5.cloned.1.call-update) | async-done | bytes 131088 | tf_op jit(solution)/shard_map/while/body/eval_jaxpr/reduce_scatter | solution.py:31
  611.7 14.5 %all_gather.30 = bf16[128,1024]{1,0:T(8,128)(2,1)S(1)} all-gather(bf16[32,1024]{1,0:T(8,128)(2,1)S(1)} %fusion.66), channel_id=1, replica_groups=mesh['section'=4,'rep'=2,'tp'=4] {'tp'}, dimensions={0}, use_global_device_ids=true | all-gather | bytes 327680 | tf_op jit(solution)/shard_map/while/body/eval_jaxpr/all_gather | solution.py:23
  637.8 14.6 %reduce-scatter.5.cloned.1.call-done = f32[32,1024]{1,0:T(8,128)} async-done(((f32[128,1024]{1,0:T(8,128)}), f32[32,1024]{1,0:T(8,128)}) %reduce-scatter.5.cloned.1.call-update) | async-done | bytes 131088 | tf_op jit(solution)/shard_map/while/body/eval_jaxpr/reduce_scatter | solution.py:31
  660.9 14.5 %all_gather.30 = bf16[128,1024]{1,0:T(8,128)(2,1)S(1)} all-gather(bf16[32,1024]{1,0:T(8,128)(2,1)S(1)} %fusion.66), channel_id=1, replica_groups=mesh['section'=4,'rep'=2,'tp'=4] {'tp'}, dimensions={0}, use_global_device_ids=true | all-gather | bytes 327680 | tf_op jit(solution)/shard_map/while/body/eval_jaxpr/all_gather | solution.py:23
  687.0 14.7 %reduce-scatter.5.cloned.1.call-done = f32[32,1024]{1,0:T(8,128)} async-done(((f32[128,1024]{1,0:T(8,128)}), f32[32,1024]{1,0:T(8,128)}) %reduce-scatter.5.cloned.1.call-update) | async-done | bytes 131088 | tf_op jit(solution)/shard_map/while/body/eval_jaxpr/reduce_scatter | solution.py:31
  710.2 14.5 %all_gather.30 = bf16[128,1024]{1,0:T(8,128)(2,1)S(1)} all-gather(bf16[32,1024]{1,0:T(8,128)(2,1)S(1)} %fusion.66), channel_id=1, replica_groups=mesh['section'=4,'rep'=2,'tp'=4] {'tp'}, dimensions={0}, use_global_device_ids=true | all-gather | bytes 327680 | tf_op jit(solution)/shard_map/while/body/eval_jaxpr/all_gather | solution.py:23
  736.2 14.7 %reduce-scatter.5.cloned.1.call-done = f32[32,1024]{1,0:T(8,128)} async-done(((f32[128,1024]{1,0:T(8,128)}), f32[32,1024]{1,0:T(8,128)}) %reduce-scatter.5.cloned.1.call-update) | async-done | bytes 131088 | tf_op jit(solution)/shard_map/while/body/eval_jaxpr/reduce_scatter | solution.py:31
  759.4 14.5 %all_gather.30 = bf16[128,1024]{1,0:T(8,128)(2,1)S(1)} all-gather(bf16[32,1024]{1,0:T(8,128)(2,1)S(1)} %fusion.66), channel_id=1, replica_groups=mesh['section'=4,'rep'=2,'tp'=4] {'tp'}, dimensions={0}, use_global_device_ids=true | all-gather | bytes 327680 | tf_op jit(solution)/shard_map/while/body/eval_jaxpr/all_gather | solution.py:23
  785.4 14.6 %reduce-scatter.5.cloned.1.call-done = f32[32,1024]{1,0:T(8,128)} async-done(((f32[128,1024]{1,0:T(8,128)}), f32[32,1024]{1,0:T(8,128)}) %reduce-scatter.5.cloned.1.call-update) | async-done | bytes 131088 | tf_op jit(solution)/shard_map/while/body/eval_jaxpr/reduce_scatter | solution.py:31
  808.6 14.5 %all_gather.30 = bf16[128,1024]{1,0:T(8,128)(2,1)S(1)} all-gather(bf16[32,1024]{1,0:T(8,128)(2,1)S(1)} %fusion.66), channel_id=1, replica_groups=mesh['section'=4,'rep'=2,'tp'=4] {'tp'}, dimensions={0}, use_global_device_ids=true | all-gather | bytes 327680 | tf_op jit(solution)/shard_map/while/body/eval_jaxpr/all_gather | solution.py:23
  834.6 14.6 %reduce-scatter.5.cloned.1.call-done = f32[32,1024]{1,0:T(8,128)} async-done(((f32[128,1024]{1,0:T(8,128)}), f32[32,1024]{1,0:T(8,128)}) %reduce-scatter.5.cloned.1.call-update) | async-done | bytes 131088 | tf_op jit(solution)/shard_map/while/body/eval_jaxpr/reduce_scatter | solution.py:31
  857.8 14.5 %all_gather.30 = bf16[128,1024]{1,0:T(8,128)(2,1)S(1)} all-gather(bf16[32,1024]{1,0:T(8,128)(2,1)S(1)} %fusion.66), channel_id=1, replica_groups=mesh['section'=4,'rep'=2,'tp'=4] {'tp'}, dimensions={0}, use_global_device_ids=true | all-gather | bytes 327680 | tf_op jit(solution)/shard_map/while/body/eval_jaxpr/all_gather | solution.py:23
  883.8 14.6 %reduce-scatter.5.cloned.1.call-done = f32[32,1024]{1,0:T(8,128)} async-done(((f32[128,1024]{1,0:T(8,128)}), f32[32,1024]{1,0:T(8,128)}) %reduce-scatter.5.cloned.1.call-update) | async-done | bytes 131088 | tf_op jit(solution)/shard_map/while/body/eval_jaxpr/reduce_scatter | solution.py:31
  906.9 14.5 %all_gather.30 = bf16[128,1024]{1,0:T(8,128)(2,1)S(1)} all-gather(bf16[32,1024]{1,0:T(8,128)(2,1)S(1)} %fusion.66), channel_id=1, replica_groups=mesh['section'=4,'rep'=2,'tp'=4] {'tp'}, dimensions={0}, use_global_device_ids=true | all-gather | bytes 327680 | tf_op jit(solution)/shard_map/while/body/eval_jaxpr/all_gather | solution.py:23
  932.9 14.7 %reduce-scatter.5.cloned.1.call-done = f32[32,1024]{1,0:T(8,128)} async-done(((f32[128,1024]{1,0:T(8,128)}), f32[32,1024]{1,0:T(8,128)}) %reduce-scatter.5.cloned.1.call-update) | async-done | bytes 131088 | tf_op jit(solution)/shard_map/while/body/eval_jaxpr/reduce_scatter | solution.py:31
  956.1 14.5 %all_gather.30 = bf16[128,1024]{1,0:T(8,128)(2,1)S(1)} all-gather(bf16[32,1024]{1,0:T(8,128)(2,1)S(1)} %fusion.66), channel_id=1, replica_groups=mesh['section'=4,'rep'=2,'tp'=4] {'tp'}, dimensions={0}, use_global_device_ids=true | all-gather | bytes 327680 | tf_op jit(solution)/shard_map/while/body/eval_jaxpr/all_gather | solution.py:23
  982.1 14.6 %reduce-scatter.5.cloned.1.call-done = f32[32,1024]{1,0:T(8,128)} async-done(((f32[128,1024]{1,0:T(8,128)}), f32[32,1024]{1,0:T(8,128)}) %reduce-scatter.5.cloned.1.call-update) | async-done | bytes 131088 | tf_op jit(solution)/shard_map/while/body/eval_jaxpr/reduce_scatter | solution.py:31
  1005.3 14.5 %all_gather.30 = bf16[128,1024]{1,0:T(8,128)(2,1)S(1)} all-gather(bf16[32,1024]{1,0:T(8,128)(2,1)S(1)} %fusion.66), channel_id=1, replica_groups=mesh['section'=4,'rep'=2,'tp'=4] {'tp'}, dimensions={0}, use_global_device_ids=true | all-gather | bytes 327680 | tf_op jit(solution)/shard_map/while/body/eval_jaxpr/all_gather | solution.py:23
  1031.3 14.6 %reduce-scatter.5.cloned.1.call-done = f32[32,1024]{1,0:T(8,128)} async-done(((f32[128,1024]{1,0:T(8,128)}), f32[32,1024]{1,0:T(8,128)}) %reduce-scatter.5.cloned.1.call-update) | async-done | bytes 131088 | tf_op jit(solution)/shard_map/while/body/eval_jaxpr/reduce_scatter | solution.py:31
  1054.4 14.5 %all_gather.30 = bf16[128,1024]{1,0:T(8,128)(2,1)S(1)} all-gather(bf16[32,1024]{1,0:T(8,128)(2,1)S(1)} %fusion.66), channel_id=1, replica_groups=mesh['section'=4,'rep'=2,'tp'=4] {'tp'}, dimensions={0}, use_global_device_ids=true | all-gather | bytes 327680 | tf_op jit(solution)/shard_map/while/body/eval_jaxpr/all_gather | solution.py:23
  1080.4 14.7 %reduce-scatter.5.cloned.1.call-done = f32[32,1024]{1,0:T(8,128)} async-done(((f32[128,1024]{1,0:T(8,128)}), f32[32,1024]{1,0:T(8,128)}) %reduce-scatter.5.cloned.1.call-update) | async-done | bytes 131088 | tf_op jit(solution)/shard_map/while/body/eval_jaxpr/reduce_scatter | solution.py:31
  1114.0 34.3 %all-gather.7.cloned.1.call-done = bf16[2,704,1024]{2,1,0:T(8,128)(2,1)} async-done(((bf16[1,704,1024]{2,1,0:T(8,128)(2,1)}), bf16[2,704,1024]{2,1,0:T(8,128)(2,1)}) %all-gather.7.cloned.1.call-update) | async-done | bytes 2883600 | tf_op jit(solution)/shard_map/all_gather | solution.py:173
  1160.5 64.4 %all-gather.5.cloned.1.call-done = bf16[2,2,1024,704]{2,3,1,0:T(8,128)(2,1)} async-done(((bf16[1,2,1024,704]{2,3,1,0:T(8,128)(2,1)}), bf16[2,2,1024,704]{2,3,1,0:T(8,128)(2,1)}) %all-gather.5.cloned.1.call-update) | async-done | bytes 5767184 | tf_op jit(solution)/shard_map/all_gather | solution.py:172
  (382 shorter events, 375.6 us)
Async XLA Ops:
  7.2 45.6 %all-reduce.2.cloned.1.call-start = ((), (), s32[]{:S(2)}) async-start(), calls=%async_computation.2 | async-start | bytes 1048576 | tf_op jit(solution)/shard_map/psum | solution.py:94
  58.9 41.3 %reduce-scatter.3.cloned.1.call-start = ((), (), s32[]{:S(2)}) async-start(), calls=%async_computation.5 | async-start | bytes 655360 | tf_op jit(solution)/shard_map/while/body/eval_jaxpr/reduce_scatter | solution.py:31
  101.0 2.2 collective-permute-start
  103.2 42.5 %reduce-scatter.3.cloned.1.call-start = ((), (), s32[]{:S(2)}) async-start(), calls=%async_computation.5 | async-start | bytes 655360 | tf_op jit(solution)/shard_map/while/body/eval_jaxpr/reduce_scatter | solution.py:31
  146.7 2.2 collective-permute-start
  148.9 42.6 %reduce-scatter.3.cloned.1.call-start = ((), (), s32[]{:S(2)}) async-start(), calls=%async_computation.5 | async-start | bytes 655360 | tf_op jit(solution)/shard_map/while/body/eval_jaxpr/reduce_scatter | solution.py:31
  192.4 2.2 collective-permute-start
  194.5 42.6 %reduce-scatter.3.cloned.1.call-start = ((), (), s32[]{:S(2)}) async-start(), calls=%async_computation.5 | async-start | bytes 655360 | tf_op jit(solution)/shard_map/while/body/eval_jaxpr/reduce_scatter | solution.py:31
  238.0 2.2 collective-permute-start
  240.2 42.6 %reduce-scatter.3.cloned.1.call-start = ((), (), s32[]{:S(2)}) async-start(), calls=%async_computation.5 | async-start | bytes 655360 | tf_op jit(solution)/shard_map/while/body/eval_jaxpr/reduce_scatter | solution.py:31
  283.7 2.2 collective-permute-start
  285.9 42.6 %reduce-scatter.3.cloned.1.call-start = ((), (), s32[]{:S(2)}) async-start(), calls=%async_computation.5 | async-start | bytes 655360 | tf_op jit(solution)/shard_map/while/body/eval_jaxpr/reduce_scatter | solution.py:31
  329.4 2.2 collective-permute-start
  331.6 42.4 %reduce-scatter.3.cloned.1.call-start = ((), (), s32[]{:S(2)}) async-start(), calls=%async_computation.5 | async-start | bytes 655360 | tf_op jit(solution)/shard_map/while/body/eval_jaxpr/reduce_scatter | solution.py:31
  374.9 2.2 collective-permute-start
  377.1 42.5 %reduce-scatter.3.cloned.1.call-start = ((), (), s32[]{:S(2)}) async-start(), calls=%async_computation.5 | async-start | bytes 655360 | tf_op jit(solution)/shard_map/while/body/eval_jaxpr/reduce_scatter | solution.py:31
  420.5 2.2 collective-permute-start
  422.7 42.5 %reduce-scatter.3.cloned.1.call-start = ((), (), s32[]{:S(2)}) async-start(), calls=%async_computation.5 | async-start | bytes 655360 | tf_op jit(solution)/shard_map/while/body/eval_jaxpr/reduce_scatter | solution.py:31
  422.7 18.2 %copy-start.7 = (bf16[1,1,704,1024]{3,2,1,0:T(8,128)(2,1)S(1)}, bf16[1,1,704,1024]{3,2,1,0:T(8,128)(2,1)}, u32[]{:S(2)}) copy-start(bf16[1,1,704,1024]{3,2,1,0:T(8,128)(2,1)} %get-tuple-element.843) | copy-start | bytes 4325380 | tf_op jit(solution)/shard_map/while
  466.2 2.2 collective-permute-start
  468.4 42.6 %reduce-scatter.3.cloned.1.call-start = ((), (), s32[]{:S(2)}) async-start(), calls=%async_computation.5 | async-start | bytes 655360 | tf_op jit(solution)/shard_map/while/body/eval_jaxpr/reduce_scatter | solution.py:31
  511.8 2.2 collective-permute-start
  514.0 42.6 %reduce-scatter.3.cloned.1.call-start = ((), (), s32[]{:S(2)}) async-start(), calls=%async_computation.5 | async-start | bytes 655360 | tf_op jit(solution)/shard_map/while/body/eval_jaxpr/reduce_scatter | solution.py:31
  557.5 2.2 collective-permute-start
  560.3 43.9 %reduce-scatter.5.cloned.1.call-start = ((), (), s32[]{:S(2)}) async-start(), calls=%async_computation.6 | async-start | bytes 655360 | tf_op jit(solution)/shard_map/while/body/eval_jaxpr/reduce_scatter | solution.py:31
  606.3 4.5 collective-permute-start.1
  610.8 41.6 %reduce-scatter.5.cloned.1.call-start = ((), (), s32[]{:S(2)}) async-start(), calls=%async_computation.6 | async-start | bytes 655360 | tf_op jit(solution)/shard_map/while/body/eval_jaxpr/reduce_scatter | solution.py:31
  654.6 5.5 collective-permute-start.1
  660.0 41.6 %reduce-scatter.5.cloned.1.call-start = ((), (), s32[]{:S(2)}) async-start(), calls=%async_computation.6 | async-start | bytes 655360 | tf_op jit(solution)/shard_map/while/body/eval_jaxpr/reduce_scatter | solution.py:31
  703.8 5.5 collective-permute-start.1
  709.3 41.6 %reduce-scatter.5.cloned.1.call-start = ((), (), s32[]{:S(2)}) async-start(), calls=%async_computation.6 | async-start | bytes 655360 | tf_op jit(solution)/shard_map/while/body/eval_jaxpr/reduce_scatter | solution.py:31
  753.0 5.5 collective-permute-start.1
  758.5 41.5 %reduce-scatter.5.cloned.1.call-start = ((), (), s32[]{:S(2)}) async-start(), calls=%async_computation.6 | async-start | bytes 655360 | tf_op jit(solution)/shard_map/while/body/eval_jaxpr/reduce_scatter | solution.py:31
  802.2 5.5 collective-permute-start.1
  807.7 41.6 %reduce-scatter.5.cloned.1.call-start = ((), (), s32[]{:S(2)}) async-start(), calls=%async_computation.6 | async-start | bytes 655360 | tf_op jit(solution)/shard_map/while/body/eval_jaxpr/reduce_scatter | solution.py:31
  851.4 5.5 collective-permute-start.1
  856.9 41.5 %reduce-scatter.5.cloned.1.call-start = ((), (), s32[]{:S(2)}) async-start(), calls=%async_computation.6 | async-start | bytes 655360 | tf_op jit(solution)/shard_map/while/body/eval_jaxpr/reduce_scatter | solution.py:31
  900.5 5.5 collective-permute-start.1
  906.0 41.6 %reduce-scatter.5.cloned.1.call-start = ((), (), s32[]{:S(2)}) async-start(), calls=%async_computation.6 | async-start | bytes 655360 | tf_op jit(solution)/shard_map/while/body/eval_jaxpr/reduce_scatter | solution.py:31
  949.7 5.5 collective-permute-start.1
  955.2 41.5 %reduce-scatter.5.cloned.1.call-start = ((), (), s32[]{:S(2)}) async-start(), calls=%async_computation.6 | async-start | bytes 655360 | tf_op jit(solution)/shard_map/while/body/eval_jaxpr/reduce_scatter | solution.py:31
  998.9 5.5 collective-permute-start.1
  1004.4 41.5 %reduce-scatter.5.cloned.1.call-start = ((), (), s32[]{:S(2)}) async-start(), calls=%async_computation.6 | async-start | bytes 655360 | tf_op jit(solution)/shard_map/while/body/eval_jaxpr/reduce_scatter | solution.py:31
  1048.0 5.5 collective-permute-start.1
  1053.5 41.6 %reduce-scatter.5.cloned.1.call-start = ((), (), s32[]{:S(2)}) async-start(), calls=%async_computation.6 | async-start | bytes 655360 | tf_op jit(solution)/shard_map/while/body/eval_jaxpr/reduce_scatter | solution.py:31
  1097.2 5.5 collective-permute-start.1
  1102.7 45.6 %all-gather.7.cloned.1.call-start = ((), (), s32[]{:S(2)}) async-start(), calls=%async_computation.4 | async-start | bytes 4325376 | tf_op jit(solution)/shard_map/all_gather | solution.py:173
  1106.6 118.3 %all-gather.5.cloned.1.call-start = ((), (), s32[]{:S(2)}) async-start(), calls=%async_computation.3 | async-start | bytes 8650752 | tf_op jit(solution)/shard_map/all_gather | solution.py:172
  (42 other events, 418.6 us)
Sparse Core Ops, SparseCore 0:
  16.6 36.1 all-reduce.1
  77.8 22.2 reduce-scatter.2
  122.8 22.9 reduce-scatter.2
  168.3 23.0 reduce-scatter.2
  214.0 23.0 reduce-scatter.2
  259.7 23.0 reduce-scatter.2
  305.3 23.0 reduce-scatter.2
  351.0 22.9 reduce-scatter.2
  396.6 22.9 reduce-scatter.2
  442.3 22.9 reduce-scatter.2
  487.8 23.0 reduce-scatter.2
  533.5 23.0 reduce-scatter.2
  581.1 22.9 reduce-scatter.4
  631.7 20.6 reduce-scatter.4
  680.9 20.6 reduce-scatter.4
  730.2 20.6 reduce-scatter.4
  779.4 20.6 reduce-scatter.4
  828.6 20.6 reduce-scatter.4
  877.7 20.5 reduce-scatter.4
  926.9 20.6 reduce-scatter.4
  976.1 20.6 reduce-scatter.4
  1025.2 20.6 reduce-scatter.4
  1074.4 20.6 reduce-scatter.4
  1106.7 41.5 all-gather.6
  1150.4 74.4 all-gather.4
where the time goes:
time: 1250 us
  waiting for transfers between devices  555 us (44%)
  blocking collectives  318 us (25%)
  matrix products  182 us (15%)
  other arithmetic  114 us (9%)
  local copies, waits for them, and re-layouts  36.4 us (3%)
  starting transfers between devices  28.7 us (2%)
  between operations  14.5 us (1%)
    reduce_scatter x22, waiting for transfers between devices, reduce_rows(): lax.psum_scatter(jnp.einsum(form, left, right, preferred_element_type=jnp...  419 us
    all_gather x22, blocking collectives, gather_rows(): return lax.all_gather(values, 'tp', axis=0, tiled=True)  318 us
    dot_general x11, matrix products, layer_backward(): jnp.einsum('td,tkf->kdf', normed, d_both, preferred_element_type=jnp.floa...  66.1 us
    all_gather x1, waiting for transfers between devices, shards(): lax.all_gather(new_pair[None], 'rep', axis=0, tiled=True)  64.4 us
    dot_general x11, matrix products, layer_backward(): jnp.einsum('tf,td->fd', hidden, grad_full, preferred_element_type=jnp.flo...  45 us
    psum x1, waiting for transfers between devices, shards(): start_rows = lax.psum(looked.astype(jnp.bfloat16), 'section')  36.3 us
    all_gather x1, waiting for transfers between devices, shards(): lax.all_gather(new_out[None], 'rep', axis=0, tiled=True)  34.3 us
    dot_general x22, matrix products, reduce_rows(): jnp.einsum(form, left, right, preferred_element_type=jnp.float32)  29 us
  transfers between devices with their start and end apart: 47, of which 36 were waited for; matrix products, arithmetic and copies ran while one was open for 11% of the time, Pallas kernels for 0%

commit v1 on v0

v1 whole, which is shorter than its diff:
```python
import functools

import jax
import jax.numpy as jnp
from jax import lax
from jax.experimental import pallas as pl
from jax.experimental.pallas import tpu as pltpu
from jax.sharding import PartitionSpec as P


EPS = 1e-05
INNER_LR = 0.001
OUTER_LR = 0.7
MOMENTUM = 0.9
F32 = jnp.float32
BF16 = jnp.bfloat16
VMEM = pl.BlockSpec(memory_space=pltpu.VMEM)
NN = ((1,), (0,))
NT = ((1,), (1,))
TN = ((0,), (0,))


def call(body, outs, args, flops, vmem=20 << 20):
    moved = sum(a.size * a.dtype.itemsize for a in args)
    return pl.pallas_call(
        body,
        out_shape=outs,
        in_specs=[VMEM] * len(args),
        out_specs=[VMEM] * len(outs),
        compiler_params=pltpu.CompilerParams(vmem_limit_bytes=vmem),
        cost_estimate=pl.CostEstimate(flops=flops, bytes_accessed=moved, transcendentals=0),
    )(*args)


def sds(shape, dtype=BF16):
    return jax.ShapeDtypeStruct(shape, dtype)


def dot(a, b, dims):
    return lax.dot_general(a, b, (dims, ((), ())), preferred_element_type=F32)


def rows_scale(x):
    return lax.rsqrt(jnp.mean(x * x, axis=-1, keepdims=True) + EPS)


def lanes(size):
    return -(-size // 128) * 128


def span(width, ff, b):
    at = width + b * lanes(ff)
    return slice(at, at + ff)


def put_parts(outs, value, rows):
    outs[0][...] = value[:rows]
    for k in range(1, len(outs)):
        outs[k][...] = value[k * rows : (k + 1) * rows].astype(BF16)


def part_shapes(tp, rows, width):
    return [sds((rows, width), F32)] + [sds((rows, width))] * (tp - 1)


def norm_body(*refs):
    parts, (x_out, n_out) = refs[:-2], refs[-2:]
    total = parts[0][...]
    for part in parts[1:]:
        total = total + part[...]
    x_out[...] = total
    x = total.astype(F32)
    n_out[...] = (x * rows_scale(x)).astype(BF16)


def norm(parts):
    x = parts[0]
    return call(norm_body, [sds(x.shape), sds(x.shape)], parts, 8 * x.size)


def fwd_body(tp, blocks, down, *refs):
    chunks, refs = refs[:tp], refs[tp:]
    pairs, refs = refs[:blocks], refs[blocks:]
    downs, outs = (refs[:blocks], refs[blocks:]) if down else ((), refs)
    rows = chunks[0].shape[0]
    full = jnp.concatenate([c[...] for c in chunks], axis=0)
    acts_out, gates_out = outs[:2]
    width, ff = full.shape[1], pairs[0].shape[1]
    acts_out[:, :width] = full
    out = None
    for b, pair in enumerate(pairs):
        gate = dot(full, pair[0], NT)
        up = dot(full, pair[1], NT)
        gates_out[2 * b] = gate
        gates_out[2 * b + 1] = up
        hidden = (gate * jax.nn.sigmoid(gate) * up).astype(BF16)
        acts_out[:, span(width, ff, b)] = hidden
        if down:
            term = dot(hidden, downs[b][...], NN)
            out = term if out is None else out + term
    if down:
        put_parts(outs[2:], out, rows)


def fwd_layer(chunks, pairs, downs):
    tp, blocks = len(chunks), len(pairs)
    rows, width = chunks[0].shape
    ff = pairs[0].shape[1]
    outs = [sds((tp * rows, width + blocks * lanes(ff)))]
    outs += [sds((2 * blocks, tp * rows, ff), F32)]
    outs += part_shapes(tp, rows, width) if downs else []
    weights = [*pairs, *downs]
    flops = 2 * tp * rows * sum(w.size for w in weights)
    body = functools.partial(fwd_body, tp, blocks, bool(downs))
    res = call(body, outs, [*chunks, *weights], flops)
    return res[:2], res[2:]


def down_body(blocks, acts, *refs):
    downs, outs = refs[:blocks], refs[blocks:]
    ff, width = downs[0].shape
    out = None
    for b in range(blocks):
        term = dot(acts[:, span(width, ff, b)], downs[b][...], NN)
        out = term if out is None else out + term
    put_parts(outs, out, outs[0].shape[0])


def down_layer(acts, downs, tp):
    tokens, width = acts.shape[0], downs[0].shape[1]
    flops = 2 * tokens * sum(w.size for w in downs)
    body = functools.partial(down_body, len(downs))
    return call(body, part_shapes(tp, tokens // tp, width), [acts, *downs], flops)


def join_body(*refs):
    x_ref, own = refs[:2]
    parts, (x_out, n_out) = refs[2:-2], refs[-2:]
    total = own[...]
    for part in parts:
        total = total + part[...].astype(F32)
    x = (x_ref[...].astype(F32) + total).astype(BF16)
    x_out[...] = x
    xf = x.astype(F32)
    n_out[...] = (xf * rows_scale(xf)).astype(BF16)


def join(x, own, parts):
    return call(join_body, [sds(x.shape), sds(x.shape)], [x, own, *parts], 20 * x.size)


def bwd_body(tp, blocks, last, *refs):
    chunks, gates, refs = refs[:tp], refs[tp], refs[tp + 1 :]
    downs, refs = refs[:blocks], refs[blocks:]
    pairs, outs = ((), refs) if last else (refs[:blocks], refs[blocks:])
    rows = chunks[0].shape[0]
    grad = jnp.concatenate([c[...] for c in chunks], axis=0)
    acts_out = outs[0]
    ff, width = downs[0].shape
    acts_out[:, :width] = grad
    d_norm = None
    for b, down in enumerate(downs):
        d_hidden = dot(grad, down[...], NT)
        gate, up = gates[2 * b], gates[2 * b + 1]
        sig = jax.nn.sigmoid(gate)
        d_gate = (d_hidden * up * sig * (1.0 + gate * (1.0 - sig))).astype(BF16)
        d_up = (d_hidden * (gate * sig)).astype(BF16)
        acts_out[:, span(width, ff, 2 * b)] = d_gate
        acts_out[:, span(width, ff, 2 * b + 1)] = d_up
        if not last:
            term = dot(d_gate, pairs[b][0], NN) + dot(d_up, pairs[b][1], NN)
            d_norm = term if d_norm is None else d_norm + term
    if not last:
        put_parts(outs[1:], d_norm, rows)


def bwd_layer(chunks, gates, pairs, downs, last):
    tp, blocks = len(chunks), len(downs)
    rows, width = chunks[0].shape
    outs = [sds((tp * rows, width + 2 * blocks * lanes(gates.shape[-1])))]
    outs += [] if last else part_shapes(tp, rows, width)
    weights = [*downs] if last else [*downs, *pairs]
    flops = 2 * tp * rows * sum(w.size for w in weights)
    res = call(functools.partial(bwd_body, tp, blocks, last), outs, [*chunks, gates, *weights], flops)
    return res[0], res[1:]


def back_body(*refs):
    g_ref, x_ref, own = refs[:3]
    parts, out = refs[3:-1], refs[-1]
    d_norm = own[...]
    for part in parts:
        d_norm = d_norm + part[...].astype(F32)
    xf = x_ref[...].astype(F32)
    rinv = rows_scale(xf)
    mean = jnp.mean(d_norm * xf, axis=-1, keepdims=True)
    d_x = g_ref[...].astype(F32) + rinv * d_norm - xf * (rinv * rinv * rinv) * mean
    out[...] = d_x.astype(BF16)


def back(grad, x, own, parts):
    return call(back_body, [sds(x.shape)], [grad, x, own, *parts], 20 * x.size)[0]


def wgrad_body(sources, stages, stage_ref, *refs):
    pair_out, down_out = refs[-2:]
    blocks, ff, width = down_out.shape
    stage = stage_ref[0]

    def value(late, source, at):
        out = None
        for s in range(stages):
            one = refs[(late * sources + source) * stages + s][:, at]
            out = one if out is None else jnp.where(stage == s, one, out)
        return out

    def over(late, b, right):
        total = None
        for source in range(sources):
            term = dot(value(late, source, span(width, ff, b)), rights[right][source], TN)
            total = term if total is None else total + term
        return total.astype(BF16)

    top = slice(0, width)
    rights = [[value(late, source, top) for source in range(sources)] for late in range(2)]
    for b in range(blocks):
        pair_out[b, 0] = over(1, 2 * b, 0)
        pair_out[b, 1] = over(1, 2 * b + 1, 0)
        down_out[b] = over(0, b, 1)


def wgrad(stage, blocks, ff, width, acts):
    sources, stages = len(acts[0]), len(acts[0][0])
    outs = [sds((blocks, 2, ff, width)), sds((blocks, ff, width))]
    args = [v for kind in acts for source in kind for v in source]
    flops = 2 * sources * args[0].shape[0] * 3 * blocks * ff * width
    return pl.pallas_call(
        functools.partial(wgrad_body, sources, stages),
        out_shape=outs,
        in_specs=[pl.BlockSpec(memory_space=pltpu.SMEM)] + [VMEM] * len(args),
        out_specs=[VMEM] * 2,
        compiler_params=pltpu.CompilerParams(vmem_limit_bytes=40 << 20),
        cost_estimate=pl.CostEstimate(flops=flops, bytes_accessed=flops // 512, transcendentals=0),
    )(stage.astype(jnp.int32).reshape(1), *args)


def settle_body(flip, w_ref, own, *refs):
    other, out = refs if len(refs) == 2 else (None, refs[0])
    blocks = own.shape[0]
    size = own.shape[-2]
    for b in range(blocks):
        g = own[b].astype(F32)
        if other is not None:
            g = g + other[blocks - 1 - b].astype(F32)
        h = blocks - 1 - b if flip else b
        at = (Ellipsis, slice(h * size, (h + 1) * size), slice(None))
        out[at] = (w_ref[at].astype(F32) - INNER_LR * g).astype(BF16)


def settle(w, own, others, flip):
    body = functools.partial(settle_body, flip)
    return call(body, [sds(w.shape)], [w, own, *others], 4 * w.size, 40 << 20)[0]


def after(value, *others):
    return lax.optimization_barrier((value, others))[0]


def spread(value):
    tp = lax.axis_size("tp")
    return [value] + [
        lax.ppermute(value, "tp", [(i, (i + k) % tp) for i in range(tp)]) for k in range(1, tp)
    ]


def collect(parts):
    tp = lax.axis_size("tp")
    return [
        lax.ppermute(parts[k], "tp", [(i, (i - k) % tp) for i in range(tp)]) for k in range(1, tp)
    ]


def choose(index, values):
    out = values[0]
    for i, value in enumerate(values[1:], 1):
        out = jnp.where(index == i, value, out)
    return out


def shards(
    token_ids,
    embed,
    w_in,
    w_down,
    outer_in,
    outer_down,
    moment_in,
    moment_down,
    cotangent,
    fragment,
):
    sections = lax.axis_size("section")
    section = lax.axis_index("section")
    replicas = lax.axis_size("rep")
    group = 2 if sections % 2 == 0 else 1
    stages = sections // group
    stage, core = section // group, section % group
    shifts = range(1, stages)
    width = embed.shape[1]
    even = core == 0

    def swap(value):
        return lax.ppermute(value, "section", [(s, s ^ 1) for s in range(sections)])

    def shift(value, j):
        pairs = [(s, (s + j * group) % sections) for s in range(sections)]
        return lax.ppermute(value, "section", pairs)

    def to_member(value, member):
        pairs = [(s * group + 1 - member, s * group + member) for s in range(stages)]
        return lax.ppermute(value, "section", pairs)

    pairs = jnp.swapaxes(w_in[0], -1, -2)
    downs = w_down[0]
    depth = pairs.shape[0]
    ff = downs.shape[1]
    block = ff // group

    def cut(value, index):
        return lax.dynamic_slice_in_dim(value, index * block, block, value.ndim - 2)

    own = [pairs, downs]
    if group == 2:
        mine = [cut(w, core) for w in own]
        theirs = [cut(w, 1 - core) for w in own]
        away = [swap(w) for w in theirs]
        homes = [
            [jnp.where(even, m, a) for m, a in zip(mine, away)],
            [jnp.where(even, a, m) for m, a in zip(mine, away)],
        ]
    else:
        theirs, homes = own, [own]
    gathered = [[None, None] for _ in homes]

    def gather_weights(g, kind, ready):
        w = after(homes[g][kind], ready)
        gathered[g][kind] = [w] + [shift(w, j) for j in shifts]

    gather_weights(0, 0, theirs)

    def layer_weights(s, g, kind, ready):
        parts = gathered[g][kind]
        parts = [parts[0]] + [after(w, ready) for w in parts[1:]]
        ordered = choose((stage - s) % stages, parts)
        both = [ordered] + ([swap(ordered)] if group == 2 else [])
        return [[w[d] for w in both] for d in range(depth)]

    ids = token_ids[0].reshape(stages, group, -1)
    rows = ids.shape[-1]
    ids = lax.dynamic_slice_in_dim(jnp.concatenate([ids, ids], axis=0), stage, stages, 0)
    ids = lax.dynamic_slice_in_dim(jnp.concatenate([ids, ids], axis=1), core, group, 1)
    ids = jnp.swapaxes(ids, 0, 1).reshape(-1)
    vocab_part = embed.shape[0]
    local_ids = after(ids, *theirs) - section * vocab_part
    inside = (local_ids >= 0) & (local_ids < vocab_part)
    looked = jnp.take(embed, jnp.clip(local_ids, 0, vocab_part - 1), axis=0)
    looked = jnp.where(inside[:, None], looked, jnp.zeros((), BF16))
    if group == 2:
        split = stages * rows
        looked = looked[:split] + swap(looked[split:])
    gather_weights(0, 1, looked)
    seeds = cotangent[0].reshape(-1, width)
    grad = lax.dynamic_slice_in_dim(seeds, section * rows, rows, 0)
    seed_chunks = spread(grad)
    looks = [shift(looked[j * rows : (j + 1) * rows], j) for j in shifts]
    for g in range(1, group):
        gather_weights(g, 0, looked)
        gather_weights(g, 1, looked)
    x, normed = norm([looked[:rows]] + looks)

    count = stages * group * depth
    saved, xs, layers = [], [], []
    for l in range(count):
        s, g, d = l // (group * depth), l // depth % group, l % depth
        xs.append(x)
        chunks = spread(normed)
        if d == 0:
            ready = normed if l == 0 else chunks if l < group * depth else before
            by_kind = [layer_weights(s, g, 0, ready), layer_weights(s, g, 1, chunks)]
        before = chunks
        if l == 0:
            kept, _ = fwd_layer(chunks, by_kind[0][d], [])
            parts = down_layer(kept[0], by_kind[1][d], len(chunks))
        else:
            downs_used = by_kind[1][d] if l < count - 1 else []
            kept, parts = fwd_layer(chunks, by_kind[0][d], downs_used)
        layers.append((by_kind[0][d], by_kind[1][d]))
        saved.append(kept)
        if l < count - 1:
            x, normed = join(x, parts[0], collect(parts))

    def to_home(value, s):
        out = [value]
        for j in shifts:
            t = (s + j) % stages
            pairs = [(t * group + g, s * group + g) for g in range(group)]
            out.append(lax.ppermute(value, "section", pairs))
        return out

    acts = []
    for l in range(count):
        acts.append([to_home(saved[l][0], l // (group * depth))])

    def grads_of(g):
        sets = []
        for d in range(depth):
            of = [acts[(s * group + g) * depth + d] for s in range(stages)]
            kinds = [[[a[kind][j] for a in of] for j in range(stages)] for kind in range(2)]
            sets.append(wgrad(stage, group, block, width, kinds))
        out = []
        for i in range(2):
            own = jnp.stack([one[i] for one in sets], axis=1)
            out.append((own, [to_member(own, g)] if group == 2 else []))
        return out

    sums = [None] * group
    for l in reversed(range(count)):
        gates = saved[l][1]
        chunks = seed_chunks if l == count - 1 else spread(grad)
        if l == group * depth - 1:
            gates = after(gates, *[v for a in acts for kind in a[:1] for v in kind[1:]])
        if (l + 1) % depth == 0 and 0 < (l + 1) // depth < group:
            for a in acts[l + 1 :]:
                a[1][1:] = [after(v, grad) for v in a[1][1:]]
            sums[(l + 1) // depth] = grads_of((l + 1) // depth)
            gates = after(gates, *[own for own, _ in sums[(l + 1) // depth]])
        late, parts = bwd_layer(chunks, gates, *layers[l], l == 0)
        acts[l].append(to_home(late, l // (group * depth)))
        if l > 0:
            grad = back(grad, xs[l], parts[0], collect(parts))

    starts = [pairs, downs]

    def exchange(inner, member):
        if replicas != 2:
            every = lax.all_gather(inner, "rep", axis=0).astype(F32)
            return jnp.sum(every, axis=0) - inner.astype(F32)
        ring = [
            ((s * group + member) * 2 + r, (s * group + member) * 2 + 1 - r)
            for s in range(stages)
            for r in range(2)
        ]
        return lax.ppermute(inner, ("section", "rep"), ring)

    inners, others = [[], []], [[], []]
    ready = acts[0][1][0]
    for g in reversed(range(group)):
        if sums[g] is None:
            for a in acts:
                a[1][1:] = [after(v, ready) for v in a[1][1:]]
            sums[g] = grads_of(g)
        for i, (own, away) in enumerate(sums[g]):
            away = [after(v, ready) for v in away]
            inner = settle(starts[i], own, away, g > 0)
            inners[i].insert(0, inner)
            others[i].insert(0, exchange(inner, g))
            ready = inner

    flag = lax.dynamic_index_in_dim(fragment, section, 0, keepdims=False)
    chosen = flag == 1

    def finish(i, outer, moment):
        inner = choose(core, inners[i])
        total = inner.astype(F32) + choose(core, others[i]).astype(F32)
        mean = outer - total / replicas
        next_moment = MOMENTUM * moment + mean
        next_outer = outer - OUTER_LR * (mean + MOMENTUM * next_moment)
        return (
            jnp.where(chosen, next_outer.astype(BF16), inner),
            jnp.where(chosen, next_outer, outer),
            jnp.where(chosen, next_moment, moment),
        )

    flip = lambda v: jnp.swapaxes(v, -1, -2)
    new_in, next_in, next_m_in = finish(0, flip(outer_in), flip(moment_in))
    outer_down, moment_down = after((outer_down, moment_down), next_in)
    new_down, next_down, next_m_down = finish(1, outer_down, moment_down)
    return (
        flip(new_in)[None],
        new_down[None],
        flip(next_in),
        next_down,
        flip(next_m_in),
        next_m_down,
    )


def solution(mesh):
    return jax.shard_map(
        shards,
        mesh=mesh,
        in_specs=(
            P("rep", None, "tp"),
            P("section", None),
            P("rep", "section", None, None, "tp"),
            P("rep", "section", "tp", None),
            P("section", None, None, "tp"),
            P("section", "tp", None),
            P("section", None, None, "tp"),
            P("section", "tp", None),
            P("rep", None, "tp", None),
            P(),
        ),
        out_specs=(
            P("rep", "section", None, None, "tp"),
            P("rep", "section", "tp", None),
            P("section", None, None, "tp"),
            P("section", "tp", None),
            P("section", None, None, "tp"),
            P("section", "tp", None),
        ),
        check_vma=False,
    )
```

time: 1250 us -> 483 us (0.39)
  waiting for transfers between devices: 555 us -> 235 us
  blocking collectives: 318 us -> 0 us
  matrix products: 182 us -> 0 us
  starting transfers between devices: 28.7 us -> 110 us
  other arithmetic: 114 us -> 43.3 us
  Pallas kernels: 0 us -> 39.2 us
    reduce_scatter x22 -> x0, waiting for transfers between devices: 419 us -> none  [reduce_rows(): lax.psum_scatter(jnp.einsum(form, left, right, preferred_element_type=jnp...]
    all_gather x22 -> x0, blocking collectives: 318 us -> none  [gather_rows(): return lax.all_gather(values, 'tp', axis=0, tiled=True)]
    ppermute x22 -> x74, waiting for transfers between devices: 0.69 us -> 235 us  [the longest x18 63.9 us: collect(): lax.ppermute(parts[k], 'tp', [(i, (i - k) % tp) for i in range(tp)])]
    dot_general x66 -> x0, matrix products: 182 us -> none  [the longest x11 66.1 us: layer_backward(): jnp.einsum('td,tkf->kdf', normed, d_both, preferred_element_type=jnp.floa...]
    all_gather x2 -> x0, waiting for transfers between devices: 98.7 us -> none  [the longest x1 64.4 us: shards(): lax.all_gather(new_pair[None], 'rep', axis=0, tiled=True)]
    ppermute x22 -> x74, starting transfers between devices: 28.4 us -> 110 us  [the longest x24 39.5 us: spread(): lax.ppermute(value, 'tp', [(i, (i + k) % tp) for i in range(tp)])]
    pallas_call x0 -> x22, Pallas kernels: none -> 39.2 us  [the longest x20 33.2 us: call(): pl.pallas_call(body, out_shape=outs, in_specs=[VMEM] * len(args), out_spe...]
    psum x1 -> x0, waiting for transfers between devices: 36.3 us -> none  [shards(): start_rows = lax.psum(looked.astype(jnp.bfloat16), 'section')]
  transfers between devices with their start and end apart: 47 -> 74, of which waited for: 36 -> 40; matrix products, arithmetic and copies ran while one was open for 11% -> 8% of each run, Pallas kernels for 0% -> 6%
where the time goes in v1:
time: 483 us; the launch traced here: 474 us
  waiting for transfers between devices  235 us (49%)
  starting transfers between devices  110 us (23%)
  local copies, waits for them, and re-layouts  44 us (9%)
  other arithmetic  43.3 us (9%)
  Pallas kernels  39.2 us (8%)
    ppermute x18, waiting for transfers between devices, collect(): lax.ppermute(parts[k], 'tp', [(i, (i - k) % tp) for i in range(tp)])  63.9 us
    ppermute x4, waiting for transfers between devices, exchange(): return lax.ppermute(inner, ('section', 'rep'), ring)  53.8 us
    ppermute x24, starting transfers between devices, spread(): lax.ppermute(value, 'tp', [(i, (i + k) % tp) for i in range(tp)])  39.5 us
    ppermute x5, waiting for transfers between devices, shift(): return lax.ppermute(value, 'section', pairs)  39.4 us
    ppermute x24, waiting for transfers between devices, spread(): lax.ppermute(value, 'tp', [(i, (i + k) % tp) for i in range(tp)])  38.7 us
    pallas_call x20, Pallas kernels, call(): pl.pallas_call(body, out_shape=outs, in_specs=[VMEM] * len(args), out_spe...  33.2 us
    ppermute x8, waiting for transfers between devices, to_home(): out.append(lax.ppermute(value, 'section', pairs))  31.1 us
    unnamed x180, local copies, waits for them, and re-layouts  31 us
  transfers between devices with their start and end apart: 74, of which 40 were waited for; matrix products, arithmetic and copies ran while one was open for 8% of the time, Pallas kernels for 6%

profile of v1, /device:TPU:0, one launch (start us, length us, event | category | flops | bytes accessed | tf_op | source)
XLA Modules:
  0.0 473.9 jit_solution(9171657415769303510)
XLA Ops:
  7.1 3.8 bitcast_select_fusion.2
  13.8 6.8 %gather_fusion = bf16[256,1024]{1,0:T(8,128)(2,1)} fusion(bf16[4096,1024]{1,0:T(8,128)(2,1)} %param.11, s32[1024]{0:T(1024)S(1)} %pad_clamp_fusion), kind=kCustom, calls=%fused_computation | custom fusion | bytes 1049600 | tf_op jit(solution)/shard_map/jit(_take)/gather | solution.py:366
  24.1 24.7 %collective-permute-done.1.refs_1_ = bf16[64,1024]{1,0:T(8,128)(2,1)} collective-permute-done((bf16[64,1024]{1,0:T(8,128)(2,1)}, bf16[64,1024]{1,0:T(8,128)(2,1)}, u32[]{:S(2)}, u32[]{:S(2)}) %collective-permute-start.1) | collective-permute-done | bytes 131104 | tf_op jit(solution)/shard_map/ppermute | solution.py:317
  60.0 3.2 collective-permute-done.2.refs_1_
  64.8 3.7 collective-permute-done.3.refs_2_
  74.6 3.9 collective-permute-start.11
  82.4 7.3 %collective-permute-done.12.refs_3_ = bf16[64,1024]{1,0:T(8,128)(2,1)S(1)} collective-permute-done((bf16[64,1024]{1,0:T(8,128)(2,1)S(1)}, bf16[64,1024]{1,0:T(8,128)(2,1)S(1)}, u32[]{:S(2)}, u32[]{:S(2)}) %collective-permute-start.12) | collective-permute-done | bytes 131104 | tf_op jit(solution)/shard_map/ppermute | solution.py:279
  97.7 3.8 collective-permute-done.17
  104.8 10.7 %collective-permute-done.19 = bf16[1,352,1024]{2,1,0:T(8,128)(2,1)S(1)} collective-permute-done((bf16[1,352,1024]{2,1,0:T(8,128)(2,1)S(1)}, bf16[1,352,1024]{2,1,0:T(8,128)(2,1)S(1)}, u32[]{:S(2)}, u32[]{:S(2)}) %collective-permute-start.19) | collective-permute-done | bytes 720928 | tf_op jit(solution)/shard_map/ppermute | solution.py:317
  119.3 4.2 shard_map.149
  125.6 3.5 collective-permute-start.21
  130.1 3.0 collective-permute-done.21.refs_2_
  133.1 8.0 %collective-permute-done.22.refs_3_ = bf16[64,1024]{1,0:T(8,128)(2,1)S(1)} collective-permute-done((bf16[64,1024]{1,0:T(8,128)(2,1)S(1)}, bf16[64,1024]{1,0:T(8,128)(2,1)S(1)}, u32[]{:S(2)}, u32[]{:S(2)}) %collective-permute-start.22) | collective-permute-done | bytes 131104 | tf_op jit(solution)/shard_map/ppermute | solution.py:279
  143.9 3.3 collective-permute-start.26
  149.6 4.3 collective-permute-done.25.refs_2_
  160.4 3.9 collective-permute-start.29
  164.8 3.4 collective-permute-done.29.refs_2_
  168.2 8.0 %collective-permute-done.30.refs_3_ = bf16[64,1024]{1,0:T(8,128)(2,1)S(1)} collective-permute-done((bf16[64,1024]{1,0:T(8,128)(2,1)S(1)}, bf16[64,1024]{1,0:T(8,128)(2,1)S(1)}, u32[]{:S(2)}, u32[]{:S(2)}) %collective-permute-start.30) | collective-permute-done | bytes 131104 | tf_op jit(solution)/shard_map/ppermute | solution.py:279
  179.0 2.9 collective-permute-start.34
  185.9 3.8 collective-permute-done.33.refs_2_
  200.3 3.2 shard_map.153
  205.5 4.5 shard_map.154
  210.0 3.6 collective-permute-start.42
  217.5 9.2 %collective-permute-done.43.refs_4_ = bf16[64,1024]{1,0:T(8,128)(2,1)S(1)} collective-permute-done((bf16[64,1024]{1,0:T(8,128)(2,1)S(1)}, bf16[64,1024]{1,0:T(8,128)(2,1)S(1)}, u32[]{:S(2)}, u32[]{:S(2)}) %collective-permute-start.43) | collective-permute-done | bytes 131104 | tf_op jit(solution)/shard_map/ppermute | solution.py:279
  226.9 3.5 collective-permute-start.55
  233.7 7.3 %collective-permute-done.46.refs_2_ = bf16[64,1024]{1,0:T(8,128)(2,1)S(1)} collective-permute-done((bf16[64,1024]{1,0:T(8,128)(2,1)S(1)}, bf16[64,1024]{1,0:T(8,128)(2,1)S(1)}, u32[]{:S(2)}, u32[]{:S(2)}) %collective-permute-start.46) | collective-permute-done | bytes 131104 | tf_op jit(solution)/shard_map/ppermute | solution.py:272
  242.0 3.9 collective-permute-done.47.refs_3_
  248.1 2.9 collective-permute-start.48
  251.0 3.5 collective-permute-done.48.refs_3_
  254.5 5.8 %collective-permute-done.49.refs_4_ = bf16[64,1024]{1,0:T(8,128)(2,1)S(1)} collective-permute-done((bf16[64,1024]{1,0:T(8,128)(2,1)S(1)}, bf16[64,1024]{1,0:T(8,128)(2,1)S(1)}, u32[]{:S(2)}, u32[]{:S(2)}) %collective-permute-start.49) | collective-permute-done | bytes 131104 | tf_op jit(solution)/shard_map/ppermute | solution.py:279
  262.4 5.4 %collective-permute-done.50.refs_5_ = bf16[64,1024]{1,0:T(8,128)(2,1)S(1)} collective-permute-done((bf16[64,1024]{1,0:T(8,128)(2,1)S(1)}, bf16[64,1024]{1,0:T(8,128)(2,1)S(1)}, u32[]{:S(2)}, u32[]{:S(2)}) %collective-permute-start.50) | collective-permute-done | bytes 131104 | tf_op jit(solution)/shard_map/ppermute | solution.py:279
  268.3 3.2 collective-permute-start.52
  272.0 6.8 %collective-permute-start.60 = (bf16[256,2560]{1,0:T(8,128)(2,1)S(1)}, bf16[256,2560]{1,0:T(8,128)(2,1)S(1)}, u32[]{:S(2)}, u32[]{:S(2)}) collective-permute-start(bf16[256,2560]{1,0:T(8,128)(2,1)S(1)} %get-tuple-element.129.refs_5_), channel_id=1, source_target_pairs={{0,16},{8,24},{1,17},{9,25},{2,18},{10,26},{3,19},{11,27},{4,20},{... | collective-permute-start | bytes 3932168 | tf_op jit(solution)/shard_map/ppermute | solution.py:407
  278.9 4.3 shard_map.158
  289.8 3.1 collective-permute-done.57.refs_3_
  292.8 4.2 collective-permute-done.58.refs_4_
  298.3 10.4 %collective-permute-done.56.refs_6_ = bf16[256,2560]{1,0:T(8,128)(2,1)S(1)} collective-permute-done((bf16[256,2560]{1,0:T(8,128)(2,1)S(1)}, bf16[256,2560]{1,0:T(8,128)(2,1)S(1)}, u32[]{:S(2)}, u32[]{:S(2)}) %collective-permute-start.56) | collective-permute-done | bytes 1310752 | tf_op jit(solution)/shard_map/ppermute | solution.py:407
  318.8 5.2 %collective-permute-start.62 = (bf16[64,1024]{1,0:T(8,128)(2,1)S(1)}, bf16[64,1024]{1,0:T(8,128)(2,1)S(1)}, u32[]{:S(2)}, u32[]{:S(2)}) collective-permute-start(bf16[64,1024]{1,0:T(8,128)(2,1)S(1)} %shard_map.159.refs_0_), channel_id=1, source_target_pairs={{0,1},{1,2},{2,3},{3,0},{4,5},{5,6},{6,7},{7,4},{8,9},{9,10},{10,1... | collective-permute-start | bytes 393224 | tf_op jit(solution)/shard_map/ppermute | solution.py:272
  332.9 18.9 %collective-permute-done.67.refs_7_ = bf16[256,2560]{1,0:T(8,128)(2,1)S(1)} collective-permute-done((bf16[256,2560]{1,0:T(8,128)(2,1)S(1)}, bf16[256,2560]{1,0:T(8,128)(2,1)S(1)}, u32[]{:S(2)}, u32[]{:S(2)}) %collective-permute-start.67) | collective-permute-done | bytes 1310752 | tf_op jit(solution)/shard_map/ppermute | solution.py:407
  358.2 3.5 shard_map.164
  365.5 3.6 collective-permute-done.68.refs_0_
  371.8 3.3 collective-permute-start.70
  389.0 50.4 %collective-permute-done.70 = bf16[1,2,704,1024]{3,2,1,0:T(8,128)(2,1)} collective-permute-done((bf16[1,2,704,1024]{3,2,1,0:T(8,128)(2,1)}, bf16[1,2,704,1024]{3,2,1,0:T(8,128)(2,1)}, u32[]{:S(2)}, u32[]{:S(2)}) %collective-permute-start.70) | collective-permute-done | bytes 2883616 | tf_op jit(solution)/shard_map/ppermute | solution.py:453
  439.4 9.4 %fusion.1 = (f32[1,2,1024,704]{2,3,1,0:T(8,128)}, bf16[1,2,704,1024]{3,2,1,0:T(8,128)(2,1)S(1)}, bf16[1,2,704,1024]{3,2,1,0:T(8,128)(2,1)S(1)}) fusion(f32[1,2,1024,704]{2,3,1,0:T(8,128)} %param.16, f32[1,2,1024,704]{2,3,1,0:T(8,128)} %param.14, pred[]{:T(512)} %bitcast, bf16[1,2,704,1024]{3,2,1,0:T(8,128)(2,1)} %collective-permute-done.69, ...), kind=kLoop, calls=%fused_computation.4 | loop fusion | flops 14417920 | bytes 34603008 | tf_op jit(solution)/shard_map/transpose | solution.py:484
  450.8 4.0 bitcast_select_fusion.1
  454.8 3.8 select_bitcast_fusion
  458.6 3.4 collective-permute-done.73
  462.0 6.4 %fusion.2 = (f32[1,704,1024]{2,1,0:T(8,128)}, bf16[1,704,1024]{2,1,0:T(8,128)(2,1)S(1)}, bf16[1,704,1024]{2,1,0:T(8,128)(2,1)S(1)}) fusion(f32[1,704,1024]{2,1,0:T(8,128)} %param.17, f32[1,704,1024]{2,1,0:T(8,128)} %param.15, pred[]{:T(512)} %bitcast, bf16[1,704,1024]{2,1,0:T(8,128)(2,1)S(1)} %collective-permute-done.72, ...), kind=kLoop, calls=%fused_computation.10 | loop fusion | flops 7208960 | bytes 17301506 | tf_op jit(solution)/shard_map/jit(_where)/select_n | solution.py:481
  (336 shorter events, 158.3 us)
Async XLA Ops:
  10.9 42.5 %collective-permute-start.6 = (bf16[1,2,352,1024]{3,2,1,0:T(8,128)(2,1)}, bf16[1,2,352,1024]{3,2,1,0:T(8,128)(2,1)}, u32[]{:S(2)}, u32[]{:S(2)}) collective-permute-start(bf16[1,2,352,1024]{3,2,1,0:T(8,128)(2,1)} %get-tuple-element.82), channel_id=1, source_target_pairs={{0,16},{8,24},{16,0},{24,8},{1,17},{9,25},{17,1},{25,9},{2,18},{10... | collective-permute-start | bytes 4325384 | tf_op jit(solution)/shard_map/ppermute | solution.py:317
  21.9 27.9 %collective-permute-start.8 = (bf16[1,352,1024]{2,1,0:T(8,128)(2,1)}, bf16[1,352,1024]{2,1,0:T(8,128)(2,1)}, u32[]{:S(2)}, u32[]{:S(2)}) collective-permute-start(bf16[1,352,1024]{2,1,0:T(8,128)(2,1)} %dynamic-slice_bitcast_fusion.1), channel_id=1, source_target_pairs={{0,8},{8,0},{16,24},{24,16},{1,9},{9,1},{17,25},{25,17},{2,10},{10... | collective-permute-start | bytes 2162696 | tf_op jit(solution)/shard_map/ppermute | solution.py:313
  24.1 24.7 %collective-permute-start.1 = (bf16[64,1024]{1,0:T(8,128)(2,1)}, bf16[64,1024]{1,0:T(8,128)(2,1)}, u32[]{:S(2)}, u32[]{:S(2)}) collective-permute-start(bf16[64,1024]{1,0:T(8,128)(2,1)} %get-tuple-element.164), channel_id=1, source_target_pairs={{0,16},{8,24},{16,0},{24,8},{1,17},{9,25},{17,1},{25,9},{2,18},{10... | collective-permute-start | bytes 393224 | tf_op jit(solution)/shard_map/ppermute | solution.py:317
  51.5 19.1 %collective-permute-start.9 = (bf16[1,352,1024]{2,1,0:T(8,128)(2,1)S(1)}, bf16[1,352,1024]{2,1,0:T(8,128)(2,1)S(1)}, u32[]{:S(2)}, u32[]{:S(2)}) collective-permute-start(bf16[1,352,1024]{2,1,0:T(8,128)(2,1)S(1)} %get-tuple-element.85), channel_id=1, source_target_pairs={{0,16},{8,24},{16,0},{24,8},{1,17},{9,25},{17,1},{25,9},{2,18},{10... | collective-permute-start | bytes 2162696 | tf_op jit(solution)/shard_map/ppermute | solution.py:317
  54.9 15.9 %collective-permute-start.7 = (bf16[1,2,352,1024]{3,2,1,0:T(8,128)(2,1)S(1)}, bf16[1,2,352,1024]{3,2,1,0:T(8,128)(2,1)S(1)}, u32[]{:S(2)}, u32[]{:S(2)}) collective-permute-start(bf16[1,2,352,1024]{3,2,1,0:T(8,128)(2,1)S(1)} %broadcast_select_fusion.8), channel_id=1, source_target_pairs={{0,8},{8,0},{16,24},{24,16},{1,9},{9,1},{17,25},{25,17},{2,10},{10... | collective-permute-start | bytes 4325384 | tf_op jit(solution)/shard_map/ppermute | solution.py:313
  56.6 44.9 %collective-permute-start.17 = (bf16[1,2,352,1024]{3,2,1,0:T(8,128)(2,1)S(1)}, bf16[1,2,352,1024]{3,2,1,0:T(8,128)(2,1)S(1)}, u32[]{:S(2)}, u32[]{:S(2)}) collective-permute-start(bf16[1,2,352,1024]{3,2,1,0:T(8,128)(2,1)S(1)} %copy-done.72), channel_id=1, source_target_pairs={{0,16},{8,24},{16,0},{24,8},{1,17},{9,25},{17,1},{25,9},{2,18},{10... | collective-permute-start | bytes 4325384 | tf_op jit(solution)/shard_map/ppermute | solution.py:317
  57.5 11.0 %collective-permute-start.3 = (bf16[64,1024]{1,0:T(8,128)(2,1)S(1)}, bf16[64,1024]{1,0:T(8,128)(2,1)S(1)}, u32[]{:S(2)}, u32[]{:S(2)}) collective-permute-start(bf16[64,1024]{1,0:T(8,128)(2,1)S(1)} %get-tuple-element.81.refs_0_), channel_id=1, source_target_pairs={{0,2},{1,3},{2,0},{3,1},{4,6},{5,7},{6,4},{7,5},{8,10},{9,11},{10,... | collective-permute-start | bytes 393224 | tf_op jit(solution)/shard_map/ppermute | solution.py:272
  78.5 11.2 %collective-permute-start.12 = (bf16[64,1024]{1,0:T(8,128)(2,1)S(1)}, bf16[64,1024]{1,0:T(8,128)(2,1)S(1)}, u32[]{:S(2)}, u32[]{:S(2)}) collective-permute-start(bf16[64,1024]{1,0:T(8,128)(2,1)S(1)} %get-tuple-element.89), channel_id=1, source_target_pairs={{0,2},{1,3},{2,0},{3,1},{4,6},{5,7},{6,4},{7,5},{8,10},{9,11},{10,... | collective-permute-start | bytes 393224 | tf_op jit(solution)/shard_map/ppermute | solution.py:279
  78.5 11.2 %collective-permute-start.13 = (bf16[64,1024]{1,0:T(8,128)(2,1)S(1)}, bf16[64,1024]{1,0:T(8,128)(2,1)S(1)}, u32[]{:S(2)}, u32[]{:S(2)}) collective-permute-start(bf16[64,1024]{1,0:T(8,128)(2,1)S(1)} %get-tuple-element.90), channel_id=1, source_target_pairs={{0,1},{1,2},{2,3},{3,0},{4,5},{5,6},{6,7},{7,4},{8,9},{9,10},{10,1... | collective-permute-start | bytes 393224 | tf_op jit(solution)/shard_map/ppermute | solution.py:279
  89.9 11.6 %collective-permute-start.14 = (bf16[64,1024]{1,0:T(8,128)(2,1)S(1)}, bf16[64,1024]{1,0:T(8,128)(2,1)S(1)}, u32[]{:S(2)}, u32[]{:S(2)}) collective-permute-start(bf16[64,1024]{1,0:T(8,128)(2,1)S(1)} %get-tuple-element.91.refs_0_), channel_id=1, source_target_pairs={{0,1},{1,2},{2,3},{3,0},{4,5},{5,6},{6,7},{7,4},{8,9},{9,10},{10,1... | collective-permute-start | bytes 393224 | tf_op jit(solution)/shard_map/ppermute | solution.py:272
  90.7 11.6 %collective-permute-start.15 = (bf16[64,1024]{1,0:T(8,128)(2,1)S(1)}, bf16[64,1024]{1,0:T(8,128)(2,1)S(1)}, u32[]{:S(2)}, u32[]{:S(2)}) collective-permute-start(bf16[64,1024]{1,0:T(8,128)(2,1)S(1)} %get-tuple-element.91.refs_0_), channel_id=1, source_target_pairs={{0,2},{1,3},{2,0},{3,1},{4,6},{5,7},{6,4},{7,5},{8,10},{9,11},{10,... | collective-permute-start | bytes 393224 | tf_op jit(solution)/shard_map/ppermute | solution.py:272
  92.7 10.3 %collective-permute-start.16 = (bf16[64,1024]{1,0:T(8,128)(2,1)S(1)}, bf16[64,1024]{1,0:T(8,128)(2,1)S(1)}, u32[]{:S(2)}, u32[]{:S(2)}) collective-permute-start(bf16[64,1024]{1,0:T(8,128)(2,1)S(1)} %get-tuple-element.91.refs_0_), channel_id=1, source_target_pairs={{0,3},{1,0},{2,1},{3,2},{4,7},{5,4},{6,5},{7,6},{8,11},{9,8},{10,9... | collective-permute-start | bytes 393224 | tf_op jit(solution)/shard_map/ppermute | solution.py:272
  96.2 19.4 %collective-permute-start.19 = (bf16[1,352,1024]{2,1,0:T(8,128)(2,1)S(1)}, bf16[1,352,1024]{2,1,0:T(8,128)(2,1)S(1)}, u32[]{:S(2)}, u32[]{:S(2)}) collective-permute-start(bf16[1,352,1024]{2,1,0:T(8,128)(2,1)S(1)} %get-tuple-element.94), channel_id=1, source_target_pairs={{0,16},{8,24},{16,0},{24,8},{1,17},{9,25},{17,1},{25,9},{2,18},{10... | collective-permute-start | bytes 2162696 | tf_op jit(solution)/shard_map/ppermute | solution.py:317
  104.8 14.4 %collective-permute-start.18 = (bf16[1,2,352,1024]{3,2,1,0:T(8,128)(2,1)}, bf16[1,2,352,1024]{3,2,1,0:T(8,128)(2,1)}, u32[]{:S(2)}, u32[]{:S(2)}) collective-permute-start(bf16[1,2,352,1024]{3,2,1,0:T(8,128)(2,1)} %broadcast_select_fusion.7), channel_id=1, source_target_pairs={{0,8},{8,0},{16,24},{24,16},{1,9},{9,1},{17,25},{25,17},{2,10},{10... | collective-permute-start | bytes 4325384 | tf_op jit(solution)/shard_map/ppermute | solution.py:313
  118.3 37.6 %collective-permute-start.27 = (bf16[1,2,352,1024]{3,2,1,0:T(8,128)(2,1)S(1)}, bf16[1,2,352,1024]{3,2,1,0:T(8,128)(2,1)S(1)}, u32[]{:S(2)}, u32[]{:S(2)}) collective-permute-start(bf16[1,2,352,1024]{3,2,1,0:T(8,128)(2,1)S(1)} %broadcast_select_fusion.6), channel_id=1, source_target_pairs={{0,8},{8,0},{16,24},{24,16},{1,9},{9,1},{17,25},{25,17},{2,10},{10... | collective-permute-start | bytes 4325384 | tf_op jit(solution)/shard_map/ppermute | solution.py:313
  129.1 12.0 %collective-permute-start.22 = (bf16[64,1024]{1,0:T(8,128)(2,1)S(1)}, bf16[64,1024]{1,0:T(8,128)(2,1)S(1)}, u32[]{:S(2)}, u32[]{:S(2)}) collective-permute-start(bf16[64,1024]{1,0:T(8,128)(2,1)S(1)} %get-tuple-element.100), channel_id=1, source_target_pairs={{0,2},{1,3},{2,0},{3,1},{4,6},{5,7},{6,4},{7,5},{8,10},{9,11},{10,... | collective-permute-start | bytes 393224 | tf_op jit(solution)/shard_map/ppermute | solution.py:279
  129.1 12.0 %collective-permute-start.23 = (bf16[64,1024]{1,0:T(8,128)(2,1)S(1)}, bf16[64,1024]{1,0:T(8,128)(2,1)S(1)}, u32[]{:S(2)}, u32[]{:S(2)}) collective-permute-start(bf16[64,1024]{1,0:T(8,128)(2,1)S(1)} %get-tuple-element.101), channel_id=1, source_target_pairs={{0,1},{1,2},{2,3},{3,0},{4,5},{5,6},{6,7},{7,4},{8,9},{9,10},{10,1... | collective-permute-start | bytes 393224 | tf_op jit(solution)/shard_map/ppermute | solution.py:279
  141.9 12.1 %collective-permute-start.25 = (bf16[64,1024]{1,0:T(8,128)(2,1)S(1)}, bf16[64,1024]{1,0:T(8,128)(2,1)S(1)}, u32[]{:S(2)}, u32[]{:S(2)}) collective-permute-start(bf16[64,1024]{1,0:T(8,128)(2,1)S(1)} %get-tuple-element.103.refs_0_), channel_id=1, source_target_pairs={{0,2},{1,3},{2,0},{3,1},{4,6},{5,7},{6,4},{7,5},{8,10},{9,11},{10,... | collective-permute-start | bytes 393224 | tf_op jit(solution)/shard_map/ppermute | solution.py:272
  143.9 10.1 %collective-permute-start.26 = (bf16[64,1024]{1,0:T(8,128)(2,1)S(1)}, bf16[64,1024]{1,0:T(8,128)(2,1)S(1)}, u32[]{:S(2)}, u32[]{:S(2)}) collective-permute-start(bf16[64,1024]{1,0:T(8,128)(2,1)S(1)} %get-tuple-element.103.refs_0_), channel_id=1, source_target_pairs={{0,3},{1,0},{2,1},{3,2},{4,7},{5,4},{6,5},{7,6},{8,11},{9,8},{10,9... | collective-permute-start | bytes 393224 | tf_op jit(solution)/shard_map/ppermute | solution.py:272
  155.4 41.3 %collective-permute-start.35 = (bf16[1,2,352,1024]{3,2,1,0:T(8,128)(2,1)}, bf16[1,2,352,1024]{3,2,1,0:T(8,128)(2,1)}, u32[]{:S(2)}, u32[]{:S(2)}) collective-permute-start(bf16[1,2,352,1024]{3,2,1,0:T(8,128)(2,1)} %broadcast_select_fusion.5), channel_id=1, source_target_pairs={{0,8},{8,0},{16,24},{24,16},{1,9},{9,1},{17,25},{25,17},{2,10},{10... | collective-permute-start | bytes 4325384 | tf_op jit(solution)/shard_map/ppermute | solution.py:313
  164.2 12.0 %collective-permute-start.30 = (bf16[64,1024]{1,0:T(8,128)(2,1)S(1)}, bf16[64,1024]{1,0:T(8,128)(2,1)S(1)}, u32[]{:S(2)}, u32[]{:S(2)}) collective-permute-start(bf16[64,1024]{1,0:T(8,128)(2,1)S(1)} %get-tuple-element.108), channel_id=1, source_target_pairs={{0,2},{1,3},{2,0},{3,1},{4,6},{5,7},{6,4},{7,5},{8,10},{9,11},{10,... | collective-permute-start | bytes 393224 | tf_op jit(solution)/shard_map/ppermute | solution.py:279
  164.3 11.9 %collective-permute-start.31 = (bf16[64,1024]{1,0:T(8,128)(2,1)S(1)}, bf16[64,1024]{1,0:T(8,128)(2,1)S(1)}, u32[]{:S(2)}, u32[]{:S(2)}) collective-permute-start(bf16[64,1024]{1,0:T(8,128)(2,1)S(1)} %get-tuple-element.109), channel_id=1, source_target_pairs={{0,1},{1,2},{2,3},{3,0},{4,5},{5,6},{6,7},{7,4},{8,9},{9,10},{10,1... | collective-permute-start | bytes 393224 | tf_op jit(solution)/shard_map/ppermute | solution.py:279
  177.1 12.6 %collective-permute-start.33 = (bf16[64,1024]{1,0:T(8,128)(2,1)S(1)}, bf16[64,1024]{1,0:T(8,128)(2,1)S(1)}, u32[]{:S(2)}, u32[]{:S(2)}) collective-permute-start(bf16[64,1024]{1,0:T(8,128)(2,1)S(1)} %get-tuple-element.110.refs_0_), channel_id=1, source_target_pairs={{0,2},{1,3},{2,0},{3,1},{4,6},{5,7},{6,4},{7,5},{8,10},{9,11},{10,... | collective-permute-start | bytes 393224 | tf_op jit(solution)/shard_map/ppermute | solution.py:272
  179.0 11.4 %collective-permute-start.34 = (bf16[64,1024]{1,0:T(8,128)(2,1)S(1)}, bf16[64,1024]{1,0:T(8,128)(2,1)S(1)}, u32[]{:S(2)}, u32[]{:S(2)}) collective-permute-start(bf16[64,1024]{1,0:T(8,128)(2,1)S(1)} %get-tuple-element.110.refs_0_), channel_id=1, source_target_pairs={{0,3},{1,0},{2,1},{3,2},{4,7},{5,4},{6,5},{7,6},{8,11},{9,8},{10,9... | collective-permute-start | bytes 393224 | tf_op jit(solution)/shard_map/ppermute | solution.py:272
  192.0 13.5 %collective-permute-start.41 = (bf16[1,352,1024]{2,1,0:T(8,128)(2,1)}, bf16[1,352,1024]{2,1,0:T(8,128)(2,1)}, u32[]{:S(2)}, u32[]{:S(2)}) collective-permute-start(bf16[1,352,1024]{2,1,0:T(8,128)(2,1)} %broadcast_select_fusion.9), channel_id=1, source_target_pairs={{0,8},{8,0},{16,24},{24,16},{1,9},{9,1},{17,25},{25,17},{2,10},{10... | collective-permute-start | bytes 2162696 | tf_op jit(solution)/shard_map/ppermute | solution.py:313
  192.0 11.5 %collective-permute-start.38 = (bf16[64,1024]{1,0:T(8,128)(2,1)S(1)}, bf16[64,1024]{1,0:T(8,128)(2,1)S(1)}, u32[]{:S(2)}, u32[]{:S(2)}) collective-permute-start(bf16[64,1024]{1,0:T(8,128)(2,1)S(1)} %constant_dynamic-slice_fusion.refs_0_), channel_id=1, source_target_pairs={{0,1},{1,2},{2,3},{3,0},{4,5},{5,6},{6,7},{7,4},{8,9},{9,10},{10,1... | collective-permute-start | bytes 393224 | tf_op jit(solution)/shard_map/ppermute | solution.py:272
  193.8 11.6 %collective-permute-start.39 = (bf16[64,1024]{1,0:T(8,128)(2,1)S(1)}, bf16[64,1024]{1,0:T(8,128)(2,1)S(1)}, u32[]{:S(2)}, u32[]{:S(2)}) collective-permute-start(bf16[64,1024]{1,0:T(8,128)(2,1)S(1)} %constant_dynamic-slice_fusion.refs_0_), channel_id=1, source_target_pairs={{0,2},{1,3},{2,0},{3,1},{4,6},{5,7},{6,4},{7,5},{8,10},{9,11},{10,... | collective-permute-start | bytes 393224 | tf_op jit(solution)/shard_map/ppermute | solution.py:272
  196.2 9.3 %collective-permute-start.40 = (bf16[64,1024]{1,0:T(8,128)(2,1)S(1)}, bf16[64,1024]{1,0:T(8,128)(2,1)S(1)}, u32[]{:S(2)}, u32[]{:S(2)}) collective-permute-start(bf16[64,1024]{1,0:T(8,128)(2,1)S(1)} %constant_dynamic-slice_fusion.refs_0_), channel_id=1, source_target_pairs={{0,3},{1,0},{2,1},{3,2},{4,7},{5,4},{6,5},{7,6},{8,11},{9,8},{10,9... | collective-permute-start | bytes 393224 | tf_op jit(solution)/shard_map/ppermute | solution.py:272
  213.6 13.1 %collective-permute-start.43 = (bf16[64,1024]{1,0:T(8,128)(2,1)S(1)}, bf16[64,1024]{1,0:T(8,128)(2,1)S(1)}, u32[]{:S(2)}, u32[]{:S(2)}) collective-permute-start(bf16[64,1024]{1,0:T(8,128)(2,1)S(1)} %get-tuple-element.118), channel_id=1, source_target_pairs={{0,2},{1,3},{2,0},{3,1},{4,6},{5,7},{6,4},{7,5},{8,10},{9,11},{10,... | collective-permute-start | bytes 393224 | tf_op jit(solution)/shard_map/ppermute | solution.py:279
  214.8 11.9 %collective-permute-start.44 = (bf16[64,1024]{1,0:T(8,128)(2,1)S(1)}, bf16[64,1024]{1,0:T(8,128)(2,1)S(1)}, u32[]{:S(2)}, u32[]{:S(2)}) collective-permute-start(bf16[64,1024]{1,0:T(8,128)(2,1)S(1)} %get-tuple-element.119), channel_id=1, source_target_pairs={{0,1},{1,2},{2,3},{3,0},{4,5},{5,6},{6,7},{7,4},{8,9},{9,10},{10,1... | collective-permute-start | bytes 393224 | tf_op jit(solution)/shard_map/ppermute | solution.py:279
  214.8 53.5 %collective-permute-start.54 = (bf16[256,1792]{1,0:T(8,128)(2,1)S(1)}, bf16[256,1792]{1,0:T(8,128)(2,1)S(1)}, u32[]{:S(2)}, u32[]{:S(2)}) collective-permute-start(bf16[256,1792]{1,0:T(8,128)(2,1)S(1)} %copy-done.16), channel_id=1, source_target_pairs={{16,0},{24,8},{17,1},{25,9},{18,2},{26,10},{19,3},{27,11},{20,4},{... | collective-permute-start | bytes 2752520 | tf_op jit(solution)/shard_map/ppermute | solution.py:407
  216.1 55.5 %collective-permute-start.36 = (bf16[256,1792]{1,0:T(8,128)(2,1)S(1)}, bf16[256,1792]{1,0:T(8,128)(2,1)S(1)}, u32[]{:S(2)}, u32[]{:S(2)}) collective-permute-start(bf16[256,1792]{1,0:T(8,128)(2,1)S(1)} %copy-done.42), channel_id=1, source_target_pairs={{16,0},{24,8},{17,1},{25,9},{18,2},{26,10},{19,3},{27,11},{20,4},{... | collective-permute-start | bytes 2752520 | tf_op jit(solution)/shard_map/ppermute | solution.py:407
  226.9 45.1 %collective-permute-start.55 = (bf16[256,1792]{1,0:T(8,128)(2,1)S(1)}, bf16[256,1792]{1,0:T(8,128)(2,1)S(1)}, u32[]{:S(2)}, u32[]{:S(2)}) collective-permute-start(bf16[256,1792]{1,0:T(8,128)(2,1)S(1)} %copy-done.44), channel_id=1, source_target_pairs={{0,16},{8,24},{1,17},{9,25},{2,18},{10,26},{3,19},{11,27},{4,20},{... | collective-permute-start | bytes 2752520 | tf_op jit(solution)/shard_map/ppermute | solution.py:407
  230.4 48.4 %collective-permute-start.37 = (bf16[256,1792]{1,0:T(8,128)(2,1)S(1)}, bf16[256,1792]{1,0:T(8,128)(2,1)S(1)}, u32[]{:S(2)}, u32[]{:S(2)}) collective-permute-start(bf16[256,1792]{1,0:T(8,128)(2,1)S(1)} %get-tuple-element.112.refs_1_), channel_id=1, source_target_pairs={{0,16},{8,24},{1,17},{9,25},{2,18},{10,26},{3,19},{11,27},{4,20},{... | collective-permute-start | bytes 2752520 | tf_op jit(solution)/shard_map/ppermute | solution.py:407
  268.0 10.9 %collective-permute-start.51 = (bf16[64,1024]{1,0:T(8,128)(2,1)S(1)}, bf16[64,1024]{1,0:T(8,128)(2,1)S(1)}, u32[]{:S(2)}, u32[]{:S(2)}) collective-permute-start(bf16[64,1024]{1,0:T(8,128)(2,1)S(1)} %shard_map.157.refs_0_), channel_id=1, source_target_pairs={{0,1},{1,2},{2,3},{3,0},{4,5},{5,6},{6,7},{7,4},{8,9},{9,10},{10,1... | collective-permute-start | bytes 393224 | tf_op jit(solution)/shard_map/ppermute | solution.py:272
  268.3 10.5 %collective-permute-start.52 = (bf16[64,1024]{1,0:T(8,128)(2,1)S(1)}, bf16[64,1024]{1,0:T(8,128)(2,1)S(1)}, u32[]{:S(2)}, u32[]{:S(2)}) collective-permute-start(bf16[64,1024]{1,0:T(8,128)(2,1)S(1)} %shard_map.157.refs_0_), channel_id=1, source_target_pairs={{0,2},{1,3},{2,0},{3,1},{4,6},{5,7},{6,4},{7,5},{8,10},{9,11},{10,... | collective-permute-start | bytes 393224 | tf_op jit(solution)/shard_map/ppermute | solution.py:272
  272.0 25.2 %collective-permute-start.60 = (bf16[256,2560]{1,0:T(8,128)(2,1)S(1)}, bf16[256,2560]{1,0:T(8,128)(2,1)S(1)}, u32[]{:S(2)}, u32[]{:S(2)}) collective-permute-start(bf16[256,2560]{1,0:T(8,128)(2,1)S(1)} %get-tuple-element.129.refs_5_), channel_id=1, source_target_pairs={{0,16},{8,24},{1,17},{9,25},{2,18},{10,26},{3,19},{11,27},{4,20},{... | collective-permute-start | bytes 3932168 | tf_op jit(solution)/shard_map/ppermute | solution.py:407
  283.2 25.5 %collective-permute-start.56 = (bf16[256,2560]{1,0:T(8,128)(2,1)S(1)}, bf16[256,2560]{1,0:T(8,128)(2,1)S(1)}, u32[]{:S(2)}, u32[]{:S(2)}) collective-permute-start(bf16[256,2560]{1,0:T(8,128)(2,1)S(1)} %get-tuple-element.128.refs_4_), channel_id=1, source_target_pairs={{16,0},{24,8},{17,1},{25,9},{18,2},{26,10},{19,3},{27,11},{20,4},{... | collective-permute-start | bytes 3932168 | tf_op jit(solution)/shard_map/ppermute | solution.py:407
  287.5 9.6 %collective-permute-start.58 = (bf16[64,1024]{1,0:T(8,128)(2,1)S(1)}, bf16[64,1024]{1,0:T(8,128)(2,1)S(1)}, u32[]{:S(2)}, u32[]{:S(2)}) collective-permute-start(bf16[64,1024]{1,0:T(8,128)(2,1)S(1)} %get-tuple-element.132), channel_id=1, source_target_pairs={{0,2},{1,3},{2,0},{3,1},{4,6},{5,7},{6,4},{7,5},{8,10},{9,11},{10,... | collective-permute-start | bytes 393224 | tf_op jit(solution)/shard_map/ppermute | solution.py:279
  287.9 9.1 %collective-permute-start.59 = (bf16[64,1024]{1,0:T(8,128)(2,1)S(1)}, bf16[64,1024]{1,0:T(8,128)(2,1)S(1)}, u32[]{:S(2)}, u32[]{:S(2)}) collective-permute-start(bf16[64,1024]{1,0:T(8,128)(2,1)S(1)} %get-tuple-element.133), channel_id=1, source_target_pairs={{0,1},{1,2},{2,3},{3,0},{4,5},{5,6},{6,7},{7,4},{8,9},{9,10},{10,1... | collective-permute-start | bytes 393224 | tf_op jit(solution)/shard_map/ppermute | solution.py:279
  317.3 34.4 %collective-permute-start.61 = (bf16[2,1,2,352,1024]{4,3,2,1,0:T(8,128)(2,1)S(1)}, bf16[2,1,2,352,1024]{4,3,2,1,0:T(8,128)(2,1)S(1)}, u32[]{:S(2)}, u32[]{:S(2)}) collective-permute-start(bf16[2,1,2,352,1024]{4,3,2,1,0:T(8,128)(2,1)S(1)} %bitcast.97), channel_id=1, source_target_pairs={{0,8},{16,24},{1,9},{17,25},{2,10},{18,26},{3,11},{19,27},{4,12},{... | collective-permute-start | bytes 8650760 | tf_op jit(solution)/shard_map/ppermute | solution.py:321
  326.4 28.1 %collective-permute-start.66 = (bf16[2,1,352,1024]{3,2,1,0:T(8,128)(2,1)}, bf16[2,1,352,1024]{3,2,1,0:T(8,128)(2,1)S(1)}, u32[]{:S(2)}, u32[]{:S(2)}) collective-permute-start(bf16[2,1,352,1024]{3,2,1,0:T(8,128)(2,1)} %bitcast.102), channel_id=1, source_target_pairs={{0,8},{16,24},{1,9},{17,25},{2,10},{18,26},{3,11},{19,27},{4,12},{... | collective-permute-start | bytes 4325384 | tf_op jit(solution)/shard_map/ppermute | solution.py:321
  327.8 23.9 %collective-permute-start.67 = (bf16[256,2560]{1,0:T(8,128)(2,1)S(1)}, bf16[256,2560]{1,0:T(8,128)(2,1)S(1)}, u32[]{:S(2)}, u32[]{:S(2)}) collective-permute-start(bf16[256,2560]{1,0:T(8,128)(2,1)S(1)} %get-tuple-element.141.refs_5_), channel_id=1, source_target_pairs={{0,16},{8,24},{1,17},{9,25},{2,18},{10,26},{3,19},{11,27},{4,20},{... | collective-permute-start | bytes 3932168 | tf_op jit(solution)/shard_map/ppermute | solution.py:407
  331.6 26.6 %collective-permute-start.65 = (bf16[256,2560]{1,0:T(8,128)(2,1)S(1)}, bf16[256,2560]{1,0:T(8,128)(2,1)S(1)}, u32[]{:S(2)}, u32[]{:S(2)}) collective-permute-start(bf16[256,2560]{1,0:T(8,128)(2,1)S(1)} %shard_map.161.refs_4_), channel_id=1, source_target_pairs={{16,0},{24,8},{17,1},{25,9},{18,2},{26,10},{19,3},{27,11},{20,4},{... | collective-permute-start | bytes 3932168 | tf_op jit(solution)/shard_map/ppermute | solution.py:407
  363.2 25.9 %collective-permute-start.69 = (bf16[1,2,704,1024]{3,2,1,0:T(8,128)(2,1)}, bf16[1,2,704,1024]{3,2,1,0:T(8,128)(2,1)}, u32[]{:S(2)}, u32[]{:S(2)}) collective-permute-start(bf16[1,2,704,1024]{3,2,1,0:T(8,128)(2,1)} %shard_map.162), channel_id=1, source_target_pairs={{8,12},{12,8},{24,28},{28,24},{9,13},{13,9},{25,29},{29,25},{10,14... | collective-permute-start | bytes 8650760 | tf_op jit(solution)/shard_map/ppermute | solution.py:453
  371.8 67.6 %collective-permute-start.70 = (bf16[1,2,704,1024]{3,2,1,0:T(8,128)(2,1)}, bf16[1,2,704,1024]{3,2,1,0:T(8,128)(2,1)}, u32[]{:S(2)}, u32[]{:S(2)}) collective-permute-start(bf16[1,2,704,1024]{3,2,1,0:T(8,128)(2,1)} %shard_map.165), channel_id=1, source_target_pairs={{0,4},{4,0},{16,20},{20,16},{1,5},{5,1},{17,21},{21,17},{2,6},{6,2... | collective-permute-start | bytes 8650760 | tf_op jit(solution)/shard_map/ppermute | solution.py:453
  377.7 80.9 %collective-permute-start.72 = (bf16[1,704,1024]{2,1,0:T(8,128)(2,1)}, bf16[1,704,1024]{2,1,0:T(8,128)(2,1)S(1)}, u32[]{:S(2)}, u32[]{:S(2)}) collective-permute-start(bf16[1,704,1024]{2,1,0:T(8,128)(2,1)} %copy-done.13), channel_id=1, source_target_pairs={{8,12},{12,8},{24,28},{28,24},{9,13},{13,9},{25,29},{29,25},{10,14... | collective-permute-start | bytes 4325384 | tf_op jit(solution)/shard_map/ppermute | solution.py:453
  386.3 75.7 %collective-permute-start.73 = (bf16[1,704,1024]{2,1,0:T(8,128)(2,1)S(1)}, bf16[1,704,1024]{2,1,0:T(8,128)(2,1)}, u32[]{:S(2)}, u32[]{:S(2)}) collective-permute-start(bf16[1,704,1024]{2,1,0:T(8,128)(2,1)S(1)} %shard_map.166), channel_id=1, source_target_pairs={{0,4},{4,0},{16,20},{20,16},{1,5},{5,1},{17,21},{21,17},{2,6},{6,2... | collective-permute-start | bytes 4325384 | tf_op jit(solution)/shard_map/ppermute | solution.py:453
  (116 other events, 1541.0 us)

commit v2 on v1

--- a/solution.py
+++ b/solution.py
@@ -1,4 +1,5 @@
 import functools
+import math
 
 import jax
 import jax.numpy as jnp
@@ -20,7 +21,7 @@
 TN = ((0,), (0,))
 
 
-def call(body, outs, args, flops, vmem=20 << 20):
+def call(body, outs, args, flops, vmem=12 << 20):
     moved = sum(a.size * a.dtype.itemsize for a in args)
     return pl.pallas_call(
         body,
@@ -149,15 +150,22 @@
     return call(join_body, [sds(x.shape), sds(x.shape)], [x, own, *parts], 20 * x.size)
 
 
-def bwd_body(tp, blocks, last, *refs):
-    chunks, gates, refs = refs[:tp], refs[tp], refs[tp + 1 :]
+def gather_body(*refs):
+    refs[-1][...] = jnp.concatenate([c[...] for c in refs[:-1]], axis=0)
+
+
+def gather(chunks):
+    rows, width = chunks[0].shape
+    return call(gather_body, [sds((len(chunks) * rows, width))], chunks, 1 << 20)[0]
+
+
+def bwd_body(tp, blocks, last, grad_ref, gates, *refs):
     downs, refs = refs[:blocks], refs[blocks:]
     pairs, outs = ((), refs) if last else (refs[:blocks], refs[blocks:])
-    rows = chunks[0].shape[0]
-    grad = jnp.concatenate([c[...] for c in chunks], axis=0)
+    grad = grad_ref[...]
+    rows = grad.shape[0] // tp
     acts_out = outs[0]
-    ff, width = downs[0].shape
-    acts_out[:, :width] = grad
+    ff = downs[0].shape[0]
     d_norm = None
     for b, down in enumerate(downs):
         d_hidden = dot(grad, down[...], NT)
@@ -165,8 +173,8 @@
         sig = jax.nn.sigmoid(gate)
         d_gate = (d_hidden * up * sig * (1.0 + gate * (1.0 - sig))).astype(BF16)
         d_up = (d_hidden * (gate * sig)).astype(BF16)
-        acts_out[:, span(width, ff, 2 * b)] = d_gate
-        acts_out[:, span(width, ff, 2 * b + 1)] = d_up
+        acts_out[:, span(0, ff, 2 * b)] = d_gate
+        acts_out[:, span(0, ff, 2 * b + 1)] = d_up
         if not last:
             term = dot(d_gate, pairs[b][0], NN) + dot(d_up, pairs[b][1], NN)
             d_norm = term if d_norm is None else d_norm + term
@@ -174,14 +182,14 @@
         put_parts(outs[1:], d_norm, rows)
 
 
-def bwd_layer(chunks, gates, pairs, downs, last):
-    tp, blocks = len(chunks), len(downs)
-    rows, width = chunks[0].shape
-    outs = [sds((tp * rows, width + 2 * blocks * lanes(gates.shape[-1])))]
+def bwd_layer(grad, gates, pairs, downs, tp, last):
+    blocks = len(downs)
+    rows, width = grad.shape[0] // tp, grad.shape[1]
+    outs = [sds((tp * rows, 2 * blocks * lanes(gates.shape[-1])))]
     outs += [] if last else part_shapes(tp, rows, width)
     weights = [*downs] if last else [*downs, *pairs]
     flops = 2 * tp * rows * sum(w.size for w in weights)
-    res = call(functools.partial(bwd_body, tp, blocks, last), outs, [*chunks, gates, *weights], flops)
+    res = call(functools.partial(bwd_body, tp, blocks, last), outs, [grad, gates, *weights], flops)
     return res[0], res[1:]
 
 
@@ -202,64 +210,130 @@
     return call(back_body, [sds(x.shape)], [grad, x, own, *parts], 20 * x.size)[0]
 
 
-def wgrad_body(sources, stages, stage_ref, *refs):
-    pair_out, down_out = refs[-2:]
-    blocks, ff, width = down_out.shape
+def wgrad_body(sources, stages, base, stage_ref, *refs):
+    out = refs[-1]
+    blocks, kinds, ff, width = out.shape
     stage = stage_ref[0]
 
-    def value(late, source, at):
-        out = None
+    def value(side, source, at):
+        picked = None
         for s in range(stages):
-            one = refs[(late * sources + source) * stages + s][:, at]
-            out = one if out is None else jnp.where(stage == s, one, out)
-        return out
-
-    def over(late, b, right):
-        total = None
-        for source in range(sources):
-            term = dot(value(late, source, span(width, ff, b)), rights[right][source], TN)
-            total = term if total is None else total + term
-        return total.astype(BF16)
-
-    top = slice(0, width)
-    rights = [[value(late, source, top) for source in range(sources)] for late in range(2)]
+            one = refs[(side * sources + source) * stages + s][:, at]
+            picked = one if picked is None else jnp.where(stage == s, one, picked)
+        return picked
+
+    rights = [value(1, source, slice(0, width)) for source in range(sources)]
     for b in range(blocks):
-        pair_out[b, 0] = over(1, 2 * b, 0)
-        pair_out[b, 1] = over(1, 2 * b + 1, 0)
-        down_out[b] = over(0, b, 1)
-
-
-def wgrad(stage, blocks, ff, width, acts):
-    sources, stages = len(acts[0]), len(acts[0][0])
-    outs = [sds((blocks, 2, ff, width)), sds((blocks, ff, width))]
-    args = [v for kind in acts for source in kind for v in source]
-    flops = 2 * sources * args[0].shape[0] * 3 * blocks * ff * width
+        for kind in range(kinds):
+            total = None
+            for source in range(sources):
+                left = value(0, source, span(base, ff, kinds * b + kind))
+                term = dot(left, rights[source], TN)
+                total = term if total is None else total + term
+            out[b, kind] = total.astype(BF16)
+
+
+def wgrad(stage, shape, base, lefts, rights):
+    sources, stages = len(lefts), len(lefts[0])
+    args = [v for side in (lefts, rights) for source in side for v in source]
+    flops = 2 * sources * args[0].shape[0] * math.prod(shape)
     return pl.pallas_call(
-        functools.partial(wgrad_body, sources, stages),
-        out_shape=outs,
+        functools.partial(wgrad_body, sources, stages, base),
+        out_shape=sds(shape),
         in_specs=[pl.BlockSpec(memory_space=pltpu.SMEM)] + [VMEM] * len(args),
-        out_specs=[VMEM] * 2,
-        compiler_params=pltpu.CompilerParams(vmem_limit_bytes=40 << 20),
+        out_specs=VMEM,
+        compiler_params=pltpu.CompilerParams(vmem_limit_bytes=32 << 20),
         cost_estimate=pl.CostEstimate(flops=flops, bytes_accessed=flops // 512, transcendentals=0),
     )(stage.astype(jnp.int32).reshape(1), *args)
 
 
-def settle_body(flip, w_ref, own, *refs):
-    other, out = refs if len(refs) == 2 else (None, refs[0])
-    blocks = own.shape[0]
+def tile_rows(size, most=176):
+    return max(r for r in range(16, most + 1, 16) if size % r == 0)
+
+
+def settle_body(flip, blocks, w_ref, own, *refs):
+    other, outs = (refs[0], refs[1:]) if blocks == 2 else (None, refs)
+    kinds, depth = len(outs), outs[0].shape[0]
     size = own.shape[-2]
-    for b in range(blocks):
-        g = own[b].astype(F32)
-        if other is not None:
-            g = g + other[blocks - 1 - b].astype(F32)
-        h = blocks - 1 - b if flip else b
-        at = (Ellipsis, slice(h * size, (h + 1) * size), slice(None))
-        out[at] = (w_ref[at].astype(F32) - INNER_LR * g).astype(BF16)
+    step = tile_rows(size, 48)
+    for d in range(depth):
+        for kind in range(kinds):
+            for b in range(blocks):
+                h = blocks - 1 - b if flip else b
+
+                @pl.loop(0, size // step)
+                def _(i):
+                    at = pl.ds(pl.multiple_of(i * step, 16), step)
+                    to = pl.ds(pl.multiple_of(h * size + i * step, 16), step)
+                    g = own[b, d, kind, at, :].astype(F32)
+                    if other is not None:
+                        g = g + other[blocks - 1 - b, d, kind, at, :].astype(F32)
+                    w = w_ref[d, kind, to, :].astype(F32)
+                    outs[kind][d, to, :] = (w - INNER_LR * g).astype(BF16)
 
 
 def settle(w, own, others, flip):
-    body = functools.partial(settle_body, flip)
-    return call(body, [sds(w.shape)], [w, own, *others], 4 * w.size, 40 << 20)[0]
+    depth, kinds, size, width = w.shape
+    body = functools.partial(settle_body, flip, own.shape[0])
+    outs = [sds((depth, size, width))] * kinds
+    return call(body, outs, [w, own, *others], 4 * w.size, 40 << 20)
+
+
+def update_body(replicas, group, info, *refs):
+    inners, others = refs[:group], refs[group : 2 * group]
+    outer_ref, moment_ref = refs[2 * group : 2 * group + 2]
+    new_out, outer_out, moment_out = refs[-3:]
+    core, chosen = info[0], info[1] == 1
+
+    @pl.loop(0, outer_ref.shape[2] // 16)
+    def _(i):
+        at = pl.ds(pl.multiple_of(i * 16, 16), 16)
+        inner, other = inners[0][0, at, :], others[0][0, at, :]
+        for g in range(1, group):
+            inner = jnp.where(core == g, inners[g][0, at, :], inner)
+            other = jnp.where(core == g, others[g][0, at, :], other)
+        outer, moment = outer_ref[0, 0, at, :], moment_ref[0, 0, at, :]
+        mean = outer - (inner.astype(F32) + other.astype(F32)) / replicas
+        next_moment = MOMENTUM * moment + mean
+        next_outer = outer - OUTER_LR * (mean + MOMENTUM * next_moment)
+        new_out[0, 0, at, :] = jnp.where(chosen, next_outer.astype(BF16), inner)
+        outer_out[0, 0, at, :] = jnp.where(chosen, next_outer, outer)
+        moment_out[0, 0, at, :] = jnp.where(chosen, next_moment, moment)
+
+
+def update(info, kind, replicas, inners, others, outer, moment, done):
+    group = len(inners)
+    depth, kinds, size, width = outer.shape
+    rows = tile_rows(size)
+
+    def member(g):
+        def at(d, i, info):
+            mine = info[0] == g
+            return (jnp.where(mine, d, 0), jnp.where(mine, i, 0), 0)
+
+        return pl.BlockSpec((1, rows, width), at)
+
+    whole = pl.BlockSpec((1, 1, rows, width), lambda d, i, info: (d, kind, i, 0))
+    specs = [member(g) for g in range(group)] * 2 + [whole] * 2
+    specs += [pl.BlockSpec(memory_space=pl.ANY)] * len(done)
+    first = 1 + 2 * group + 2
+    return pl.pallas_call(
+        functools.partial(update_body, replicas, group),
+        out_shape=[sds(outer.shape), sds(outer.shape, F32), sds(outer.shape, F32)],
+        grid_spec=pltpu.PrefetchScalarGridSpec(
+            num_scalar_prefetch=1,
+            grid=(depth, size // rows),
+            in_specs=specs,
+            out_specs=[whole] * 3,
+        ),
+        input_output_aliases={first + i: i for i in range(len(done))},
+        compiler_params=pltpu.CompilerParams(vmem_limit_bytes=60 << 20),
+        cost_estimate=pl.CostEstimate(
+            flops=10 * outer.size // kinds,
+            bytes_accessed=22 * outer.size // kinds,
+            transcendentals=0,
+        ),
+    )(info, *inners, *others, outer, moment, *done)
 
 
 def after(value, *others):
@@ -397,7 +471,8 @@
         layers.append((by_kind[0][d], by_kind[1][d]))
         saved.append(kept)
         if l < count - 1:
-            x, normed = join(x, parts[0], collect(parts))
+            collected = collect(parts)
+            x, normed = join(x, parts[0], collected)
 
     def to_home(value, s):
         out = [value]
@@ -411,35 +486,42 @@
     for l in range(count):
         acts.append([to_home(saved[l][0], l // (group * depth))])
 
-    def grads_of(g):
+    def grads_of(g, pair, ready):
         sets = []
         for d in range(depth):
             of = [acts[(s * group + g) * depth + d] for s in range(stages)]
-            kinds = [[[a[kind][j] for a in of] for j in range(stages)] for kind in range(2)]
-            sets.append(wgrad(stage, group, block, width, kinds))
-        out = []
-        for i in range(2):
-            own = jnp.stack([one[i] for one in sets], axis=1)
-            out.append((own, [to_member(own, g)] if group == 2 else []))
-        return out
-
-    sums = [None] * group
+            kinds = [[[a[kind][j] for a in of] for j in range(stages)] for kind in range(3 if pair else 2)]
+            kinds[-1][1:] = [[after(v, ready) for v in one] for one in kinds[-1][1:]]
+            if pair:
+                shape = (group, 2, block, width)
+                sets.append(wgrad(stage, shape, 0, kinds[2], kinds[0]))
+            else:
+                shape = (group, 1, block, width)
+                sets.append(wgrad(stage, shape, width, kinds[0], kinds[1]))
+        own = jnp.stack(sets, axis=1)
+        return own, [to_member(own, g)] if group == 2 else []
+
+    sums = {}
     for l in reversed(range(count)):
+        s, g = l // (group * depth), (l + 1) // depth
         gates = saved[l][1]
         chunks = seed_chunks if l == count - 1 else spread(grad)
         if l == group * depth - 1:
-            gates = after(gates, *[v for a in acts for kind in a[:1] for v in kind[1:]])
-        if (l + 1) % depth == 0 and 0 < (l + 1) // depth < group:
-            for a in acts[l + 1 :]:
-                a[1][1:] = [after(v, grad) for v in a[1][1:]]
-            sums[(l + 1) // depth] = grads_of((l + 1) // depth)
-            gates = after(gates, *[own for own, _ in sums[(l + 1) // depth]])
-        late, parts = bwd_layer(chunks, gates, *layers[l], l == 0)
-        acts[l].append(to_home(late, l // (group * depth)))
+            gates = after(gates, *[v for a in acts for v in a[0][1:]])
+        whole = gather(chunks)
+        acts[l].append(to_home(whole, s))
+        if (l + 1) % depth == 0 and 0 < g < group:
+            sums[g, True] = grads_of(g, True, grad)
+            gates = after(gates, sums[g, True][0])
+        late, parts = bwd_layer(whole, gates, *layers[l], len(chunks), l == 0)
+        acts[l].append(to_home(late, s))
+        if l < group * depth and l % depth == 0:
+            sums[l // depth, False] = grads_of(l // depth, False, late)
         if l > 0:
-            grad = back(grad, xs[l], parts[0], collect(parts))
-
-    starts = [pairs, downs]
+            collected = collect(parts)
+            grad = back(grad, xs[l], parts[0], collected)
+
+    starts = [pairs, downs[:, None]]
 
     def exchange(inner, member):
         if replicas != 2:
@@ -452,46 +534,36 @@
         ]
         return lax.ppermute(inner, ("section", "rep"), ring)
 
-    inners, others = [[], []], [[], []]
-    ready = acts[0][1][0]
+    inners, others = [[], [], []], [[], [], []]
+    sums[0, True] = grads_of(0, True, acts[0][2][0])
     for g in reversed(range(group)):
-        if sums[g] is None:
-            for a in acts:
-                a[1][1:] = [after(v, ready) for v in a[1][1:]]
-            sums[g] = grads_of(g)
-        for i, (own, away) in enumerate(sums[g]):
-            away = [after(v, ready) for v in away]
-            inner = settle(starts[i], own, away, g > 0)
-            inners[i].insert(0, inner)
-            others[i].insert(0, exchange(inner, g))
-            ready = inner
-
-    flag = lax.dynamic_index_in_dim(fragment, section, 0, keepdims=False)
-    chosen = flag == 1
-
-    def finish(i, outer, moment):
-        inner = choose(core, inners[i])
-        total = inner.astype(F32) + choose(core, others[i]).astype(F32)
-        mean = outer - total / replicas
-        next_moment = MOMENTUM * moment + mean
-        next_outer = outer - OUTER_LR * (mean + MOMENTUM * next_moment)
-        return (
-            jnp.where(chosen, next_outer.astype(BF16), inner),
-            jnp.where(chosen, next_outer, outer),
-            jnp.where(chosen, next_moment, moment),
-        )
+        for i in (1, 0):
+            own, away = sums[g, i == 0]
+            settled = settle(starts[i], own, away, g > 0)
+            for j, inner in enumerate(settled, 2 * i):
+                inners[j].insert(0, inner)
+                others[j].insert(0, exchange(inner, g))
+
+    info = jnp.stack([core, lax.dynamic_index_in_dim(fragment, section, 0, keepdims=False)])
+
+    def finish(kind, first, outer, moment, done):
+        at = kind - first
+        return update(info, at, replicas, inners[kind], others[kind], outer, moment, done)
 
     flip = lambda v: jnp.swapaxes(v, -1, -2)
-    new_in, next_in, next_m_in = finish(0, flip(outer_in), flip(moment_in))
-    outer_down, moment_down = after((outer_down, moment_down), next_in)
-    new_down, next_down, next_m_down = finish(1, outer_down, moment_down)
+    outer_in, moment_in = flip(outer_in), flip(moment_in)
+    outer_down, moment_down = outer_down[:, None], moment_down[:, None]
+    new_down, next_down, next_m_down = finish(2, 2, outer_down, moment_down, [])
+    outer_in, moment_in = after((outer_in, moment_in), next_down)
+    done = finish(0, 0, outer_in, moment_in, [])
+    new_in, next_in, next_m_in = finish(1, 0, outer_in, moment_in, done)
     return (
         flip(new_in)[None],
-        new_down[None],
+        new_down[None, :, 0],
         flip(next_in),
-        next_down,
+        next_down[:, 0],
         flip(next_m_in),
-        next_m_down,
+        next_m_down[:, 0],
     )
 
 

time: 483 us -> 491 us (1.017); the launches traced: 474 us -> 489 us
  waiting for transfers between devices: 235 us -> 264 us
  other arithmetic: 43.3 us -> 15.9 us
  Pallas kernels: 39.2 us -> 63.9 us
  local copies, waits for them, and re-layouts: 44 us -> 31.9 us
    ppermute x24, waiting for transfers between devices: 38.7 us -> 65.4 us  [spread(): lax.ppermute(value, 'tp', [(i, (i + k) % tp) for i in range(tp)])]
    pallas_call x2 -> x7, Pallas kernels: 5.99 us -> 29.9 us  [the longest x3 24.7 us: update(): pl.pallas_call(functools.partial(update_body, replicas, group), out_shape...]
    ppermute x8 -> x12, starting transfers between devices: 18.3 us -> 31.5 us  [to_home(): out.append(lax.ppermute(value, 'section', pairs))]
    select_n x3 -> x0, other arithmetic: 13.2 us -> none  [the longest x2 6.76 us: finish(): jnp.where(chosen, next_outer, outer)]
    ppermute x24, starting transfers between devices: 39.5 us -> 26.4 us  [spread(): lax.ppermute(value, 'tp', [(i, (i + k) % tp) for i in range(tp)])]
    unnamed x180 -> x136, local copies, waits for them, and re-layouts: 31 us -> 18.9 us
    transpose x1 -> x0, other arithmetic: 9.42 us -> none  [shards(): flip = lambda v: jnp.swapaxes(v, -1, -2)]
    ppermute x18, starting transfers between devices: 27.8 us -> 19.6 us  [collect(): lax.ppermute(parts[k], 'tp', [(i, (i - k) % tp) for i in range(tp)])]
  transfers between devices with their start and end apart: 74 -> 80, of which waited for: 40 -> 41; matrix products, arithmetic and copies ran while one was open for 8% -> 5% of each run, Pallas kernels for 6% -> 10%
where the time goes in v2:
time: 491 us; the launch traced here: 489 us
  waiting for transfers between devices  264 us (54%)
  starting transfers between devices  111 us (23%)
  Pallas kernels  63.9 us (13%)
  local copies, waits for them, and re-layouts  31.9 us (6%)
  other arithmetic  15.9 us (3%)
    ppermute x18, waiting for transfers between devices, collect(): lax.ppermute(parts[k], 'tp', [(i, (i - k) % tp) for i in range(tp)])  68.3 us
    ppermute x24, waiting for transfers between devices, spread(): lax.ppermute(value, 'tp', [(i, (i + k) % tp) for i in range(tp)])  65.4 us
    ppermute x6, waiting for transfers between devices, exchange(): return lax.ppermute(inner, ('section', 'rep'), ring)  58 us
    ppermute x5, waiting for transfers between devices, shift(): return lax.ppermute(value, 'section', pairs)  38.3 us
    pallas_call x24, Pallas kernels, call(): pl.pallas_call(body, out_shape=outs, in_specs=[VMEM] * len(args), out_spe...  34 us
    ppermute x12, starting transfers between devices, to_home(): out.append(lax.ppermute(value, 'section', pairs))  31.5 us
    ppermute x12, waiting for transfers between devices, to_home(): out.append(lax.ppermute(value, 'section', pairs))  31.2 us
    ppermute x24, starting transfers between devices, spread(): lax.ppermute(value, 'tp', [(i, (i + k) % tp) for i in range(tp)])  26.4 us
  transfers between devices with their start and end apart: 80, of which 41 were waited for; matrix products, arithmetic and copies ran while one was open for 5% of the time, Pallas kernels for 10%

profile of v2, /device:TPU:0, one launch (start us, length us, event | category | flops | bytes accessed | tf_op | source)
XLA Modules:
  0.0 488.6 jit_solution(54474524711430715)
XLA Ops:
  7.1 3.8 bitcast_select_fusion
  13.8 6.8 %gather_fusion = bf16[256,1024]{1,0:T(8,128)(2,1)} fusion(bf16[4096,1024]{1,0:T(8,128)(2,1)} %param.11, s32[1024]{0:T(1024)S(1)} %pad_clamp_fusion), kind=kCustom, calls=%fused_computation | custom fusion | bytes 1049600 | tf_op jit(solution)/shard_map/jit(_take)/gather | solution.py:440
  24.1 24.7 %collective-permute-done.1.refs_1_ = bf16[64,1024]{1,0:T(8,128)(2,1)} collective-permute-done((bf16[64,1024]{1,0:T(8,128)(2,1)}, bf16[64,1024]{1,0:T(8,128)(2,1)}, u32[]{:S(2)}, u32[]{:S(2)}) %collective-permute-start.1) | collective-permute-done | bytes 131104 | tf_op jit(solution)/shard_map/ppermute | solution.py:391
  55.1 3.7 collective-permute-start.4
  59.2 3.4 collective-permute-done.4.refs_3_
  62.6 8.3 %collective-permute-done.3.refs_2_ = bf16[64,1024]{1,0:T(8,128)(2,1)S(1)} collective-permute-done((bf16[64,1024]{1,0:T(8,128)(2,1)S(1)}, bf16[64,1024]{1,0:T(8,128)(2,1)S(1)}, u32[]{:S(2)}, u32[]{:S(2)}) %collective-permute-start.3) | collective-permute-done | bytes 131104 | tf_op jit(solution)/shard_map/ppermute | solution.py:346
  74.3 3.5 collective-permute-start.11
  81.8 8.1 %collective-permute-done.12.refs_3_ = bf16[64,1024]{1,0:T(8,128)(2,1)S(1)} collective-permute-done((bf16[64,1024]{1,0:T(8,128)(2,1)S(1)}, bf16[64,1024]{1,0:T(8,128)(2,1)S(1)}, u32[]{:S(2)}, u32[]{:S(2)}) %collective-permute-start.12) | collective-permute-done | bytes 131104 | tf_op jit(solution)/shard_map/ppermute | solution.py:353
  96.8 4.7 collective-permute-done.17
  106.6 8.9 %collective-permute-done.19 = bf16[1,352,1024]{2,1,0:T(8,128)(2,1)S(1)} collective-permute-done((bf16[1,352,1024]{2,1,0:T(8,128)(2,1)S(1)}, bf16[1,352,1024]{2,1,0:T(8,128)(2,1)S(1)}, u32[]{:S(2)}, u32[]{:S(2)}) %collective-permute-start.19) | collective-permute-done | bytes 720928 | tf_op jit(solution)/shard_map/ppermute | solution.py:391
  119.2 4.2 shard_map.149
  124.6 3.5 collective-permute-start.21
  132.1 7.7 %collective-permute-done.22.refs_3_ = bf16[64,1024]{1,0:T(8,128)(2,1)S(1)} collective-permute-done((bf16[64,1024]{1,0:T(8,128)(2,1)S(1)}, bf16[64,1024]{1,0:T(8,128)(2,1)S(1)}, u32[]{:S(2)}, u32[]{:S(2)}) %collective-permute-start.22) | collective-permute-done | bytes 131104 | tf_op jit(solution)/shard_map/ppermute | solution.py:353
  145.6 8.3 %collective-permute-done.25.refs_2_ = bf16[64,1024]{1,0:T(8,128)(2,1)S(1)} collective-permute-done((bf16[64,1024]{1,0:T(8,128)(2,1)S(1)}, bf16[64,1024]{1,0:T(8,128)(2,1)S(1)}, u32[]{:S(2)}, u32[]{:S(2)}) %collective-permute-start.25) | collective-permute-done | bytes 131104 | tf_op jit(solution)/shard_map/ppermute | solution.py:346
  166.7 7.2 %collective-permute-done.30.refs_3_ = bf16[64,1024]{1,0:T(8,128)(2,1)S(1)} collective-permute-done((bf16[64,1024]{1,0:T(8,128)(2,1)S(1)}, bf16[64,1024]{1,0:T(8,128)(2,1)S(1)}, u32[]{:S(2)}, u32[]{:S(2)}) %collective-permute-start.30) | collective-permute-done | bytes 131104 | tf_op jit(solution)/shard_map/ppermute | solution.py:353
  180.7 7.8 %collective-permute-done.36.refs_2_ = bf16[64,1024]{1,0:T(8,128)(2,1)S(1)} collective-permute-done((bf16[64,1024]{1,0:T(8,128)(2,1)S(1)}, bf16[64,1024]{1,0:T(8,128)(2,1)S(1)}, u32[]{:S(2)}, u32[]{:S(2)}) %collective-permute-start.36) | collective-permute-done | bytes 131104 | tf_op jit(solution)/shard_map/ppermute | solution.py:346
  193.1 4.9 %collective-permute-done.34.refs_3_ = bf16[64,1024]{1,0:T(8,128)(2,1)S(1)} collective-permute-done((bf16[64,1024]{1,0:T(8,128)(2,1)S(1)}, bf16[64,1024]{1,0:T(8,128)(2,1)S(1)}, u32[]{:S(2)}, u32[]{:S(2)}) %collective-permute-start.34) | collective-permute-done | bytes 131104 | tf_op jit(solution)/shard_map/ppermute | solution.py:346
  198.0 5.6 %collective-permute-done.33.refs_2_ = bf16[64,1024]{1,0:T(8,128)(2,1)S(1)} collective-permute-done((bf16[64,1024]{1,0:T(8,128)(2,1)S(1)}, bf16[64,1024]{1,0:T(8,128)(2,1)S(1)}, u32[]{:S(2)}, u32[]{:S(2)}) %collective-permute-start.33) | collective-permute-done | bytes 131104 | tf_op jit(solution)/shard_map/ppermute | solution.py:346
  207.3 3.2 shard_map.154
  210.6 4.5 shard_map.155
  220.4 9.5 %collective-permute-done.41.refs_4_ = bf16[64,1024]{1,0:T(8,128)(2,1)S(1)} collective-permute-done((bf16[64,1024]{1,0:T(8,128)(2,1)S(1)}, bf16[64,1024]{1,0:T(8,128)(2,1)S(1)}, u32[]{:S(2)}, u32[]{:S(2)}) %collective-permute-start.41) | collective-permute-done | bytes 131104 | tf_op jit(solution)/shard_map/ppermute | solution.py:353
  236.0 4.3 collective-permute-start.54
  243.0 3.5 collective-permute-start.55
  248.8 5.0 %collective-permute-done.46.refs_3_ = bf16[64,1024]{1,0:T(8,128)(2,1)S(1)} collective-permute-done((bf16[64,1024]{1,0:T(8,128)(2,1)S(1)}, bf16[64,1024]{1,0:T(8,128)(2,1)S(1)}, u32[]{:S(2)}, u32[]{:S(2)}) %collective-permute-start.46) | collective-permute-done | bytes 131104 | tf_op jit(solution)/shard_map/ppermute | solution.py:353
  253.8 6.6 %collective-permute-done.47.refs_4_ = bf16[64,1024]{1,0:T(8,128)(2,1)S(1)} collective-permute-done((bf16[64,1024]{1,0:T(8,128)(2,1)S(1)}, bf16[64,1024]{1,0:T(8,128)(2,1)S(1)}, u32[]{:S(2)}, u32[]{:S(2)}) %collective-permute-start.47) | collective-permute-done | bytes 131104 | tf_op jit(solution)/shard_map/ppermute | solution.py:353
  260.3 7.3 %collective-permute-done.48.refs_5_ = bf16[64,1024]{1,0:T(8,128)(2,1)S(1)} collective-permute-done((bf16[64,1024]{1,0:T(8,128)(2,1)S(1)}, bf16[64,1024]{1,0:T(8,128)(2,1)S(1)}, u32[]{:S(2)}, u32[]{:S(2)}) %collective-permute-start.48) | collective-permute-done | bytes 131104 | tf_op jit(solution)/shard_map/ppermute | solution.py:353
  268.3 4.6 collective-permute-done.51.refs_3_
  272.8 8.7 %collective-permute-done.50.refs_2_ = bf16[64,1024]{1,0:T(8,128)(2,1)S(1)} collective-permute-done((bf16[64,1024]{1,0:T(8,128)(2,1)S(1)}, bf16[64,1024]{1,0:T(8,128)(2,1)S(1)}, u32[]{:S(2)}, u32[]{:S(2)}) %collective-permute-start.50) | collective-permute-done | bytes 131104 | tf_op jit(solution)/shard_map/ppermute | solution.py:346
  281.5 6.8 %collective-permute-done.49.refs_1_ = bf16[64,1024]{1,0:T(8,128)(2,1)S(1)} collective-permute-done((bf16[64,1024]{1,0:T(8,128)(2,1)S(1)}, bf16[64,1024]{1,0:T(8,128)(2,1)S(1)}, u32[]{:S(2)}, u32[]{:S(2)}) %collective-permute-start.49) | collective-permute-done | bytes 131104 | tf_op jit(solution)/shard_map/ppermute | solution.py:346
  289.7 4.3 shard_map.161
  297.6 4.6 collective-permute-done.56.refs_3_
  309.8 7.3 %collective-permute-start.65 = (bf16[256,1536]{1,0:T(8,128)(2,1)S(1)}, bf16[256,1536]{1,0:T(8,128)(2,1)S(1)}, u32[]{:S(2)}, u32[]{:S(2)}) collective-permute-start(bf16[256,1536]{1,0:T(8,128)(2,1)S(1)} %get-tuple-element.146.refs_1_), channel_id=1, source_target_pairs={{0,16},{8,24},{1,17},{9,25},{2,18},{10,26},{3,19},{11,27},{4,20},{... | collective-permute-start | bytes 2359304 | tf_op jit(solution)/shard_map/ppermute | solution.py:482
  321.1 5.9 %collective-permute-start.74 = (bf16[256,1024]{1,0:T(8,128)(2,1)S(1)}, bf16[256,1024]{1,0:T(8,128)(2,1)S(1)}, u32[]{:S(2)}, u32[]{:S(2)}) collective-permute-start(bf16[256,1024]{1,0:T(8,128)(2,1)S(1)} %shard_map.153.grad_ref.refs_5_), channel_id=1, source_target_pairs={{0,16},{8,24},{1,17},{9,25},{2,18},{10,26},{3,19},{11,27},{4,20},{... | collective-permute-start | bytes 1572872 | tf_op jit(solution)/shard_map/ppermute | solution.py:482
  328.3 9.4 %collective-permute-done.74.refs_7_ = bf16[256,1024]{1,0:T(8,128)(2,1)S(1)} collective-permute-done((bf16[256,1024]{1,0:T(8,128)(2,1)S(1)}, bf16[256,1024]{1,0:T(8,128)(2,1)S(1)}, u32[]{:S(2)}, u32[]{:S(2)}) %collective-permute-start.74) | collective-permute-done | bytes 524320 | tf_op jit(solution)/shard_map/ppermute | solution.py:482
  337.7 8.2 %collective-permute-done.73.refs_6_ = bf16[256,1024]{1,0:T(8,128)(2,1)S(1)} collective-permute-done((bf16[256,1024]{1,0:T(8,128)(2,1)S(1)}, bf16[256,1024]{1,0:T(8,128)(2,1)S(1)}, u32[]{:S(2)}, u32[]{:S(2)}) %collective-permute-start.73) | collective-permute-done | bytes 524320 | tf_op jit(solution)/shard_map/ppermute | solution.py:482
  351.4 3.4 collective-permute-start.75
  357.7 9.4 %collective-permute-done.71.refs_7_ = bf16[256,1024]{1,0:T(8,128)(2,1)S(1)} collective-permute-done((bf16[256,1024]{1,0:T(8,128)(2,1)S(1)}, bf16[256,1024]{1,0:T(8,128)(2,1)S(1)}, u32[]{:S(2)}, u32[]{:S(2)}) %collective-permute-start.71) | collective-permute-done | bytes 524320 | tf_op jit(solution)/shard_map/ppermute | solution.py:482
  367.1 4.1 collective-permute-done.70.refs_6_
  379.3 7.5 %collective-permute-start.76 = (bf16[1,704,1024]{2,1,0:T(8,128)(2,1)}, bf16[1,704,1024]{2,1,0:T(8,128)(2,1)}, u32[]{:S(2)}, u32[]{:S(2)}) collective-permute-start(bf16[1,704,1024]{2,1,0:T(8,128)(2,1)} %shard_map.170.refs_0_), channel_id=1, source_target_pairs={{0,4},{4,0},{16,20},{20,16},{1,5},{5,1},{17,21},{21,17},{2,6},{6,2... | collective-permute-start | bytes 4325384 | tf_op jit(solution)/shard_map/ppermute | solution.py:535
  386.9 3.0 shard_map.168
  391.8 3.2 shard_map.167
  398.8 3.9 collective-permute-start.68
  404.6 15.0 %collective-permute-done.76.refs_2_ = bf16[1,704,1024]{2,1,0:T(8,128)(2,1)} collective-permute-done((bf16[1,704,1024]{2,1,0:T(8,128)(2,1)}, bf16[1,704,1024]{2,1,0:T(8,128)(2,1)}, u32[]{:S(2)}, u32[]{:S(2)}) %collective-permute-start.76) | collective-permute-done | bytes 1441824 | tf_op jit(solution)/shard_map/ppermute | solution.py:535
  419.6 8.2 %shard_map.173 = (bf16[1,1,704,1024]{3,2,1,0:T(8,128)(2,1)}, f32[1,1,704,1024]{3,2,1,0:T(8,128)}, f32[1,1,704,1024]{3,2,1,0:T(8,128)}) custom-call(s32[2]{0:T(128)} %pad_add_fusion.info, bf16[1,704,1024]{2,1,0:T(8,128)(2,1)} %shard_map.170.refs_0_, bf16[1,704,1024]{2,1,0:T(8,128)(2,1)} %copy-done.14, bf16[1,704,1024]{2,1,0:T(8,128)(2,1)} %collective-permute-done.76.refs_2_, ...), custom_call_target="tpu_custom_call" | custom-call | flops 7208960 | bytes 15859712 | tf_op jit(solution)/shard_map/pallas_call | solution.py:320
  427.8 22.7 %collective-permute-done.78.refs_2_ = bf16[1,704,1024]{2,1,0:T(8,128)(2,1)} collective-permute-done((bf16[1,704,1024]{2,1,0:T(8,128)(2,1)}, bf16[1,704,1024]{2,1,0:T(8,128)(2,1)}, u32[]{:S(2)}, u32[]{:S(2)}) %collective-permute-start.78) | collective-permute-done | bytes 1441824 | tf_op jit(solution)/shard_map/ppermute | solution.py:535
  450.5 8.2 %shard_map.174 = (bf16[1,2,704,1024]{3,2,1,0:T(8,128)(2,1)}, f32[1,2,704,1024]{3,2,1,0:T(8,128)}, f32[1,2,704,1024]{3,2,1,0:T(8,128)}) custom-call(s32[2]{0:T(128)} %pad_add_fusion.info, bf16[1,704,1024]{2,1,0:T(8,128)(2,1)} %get-tuple-element.158.refs_0_, bf16[1,704,1024]{2,1,0:T(8,128)(2,1)} %get-tuple-element.159.refs_1_, ...), custom_call_target="tpu_custom_call" | custom-call | flops 7208960 | bytes 15859712 | tf_op jit(solution)/shard_map/pallas_call | solution.py:320
  458.7 20.3 %collective-permute-done.68.refs_2_ = bf16[1,704,1024]{2,1,0:T(8,128)(2,1)S(1)} collective-permute-done((bf16[1,704,1024]{2,1,0:T(8,128)(2,1)}, bf16[1,704,1024]{2,1,0:T(8,128)(2,1)S(1)}, u32[]{:S(2)}, u32[]{:S(2)}) %collective-permute-start.68) | collective-permute-done | bytes 1441824 | tf_op jit(solution)/shard_map/ppermute | solution.py:535
  480.1 8.3 %shard_map.175 = (bf16[1,2,704,1024]{3,2,1,0:T(8,128)(2,1)}, f32[1,2,704,1024]{3,2,1,0:T(8,128)}, f32[1,2,704,1024]{3,2,1,0:T(8,128)}) custom-call(s32[2]{0:T(128)} %pad_add_fusion.info, bf16[1,704,1024]{2,1,0:T(8,128)(2,1)} %get-tuple-element.149.refs_0_, ...), custom_call_target="tpu_custom_call", output_to_operand_aliasing={{0}: (7, {}), {1}: (8, {}), {2}: (9, {})} | custom-call | flops 7208960 | bytes 15859712 | tf_op jit(solution)/shard_map/pallas_call | solution.py:320
  (306 shorter events, 140.7 us)
Async XLA Ops:
  10.9 42.4 %collective-permute-start.6 = (bf16[1,2,352,1024]{3,2,1,0:T(8,128)(2,1)}, bf16[1,2,352,1024]{3,2,1,0:T(8,128)(2,1)}, u32[]{:S(2)}, u32[]{:S(2)}) collective-permute-start(bf16[1,2,352,1024]{3,2,1,0:T(8,128)(2,1)} %get-tuple-element.90), channel_id=1, source_target_pairs={{0,16},{8,24},{16,0},{24,8},{1,17},{9,25},{17,1},{25,9},{2,18},{10... | collective-permute-start | bytes 4325384 | tf_op jit(solution)/shard_map/ppermute | solution.py:391
  21.9 27.9 %collective-permute-start.8 = (bf16[1,352,1024]{2,1,0:T(8,128)(2,1)}, bf16[1,352,1024]{2,1,0:T(8,128)(2,1)}, u32[]{:S(2)}, u32[]{:S(2)}) collective-permute-start(bf16[1,352,1024]{2,1,0:T(8,128)(2,1)} %dynamic-slice_bitcast_fusion.1), channel_id=1, source_target_pairs={{0,8},{8,0},{16,24},{24,16},{1,9},{9,1},{17,25},{25,17},{2,10},{10... | collective-permute-start | bytes 2162696 | tf_op jit(solution)/shard_map/ppermute | solution.py:387
  24.1 24.7 %collective-permute-start.1 = (bf16[64,1024]{1,0:T(8,128)(2,1)}, bf16[64,1024]{1,0:T(8,128)(2,1)}, u32[]{:S(2)}, u32[]{:S(2)}) collective-permute-start(bf16[64,1024]{1,0:T(8,128)(2,1)} %get-tuple-element.174), channel_id=1, source_target_pairs={{0,16},{8,24},{16,0},{24,8},{1,17},{9,25},{17,1},{25,9},{2,18},{10... | collective-permute-start | bytes 393224 | tf_op jit(solution)/shard_map/ppermute | solution.py:391
  51.5 19.4 %collective-permute-start.9 = (bf16[1,352,1024]{2,1,0:T(8,128)(2,1)S(1)}, bf16[1,352,1024]{2,1,0:T(8,128)(2,1)S(1)}, u32[]{:S(2)}, u32[]{:S(2)}) collective-permute-start(bf16[1,352,1024]{2,1,0:T(8,128)(2,1)S(1)} %get-tuple-element.93), channel_id=1, source_target_pairs={{0,16},{8,24},{16,0},{24,8},{1,17},{9,25},{17,1},{25,9},{2,18},{10... | collective-permute-start | bytes 2162696 | tf_op jit(solution)/shard_map/ppermute | solution.py:391
  55.0 16.2 %collective-permute-start.7 = (bf16[1,2,352,1024]{3,2,1,0:T(8,128)(2,1)S(1)}, bf16[1,2,352,1024]{3,2,1,0:T(8,128)(2,1)S(1)}, u32[]{:S(2)}, u32[]{:S(2)}) collective-permute-start(bf16[1,2,352,1024]{3,2,1,0:T(8,128)(2,1)S(1)} %broadcast_select_fusion.3), channel_id=1, source_target_pairs={{0,8},{8,0},{16,24},{24,16},{1,9},{9,1},{17,25},{25,17},{2,10},{10... | collective-permute-start | bytes 4325384 | tf_op jit(solution)/shard_map/ppermute | solution.py:387
  58.7 42.8 %collective-permute-start.17 = (bf16[1,2,352,1024]{3,2,1,0:T(8,128)(2,1)S(1)}, bf16[1,2,352,1024]{3,2,1,0:T(8,128)(2,1)S(1)}, u32[]{:S(2)}, u32[]{:S(2)}) collective-permute-start(bf16[1,2,352,1024]{3,2,1,0:T(8,128)(2,1)S(1)} %copy-done.51), channel_id=1, source_target_pairs={{0,16},{8,24},{16,0},{24,8},{1,17},{9,25},{17,1},{25,9},{2,18},{10... | collective-permute-start | bytes 4325384 | tf_op jit(solution)/shard_map/ppermute | solution.py:391
  77.8 12.1 %collective-permute-start.12 = (bf16[64,1024]{1,0:T(8,128)(2,1)S(1)}, bf16[64,1024]{1,0:T(8,128)(2,1)S(1)}, u32[]{:S(2)}, u32[]{:S(2)}) collective-permute-start(bf16[64,1024]{1,0:T(8,128)(2,1)S(1)} %get-tuple-element.97), channel_id=1, source_target_pairs={{0,2},{1,3},{2,0},{3,1},{4,6},{5,7},{6,4},{7,5},{8,10},{9,11},{10,... | collective-permute-start | bytes 393224 | tf_op jit(solution)/shard_map/ppermute | solution.py:353
  77.8 12.1 %collective-permute-start.13 = (bf16[64,1024]{1,0:T(8,128)(2,1)S(1)}, bf16[64,1024]{1,0:T(8,128)(2,1)S(1)}, u32[]{:S(2)}, u32[]{:S(2)}) collective-permute-start(bf16[64,1024]{1,0:T(8,128)(2,1)S(1)} %get-tuple-element.98), channel_id=1, source_target_pairs={{0,1},{1,2},{2,3},{3,0},{4,5},{5,6},{6,7},{7,4},{8,9},{9,10},{10,1... | collective-permute-start | bytes 393224 | tf_op jit(solution)/shard_map/ppermute | solution.py:353
  91.5 12.6 %collective-permute-start.15 = (bf16[64,1024]{1,0:T(8,128)(2,1)S(1)}, bf16[64,1024]{1,0:T(8,128)(2,1)S(1)}, u32[]{:S(2)}, u32[]{:S(2)}) collective-permute-start(bf16[64,1024]{1,0:T(8,128)(2,1)S(1)} %get-tuple-element.100.refs_0_), channel_id=1, source_target_pairs={{0,2},{1,3},{2,0},{3,1},{4,6},{5,7},{6,4},{7,5},{8,10},{9,11},{10,... | collective-permute-start | bytes 393224 | tf_op jit(solution)/shard_map/ppermute | solution.py:346
  92.7 12.0 %collective-permute-start.14 = (bf16[64,1024]{1,0:T(8,128)(2,1)S(1)}, bf16[64,1024]{1,0:T(8,128)(2,1)S(1)}, u32[]{:S(2)}, u32[]{:S(2)}) collective-permute-start(bf16[64,1024]{1,0:T(8,128)(2,1)S(1)} %get-tuple-element.100.refs_0_), channel_id=1, source_target_pairs={{0,1},{1,2},{2,3},{3,0},{4,5},{5,6},{6,7},{7,4},{8,9},{9,10},{10,1... | collective-permute-start | bytes 393224 | tf_op jit(solution)/shard_map/ppermute | solution.py:346
  95.3 20.2 %collective-permute-start.19 = (bf16[1,352,1024]{2,1,0:T(8,128)(2,1)S(1)}, bf16[1,352,1024]{2,1,0:T(8,128)(2,1)S(1)}, u32[]{:S(2)}, u32[]{:S(2)}) collective-permute-start(bf16[1,352,1024]{2,1,0:T(8,128)(2,1)S(1)} %get-tuple-element.103), channel_id=1, source_target_pairs={{0,16},{8,24},{16,0},{24,8},{1,17},{9,25},{17,1},{25,9},{2,18},{10... | collective-permute-start | bytes 2162696 | tf_op jit(solution)/shard_map/ppermute | solution.py:391
  106.6 12.5 %collective-permute-start.18 = (bf16[1,2,352,1024]{3,2,1,0:T(8,128)(2,1)}, bf16[1,2,352,1024]{3,2,1,0:T(8,128)(2,1)}, u32[]{:S(2)}, u32[]{:S(2)}) collective-permute-start(bf16[1,2,352,1024]{3,2,1,0:T(8,128)(2,1)} %broadcast_select_fusion.2), channel_id=1, source_target_pairs={{0,8},{8,0},{16,24},{24,16},{1,9},{9,1},{17,25},{25,17},{2,10},{10... | collective-permute-start | bytes 4325384 | tf_op jit(solution)/shard_map/ppermute | solution.py:387
  118.3 37.6 %collective-permute-start.27 = (bf16[1,2,352,1024]{3,2,1,0:T(8,128)(2,1)S(1)}, bf16[1,2,352,1024]{3,2,1,0:T(8,128)(2,1)S(1)}, u32[]{:S(2)}, u32[]{:S(2)}) collective-permute-start(bf16[1,2,352,1024]{3,2,1,0:T(8,128)(2,1)S(1)} %broadcast_select_fusion.1), channel_id=1, source_target_pairs={{0,8},{8,0},{16,24},{24,16},{1,9},{9,1},{17,25},{25,17},{2,10},{10... | collective-permute-start | bytes 4325384 | tf_op jit(solution)/shard_map/ppermute | solution.py:387
  141.5 12.5 %collective-permute-start.25 = (bf16[64,1024]{1,0:T(8,128)(2,1)S(1)}, bf16[64,1024]{1,0:T(8,128)(2,1)S(1)}, u32[]{:S(2)}, u32[]{:S(2)}) collective-permute-start(bf16[64,1024]{1,0:T(8,128)(2,1)S(1)} %get-tuple-element.110.refs_0_), channel_id=1, source_target_pairs={{0,2},{1,3},{2,0},{3,1},{4,6},{5,7},{6,4},{7,5},{8,10},{9,11},{10,... | collective-permute-start | bytes 393224 | tf_op jit(solution)/shard_map/ppermute | solution.py:346
  155.4 48.3 %collective-permute-start.38 = (bf16[1,2,352,1024]{3,2,1,0:T(8,128)(2,1)}, bf16[1,2,352,1024]{3,2,1,0:T(8,128)(2,1)}, u32[]{:S(2)}, u32[]{:S(2)}) collective-permute-start(bf16[1,2,352,1024]{3,2,1,0:T(8,128)(2,1)} %broadcast_select_fusion), channel_id=1, source_target_pairs={{0,8},{8,0},{16,24},{24,16},{1,9},{9,1},{17,25},{25,17},{2,10},{10... | collective-permute-start | bytes 4325384 | tf_op jit(solution)/shard_map/ppermute | solution.py:387
  160.4 13.5 %collective-permute-start.30 = (bf16[64,1024]{1,0:T(8,128)(2,1)S(1)}, bf16[64,1024]{1,0:T(8,128)(2,1)S(1)}, u32[]{:S(2)}, u32[]{:S(2)}) collective-permute-start(bf16[64,1024]{1,0:T(8,128)(2,1)S(1)} %get-tuple-element.115), channel_id=1, source_target_pairs={{0,2},{1,3},{2,0},{3,1},{4,6},{5,7},{6,4},{7,5},{8,10},{9,11},{10,... | collective-permute-start | bytes 393224 | tf_op jit(solution)/shard_map/ppermute | solution.py:353
  161.7 12.2 %collective-permute-start.31 = (bf16[64,1024]{1,0:T(8,128)(2,1)S(1)}, bf16[64,1024]{1,0:T(8,128)(2,1)S(1)}, u32[]{:S(2)}, u32[]{:S(2)}) collective-permute-start(bf16[64,1024]{1,0:T(8,128)(2,1)S(1)} %get-tuple-element.116), channel_id=1, source_target_pairs={{0,1},{1,2},{2,3},{3,0},{4,5},{5,6},{6,7},{7,4},{8,9},{9,10},{10,1... | collective-permute-start | bytes 393224 | tf_op jit(solution)/shard_map/ppermute | solution.py:353
  174.7 13.7 %collective-permute-start.36 = (bf16[64,1024]{1,0:T(8,128)(2,1)S(1)}, bf16[64,1024]{1,0:T(8,128)(2,1)S(1)}, u32[]{:S(2)}, u32[]{:S(2)}) collective-permute-start(bf16[64,1024]{1,0:T(8,128)(2,1)S(1)} %get-tuple-element.118.refs_0_), channel_id=1, source_target_pairs={{0,2},{1,3},{2,0},{3,1},{4,6},{5,7},{6,4},{7,5},{8,10},{9,11},{10,... | collective-permute-start | bytes 393224 | tf_op jit(solution)/shard_map/ppermute | solution.py:346
  176.4 12.7 %collective-permute-start.35 = (bf16[64,1024]{1,0:T(8,128)(2,1)S(1)}, bf16[64,1024]{1,0:T(8,128)(2,1)S(1)}, u32[]{:S(2)}, u32[]{:S(2)}) collective-permute-start(bf16[64,1024]{1,0:T(8,128)(2,1)S(1)} %get-tuple-element.118.refs_0_), channel_id=1, source_target_pairs={{0,1},{1,2},{2,3},{3,0},{4,5},{5,6},{6,7},{7,4},{8,9},{9,10},{10,1... | collective-permute-start | bytes 393224 | tf_op jit(solution)/shard_map/ppermute | solution.py:346
  190.8 19.7 %collective-permute-start.39 = (bf16[1,352,1024]{2,1,0:T(8,128)(2,1)}, bf16[1,352,1024]{2,1,0:T(8,128)(2,1)}, u32[]{:S(2)}, u32[]{:S(2)}) collective-permute-start(bf16[1,352,1024]{2,1,0:T(8,128)(2,1)} %broadcast_select_fusion.4), channel_id=1, source_target_pairs={{0,8},{8,0},{16,24},{24,16},{1,9},{9,1},{17,25},{25,17},{2,10},{10... | collective-permute-start | bytes 2162696 | tf_op jit(solution)/shard_map/ppermute | solution.py:387
  190.8 12.8 %collective-permute-start.33 = (bf16[64,1024]{1,0:T(8,128)(2,1)S(1)}, bf16[64,1024]{1,0:T(8,128)(2,1)S(1)}, u32[]{:S(2)}, u32[]{:S(2)}) collective-permute-start(bf16[64,1024]{1,0:T(8,128)(2,1)S(1)} %constant_dynamic-slice_fusion.refs_0_), channel_id=1, source_target_pairs={{0,2},{1,3},{2,0},{3,1},{4,6},{5,7},{6,4},{7,5},{8,10},{9,11},{10,... | collective-permute-start | bytes 393224 | tf_op jit(solution)/shard_map/ppermute | solution.py:346
  191.1 12.5 %collective-permute-start.32 = (bf16[64,1024]{1,0:T(8,128)(2,1)S(1)}, bf16[64,1024]{1,0:T(8,128)(2,1)S(1)}, u32[]{:S(2)}, u32[]{:S(2)}) collective-permute-start(bf16[64,1024]{1,0:T(8,128)(2,1)S(1)} %constant_dynamic-slice_fusion.refs_0_), channel_id=1, source_target_pairs={{0,1},{1,2},{2,3},{3,0},{4,5},{5,6},{6,7},{7,4},{8,9},{9,10},{10,1... | collective-permute-start | bytes 393224 | tf_op jit(solution)/shard_map/ppermute | solution.py:346
  216.0 14.0 %collective-permute-start.41 = (bf16[64,1024]{1,0:T(8,128)(2,1)S(1)}, bf16[64,1024]{1,0:T(8,128)(2,1)S(1)}, u32[]{:S(2)}, u32[]{:S(2)}) collective-permute-start(bf16[64,1024]{1,0:T(8,128)(2,1)S(1)} %get-tuple-element.124), channel_id=1, source_target_pairs={{0,2},{1,3},{2,0},{3,1},{4,6},{5,7},{6,4},{7,5},{8,10},{9,11},{10,... | collective-permute-start | bytes 393224 | tf_op jit(solution)/shard_map/ppermute | solution.py:353
  217.9 12.1 %collective-permute-start.42 = (bf16[64,1024]{1,0:T(8,128)(2,1)S(1)}, bf16[64,1024]{1,0:T(8,128)(2,1)S(1)}, u32[]{:S(2)}, u32[]{:S(2)}) collective-permute-start(bf16[64,1024]{1,0:T(8,128)(2,1)S(1)} %get-tuple-element.125), channel_id=1, source_target_pairs={{0,1},{1,2},{2,3},{3,0},{4,5},{5,6},{6,7},{7,4},{8,9},{9,10},{10,1... | collective-permute-start | bytes 393224 | tf_op jit(solution)/shard_map/ppermute | solution.py:353
  230.2 12.8 %collective-permute-start.44 = (bf16[64,1024]{1,0:T(8,128)(2,1)S(1)}, bf16[64,1024]{1,0:T(8,128)(2,1)S(1)}, u32[]{:S(2)}, u32[]{:S(2)}) collective-permute-start(bf16[64,1024]{1,0:T(8,128)(2,1)S(1)} %shard_map.156.refs_0_), channel_id=1, source_target_pairs={{0,2},{1,3},{2,0},{3,1},{4,6},{5,7},{6,4},{7,5},{8,10},{9,11},{10,... | collective-permute-start | bytes 393224 | tf_op jit(solution)/shard_map/ppermute | solution.py:346
  231.0 15.5 %collective-permute-start.43 = (bf16[64,1024]{1,0:T(8,128)(2,1)S(1)}, bf16[64,1024]{1,0:T(8,128)(2,1)S(1)}, u32[]{:S(2)}, u32[]{:S(2)}) collective-permute-start(bf16[64,1024]{1,0:T(8,128)(2,1)S(1)} %shard_map.156.refs_0_), channel_id=1, source_target_pairs={{0,1},{1,2},{2,3},{3,0},{4,5},{5,6},{6,7},{7,4},{8,9},{9,10},{10,1... | collective-permute-start | bytes 393224 | tf_op jit(solution)/shard_map/ppermute | solution.py:346
  232.9 56.7 %collective-permute-start.52 = (bf16[256,1792]{1,0:T(8,128)(2,1)S(1)}, bf16[256,1792]{1,0:T(8,128)(2,1)S(1)}, u32[]{:S(2)}, u32[]{:S(2)}) collective-permute-start(bf16[256,1792]{1,0:T(8,128)(2,1)S(1)} %copy-done.7), channel_id=1, source_target_pairs={{16,0},{24,8},{17,1},{25,9},{18,2},{26,10},{19,3},{27,11},{20,4},{... | collective-permute-start | bytes 2752520 | tf_op jit(solution)/shard_map/ppermute | solution.py:482
  234.2 55.4 %collective-permute-start.53 = (bf16[256,1792]{1,0:T(8,128)(2,1)S(1)}, bf16[256,1792]{1,0:T(8,128)(2,1)S(1)}, u32[]{:S(2)}, u32[]{:S(2)}) collective-permute-start(bf16[256,1792]{1,0:T(8,128)(2,1)S(1)} %copy-done.16), channel_id=1, source_target_pairs={{16,0},{24,8},{17,1},{25,9},{18,2},{26,10},{19,3},{27,11},{20,4},{... | collective-permute-start | bytes 2752520 | tf_op jit(solution)/shard_map/ppermute | solution.py:482
  236.0 53.7 %collective-permute-start.54 = (bf16[256,1792]{1,0:T(8,128)(2,1)S(1)}, bf16[256,1792]{1,0:T(8,128)(2,1)S(1)}, u32[]{:S(2)}, u32[]{:S(2)}) collective-permute-start(bf16[256,1792]{1,0:T(8,128)(2,1)S(1)} %copy-done.18), channel_id=1, source_target_pairs={{0,16},{8,24},{1,17},{9,25},{2,18},{10,26},{3,19},{11,27},{4,20},{... | collective-permute-start | bytes 2752520 | tf_op jit(solution)/shard_map/ppermute | solution.py:482
  243.0 46.7 %collective-permute-start.55 = (bf16[256,1792]{1,0:T(8,128)(2,1)S(1)}, bf16[256,1792]{1,0:T(8,128)(2,1)S(1)}, u32[]{:S(2)}, u32[]{:S(2)}) collective-permute-start(bf16[256,1792]{1,0:T(8,128)(2,1)S(1)} %get-tuple-element.134.refs_5_.refs_1_), channel_id=1, source_target_pairs={{0,16},{8,24},{1,17},{9,25},{2,18},{10,26},{3,19},{11,27},{4,20},{... | collective-permute-start | bytes 2752520 | tf_op jit(solution)/shard_map/ppermute | solution.py:482
  288.3 21.5 %collective-permute-start.63 = (bf16[256,1536]{1,0:T(8,128)(2,1)S(1)}, bf16[256,1536]{1,0:T(8,128)(2,1)S(1)}, u32[]{:S(2)}, u32[]{:S(2)}) collective-permute-start(bf16[256,1536]{1,0:T(8,128)(2,1)S(1)} %get-tuple-element.142.refs_1_), channel_id=1, source_target_pairs={{0,16},{8,24},{1,17},{9,25},{2,18},{10,26},{3,19},{11,27},{4,20},{... | collective-permute-start | bytes 2359304 | tf_op jit(solution)/shard_map/ppermute | solution.py:482
  294.0 23.1 %collective-permute-start.62 = (bf16[256,1536]{1,0:T(8,128)(2,1)S(1)}, bf16[256,1536]{1,0:T(8,128)(2,1)S(1)}, u32[]{:S(2)}, u32[]{:S(2)}) collective-permute-start(bf16[256,1536]{1,0:T(8,128)(2,1)S(1)} %get-tuple-element.141.refs_0_), channel_id=1, source_target_pairs={{16,0},{24,8},{17,1},{25,9},{18,2},{26,10},{19,3},{27,11},{20,4},{... | collective-permute-start | bytes 2359304 | tf_op jit(solution)/shard_map/ppermute | solution.py:482
  305.3 11.8 %collective-permute-start.61 = (bf16[64,1024]{1,0:T(8,128)(2,1)S(1)}, bf16[64,1024]{1,0:T(8,128)(2,1)S(1)}, u32[]{:S(2)}, u32[]{:S(2)}) collective-permute-start(bf16[64,1024]{1,0:T(8,128)(2,1)S(1)} %shard_map.162.refs_0_), channel_id=1, source_target_pairs={{0,3},{1,0},{2,1},{3,2},{4,7},{5,4},{6,5},{7,6},{8,11},{9,8},{10,9... | collective-permute-start | bytes 393224 | tf_op jit(solution)/shard_map/ppermute | solution.py:346
  309.8 37.6 %collective-permute-start.65 = (bf16[256,1536]{1,0:T(8,128)(2,1)S(1)}, bf16[256,1536]{1,0:T(8,128)(2,1)S(1)}, u32[]{:S(2)}, u32[]{:S(2)}) collective-permute-start(bf16[256,1536]{1,0:T(8,128)(2,1)S(1)} %get-tuple-element.146.refs_1_), channel_id=1, source_target_pairs={{0,16},{8,24},{1,17},{9,25},{2,18},{10,26},{3,19},{11,27},{4,20},{... | collective-permute-start | bytes 2359304 | tf_op jit(solution)/shard_map/ppermute | solution.py:482
  319.8 27.6 %collective-permute-start.64 = (bf16[256,1536]{1,0:T(8,128)(2,1)S(1)}, bf16[256,1536]{1,0:T(8,128)(2,1)S(1)}, u32[]{:S(2)}, u32[]{:S(2)}) collective-permute-start(bf16[256,1536]{1,0:T(8,128)(2,1)S(1)} %shard_map.165.refs_0_), channel_id=1, source_target_pairs={{16,0},{24,8},{17,1},{25,9},{18,2},{26,10},{19,3},{27,11},{20,4},{... | collective-permute-start | bytes 2359304 | tf_op jit(solution)/shard_map/ppermute | solution.py:482
  321.1 16.6 %collective-permute-start.74 = (bf16[256,1024]{1,0:T(8,128)(2,1)S(1)}, bf16[256,1024]{1,0:T(8,128)(2,1)S(1)}, u32[]{:S(2)}, u32[]{:S(2)}) collective-permute-start(bf16[256,1024]{1,0:T(8,128)(2,1)S(1)} %shard_map.153.grad_ref.refs_5_), channel_id=1, source_target_pairs={{0,16},{8,24},{1,17},{9,25},{2,18},{10,26},{3,19},{11,27},{4,20},{... | collective-permute-start | bytes 1572872 | tf_op jit(solution)/shard_map/ppermute | solution.py:482
  327.0 18.9 %collective-permute-start.73 = (bf16[256,1024]{1,0:T(8,128)(2,1)S(1)}, bf16[256,1024]{1,0:T(8,128)(2,1)S(1)}, u32[]{:S(2)}, u32[]{:S(2)}) collective-permute-start(bf16[256,1024]{1,0:T(8,128)(2,1)S(1)} %shard_map.160.grad_ref.refs_4_), channel_id=1, source_target_pairs={{16,0},{24,8},{17,1},{25,9},{18,2},{26,10},{19,3},{27,11},{20,4},{... | collective-permute-start | bytes 1572872 | tf_op jit(solution)/shard_map/ppermute | solution.py:482
  346.0 40.9 %collective-permute-start.67 = (bf16[2,1,2,352,1024]{4,3,2,1,0:T(8,128)(2,1)S(1)}, bf16[2,1,2,352,1024]{4,3,2,1,0:T(8,128)(2,1)S(1)}, u32[]{:S(2)}, u32[]{:S(2)}) collective-permute-start(bf16[2,1,2,352,1024]{4,3,2,1,0:T(8,128)(2,1)S(1)} %bitcast.58), channel_id=1, source_target_pairs={{0,8},{16,24},{1,9},{17,25},{2,10},{18,26},{3,11},{19,27},{4,12},{... | collective-permute-start | bytes 8650760 | tf_op jit(solution)/shard_map/ppermute | solution.py:395
  349.2 42.7 %collective-permute-start.66 = (bf16[2,1,2,352,1024]{4,3,2,1,0:T(8,128)(2,1)S(1)}, bf16[2,1,2,352,1024]{4,3,2,1,0:T(8,128)(2,1)S(1)}, u32[]{:S(2)}, u32[]{:S(2)}) collective-permute-start(bf16[2,1,2,352,1024]{4,3,2,1,0:T(8,128)(2,1)S(1)} %bitcast.60), channel_id=1, source_target_pairs={{8,0},{24,16},{9,1},{25,17},{10,2},{26,18},{11,3},{27,19},{12,4},{... | collective-permute-start | bytes 8650760 | tf_op jit(solution)/shard_map/ppermute | solution.py:395
  351.4 22.0 %collective-permute-start.75 = (bf16[2,1,1,352,1024]{4,3,2,1,0:T(8,128)(2,1)S(1)}, bf16[2,1,1,352,1024]{4,3,2,1,0:T(8,128)(2,1)S(1)}, u32[]{:S(2)}, u32[]{:S(2)}) collective-permute-start(bf16[2,1,1,352,1024]{4,3,2,1,0:T(8,128)(2,1)S(1)} %bitcast.69), channel_id=1, source_target_pairs={{0,8},{16,24},{1,9},{17,25},{2,10},{18,26},{3,11},{19,27},{4,12},{... | collective-permute-start | bytes 4325384 | tf_op jit(solution)/shard_map/ppermute | solution.py:395
  354.9 12.2 %collective-permute-start.71 = (bf16[256,1024]{1,0:T(8,128)(2,1)S(1)}, bf16[256,1024]{1,0:T(8,128)(2,1)S(1)}, u32[]{:S(2)}, u32[]{:S(2)}) collective-permute-start(bf16[256,1024]{1,0:T(8,128)(2,1)S(1)} %shard_map.157.grad_ref.refs_5_), channel_id=1, source_target_pairs={{0,16},{8,24},{1,17},{9,25},{2,18},{10,26},{3,19},{11,27},{4,20},{... | collective-permute-start | bytes 1572872 | tf_op jit(solution)/shard_map/ppermute | solution.py:482
  356.4 14.9 %collective-permute-start.70 = (bf16[256,1024]{1,0:T(8,128)(2,1)S(1)}, bf16[256,1024]{1,0:T(8,128)(2,1)S(1)}, u32[]{:S(2)}, u32[]{:S(2)}) collective-permute-start(bf16[256,1024]{1,0:T(8,128)(2,1)S(1)} %shard_map.163.grad_ref.refs_4_), channel_id=1, source_target_pairs={{16,0},{24,8},{17,1},{25,9},{18,2},{26,10},{19,3},{27,11},{20,4},{... | collective-permute-start | bytes 1572872 | tf_op jit(solution)/shard_map/ppermute | solution.py:482
  376.7 21.0 %collective-permute-start.77 = (bf16[1,704,1024]{2,1,0:T(8,128)(2,1)S(1)}, bf16[1,704,1024]{2,1,0:T(8,128)(2,1)S(1)}, u32[]{:S(2)}, u32[]{:S(2)}) collective-permute-start(bf16[1,704,1024]{2,1,0:T(8,128)(2,1)S(1)} %shard_map.172.refs_1_), channel_id=1, source_target_pairs={{8,12},{12,8},{24,28},{28,24},{9,13},{13,9},{25,29},{29,25},{10,14... | collective-permute-start | bytes 4325384 | tf_op jit(solution)/shard_map/ppermute | solution.py:535
  379.3 40.3 %collective-permute-start.76 = (bf16[1,704,1024]{2,1,0:T(8,128)(2,1)}, bf16[1,704,1024]{2,1,0:T(8,128)(2,1)}, u32[]{:S(2)}, u32[]{:S(2)}) collective-permute-start(bf16[1,704,1024]{2,1,0:T(8,128)(2,1)} %shard_map.170.refs_0_), channel_id=1, source_target_pairs={{0,4},{4,0},{16,20},{20,16},{1,5},{5,1},{17,21},{21,17},{2,6},{6,2... | collective-permute-start | bytes 4325384 | tf_op jit(solution)/shard_map/ppermute | solution.py:535
  389.9 37.9 %collective-permute-start.79 = (bf16[1,704,1024]{2,1,0:T(8,128)(2,1)}, bf16[1,704,1024]{2,1,0:T(8,128)(2,1)}, u32[]{:S(2)}, u32[]{:S(2)}) collective-permute-start(bf16[1,704,1024]{2,1,0:T(8,128)(2,1)} %get-tuple-element.159.refs_1_), channel_id=1, source_target_pairs={{8,12},{12,8},{24,28},{28,24},{9,13},{13,9},{25,29},{29,25},{10,14... | collective-permute-start | bytes 4325384 | tf_op jit(solution)/shard_map/ppermute | solution.py:535
  395.0 55.5 %collective-permute-start.78 = (bf16[1,704,1024]{2,1,0:T(8,128)(2,1)}, bf16[1,704,1024]{2,1,0:T(8,128)(2,1)}, u32[]{:S(2)}, u32[]{:S(2)}) collective-permute-start(bf16[1,704,1024]{2,1,0:T(8,128)(2,1)} %get-tuple-element.158.refs_0_), channel_id=1, source_target_pairs={{0,4},{4,0},{16,20},{20,16},{1,5},{5,1},{17,21},{21,17},{2,6},{6,2... | collective-permute-start | bytes 4325384 | tf_op jit(solution)/shard_map/ppermute | solution.py:535
  396.9 61.8 %collective-permute-start.69 = (bf16[1,704,1024]{2,1,0:T(8,128)(2,1)}, bf16[1,704,1024]{2,1,0:T(8,128)(2,1)S(1)}, u32[]{:S(2)}, u32[]{:S(2)}) collective-permute-start(bf16[1,704,1024]{2,1,0:T(8,128)(2,1)} %get-tuple-element.150.refs_1_), channel_id=1, source_target_pairs={{8,12},{12,8},{24,28},{28,24},{9,13},{13,9},{25,29},{29,25},{10,14... | collective-permute-start | bytes 4325384 | tf_op jit(solution)/shard_map/ppermute | solution.py:535
  398.8 80.2 %collective-permute-start.68 = (bf16[1,704,1024]{2,1,0:T(8,128)(2,1)}, bf16[1,704,1024]{2,1,0:T(8,128)(2,1)S(1)}, u32[]{:S(2)}, u32[]{:S(2)}) collective-permute-start(bf16[1,704,1024]{2,1,0:T(8,128)(2,1)} %get-tuple-element.149.refs_0_), channel_id=1, source_target_pairs={{0,4},{4,0},{16,20},{20,16},{1,5},{5,1},{17,21},{21,17},{2,6},{6,2... | collective-permute-start | bytes 4325384 | tf_op jit(solution)/shard_map/ppermute | solution.py:535
  (100 other events, 1273.6 us)

commit v3 on v2

--- a/solution.py
+++ b/solution.py
@@ -211,8 +211,9 @@
 
 
 def wgrad_body(sources, stages, base, stage_ref, *refs):
-    out = refs[-1]
-    blocks, kinds, ff, width = out.shape
+    outs = refs[2 * sources * stages :]
+    blocks, _, ff, width = outs[0].shape
+    kinds = len(outs)
     stage = stage_ref[0]
 
     def value(side, source, at):
@@ -230,18 +231,18 @@
                 left = value(0, source, span(base, ff, kinds * b + kind))
                 term = dot(left, rights[source], TN)
                 total = term if total is None else total + term
-            out[b, kind] = total.astype(BF16)
-
-
-def wgrad(stage, shape, base, lefts, rights):
+            outs[kind][b, 0] = total.astype(BF16)
+
+
+def wgrad(stage, shape, kinds, base, lefts, rights):
     sources, stages = len(lefts), len(lefts[0])
     args = [v for side in (lefts, rights) for source in side for v in source]
-    flops = 2 * sources * args[0].shape[0] * math.prod(shape)
+    flops = 2 * sources * args[0].shape[0] * math.prod(shape) * kinds
     return pl.pallas_call(
         functools.partial(wgrad_body, sources, stages, base),
-        out_shape=sds(shape),
+        out_shape=[sds(shape)] * kinds,
         in_specs=[pl.BlockSpec(memory_space=pltpu.SMEM)] + [VMEM] * len(args),
-        out_specs=VMEM,
+        out_specs=[VMEM] * kinds,
         compiler_params=pltpu.CompilerParams(vmem_limit_bytes=32 << 20),
         cost_estimate=pl.CostEstimate(flops=flops, bytes_accessed=flops // 512, transcendentals=0),
     )(stage.astype(jnp.int32).reshape(1), *args)
@@ -251,32 +252,30 @@
     return max(r for r in range(16, most + 1, 16) if size % r == 0)
 
 
-def settle_body(flip, blocks, w_ref, own, *refs):
-    other, outs = (refs[0], refs[1:]) if blocks == 2 else (None, refs)
-    kinds, depth = len(outs), outs[0].shape[0]
+def settle_body(flip, blocks, kind, w_ref, own, *refs):
+    other, out = (refs[0], refs[1]) if blocks == 2 else (None, refs[0])
     size = own.shape[-2]
     step = tile_rows(size, 48)
-    for d in range(depth):
-        for kind in range(kinds):
-            for b in range(blocks):
-                h = blocks - 1 - b if flip else b
-
-                @pl.loop(0, size // step)
-                def _(i):
-                    at = pl.ds(pl.multiple_of(i * step, 16), step)
-                    to = pl.ds(pl.multiple_of(h * size + i * step, 16), step)
-                    g = own[b, d, kind, at, :].astype(F32)
-                    if other is not None:
-                        g = g + other[blocks - 1 - b, d, kind, at, :].astype(F32)
-                    w = w_ref[d, kind, to, :].astype(F32)
-                    outs[kind][d, to, :] = (w - INNER_LR * g).astype(BF16)
-
-
-def settle(w, own, others, flip):
-    depth, kinds, size, width = w.shape
-    body = functools.partial(settle_body, flip, own.shape[0])
-    outs = [sds((depth, size, width))] * kinds
-    return call(body, outs, [w, own, *others], 4 * w.size, 40 << 20)
+    for d in range(out.shape[0]):
+        for b in range(blocks):
+            h = blocks - 1 - b if flip else b
+
+            @pl.loop(0, size // step)
+            def _(i):
+                at = pl.ds(pl.multiple_of(i * step, 16), step)
+                to = pl.ds(pl.multiple_of(h * size + i * step, 16), step)
+                g = own[b, d, 0, at, :].astype(F32)
+                if other is not None:
+                    g = g + other[blocks - 1 - b, d, 0, at, :].astype(F32)
+                w = w_ref[d, kind, to, :].astype(F32)
+                out[d, to, :] = (w - INNER_LR * g).astype(BF16)
+
+
+def settle(w, kind, own, others, flip):
+    depth, _, size, width = w.shape
+    body = functools.partial(settle_body, flip, own.shape[0], kind)
+    outs = [sds((depth, size, width))]
+    return call(body, outs, [w, own, *others], 4 * depth * size * width, 16 << 20)[0]
 
 
 def update_body(replicas, group, info, *refs):
@@ -327,7 +326,7 @@
             out_specs=[whole] * 3,
         ),
         input_output_aliases={first + i: i for i in range(len(done))},
-        compiler_params=pltpu.CompilerParams(vmem_limit_bytes=60 << 20),
+        compiler_params=pltpu.CompilerParams(vmem_limit_bytes=67000000),
         cost_estimate=pl.CostEstimate(
             flops=10 * outer.size // kinds,
             bytes_accessed=22 * outer.size // kinds,
@@ -408,8 +407,10 @@
         mine = [cut(w, core) for w in own]
         theirs = [cut(w, 1 - core) for w in own]
         away = [swap(w) for w in theirs]
+        pair_first = jnp.where(even, mine[0], away[0])
+        mine, away = after((mine, away), pair_first)
         homes = [
-            [jnp.where(even, m, a) for m, a in zip(mine, away)],
+            [pair_first, jnp.where(even, mine[1], away[1])],
             [jnp.where(even, a, m) for m, a in zip(mine, away)],
         ]
     else:
@@ -435,7 +436,7 @@
     ids = lax.dynamic_slice_in_dim(jnp.concatenate([ids, ids], axis=1), core, group, 1)
     ids = jnp.swapaxes(ids, 0, 1).reshape(-1)
     vocab_part = embed.shape[0]
-    local_ids = after(ids, *theirs) - section * vocab_part
+    local_ids = after(ids, *theirs, homes[0][0]) - section * vocab_part
     inside = (local_ids >= 0) & (local_ids < vocab_part)
     looked = jnp.take(embed, jnp.clip(local_ids, 0, vocab_part - 1), axis=0)
     looked = jnp.where(inside[:, None], looked, jnp.zeros((), BF16))
@@ -492,14 +493,16 @@
             of = [acts[(s * group + g) * depth + d] for s in range(stages)]
             kinds = [[[a[kind][j] for a in of] for j in range(stages)] for kind in range(3 if pair else 2)]
             kinds[-1][1:] = [[after(v, ready) for v in one] for one in kinds[-1][1:]]
+            shape = (group, 1, block, width)
             if pair:
-                shape = (group, 2, block, width)
-                sets.append(wgrad(stage, shape, 0, kinds[2], kinds[0]))
+                sets.append(wgrad(stage, shape, 2, 0, kinds[2], kinds[0]))
             else:
-                shape = (group, 1, block, width)
-                sets.append(wgrad(stage, shape, width, kinds[0], kinds[1]))
-        own = jnp.stack(sets, axis=1)
-        return own, [to_member(own, g)] if group == 2 else []
+                sets.append(wgrad(stage, shape, 1, width, kinds[0], kinds[1]))
+        out = []
+        for parts in zip(*sets):
+            own = jnp.stack(parts, axis=1)
+            out.append((own, [to_member(own, g)] if group == 2 else []))
+        return out
 
     sums = {}
     for l in reversed(range(count)):
@@ -512,7 +515,7 @@
         acts[l].append(to_home(whole, s))
         if (l + 1) % depth == 0 and 0 < g < group:
             sums[g, True] = grads_of(g, True, grad)
-            gates = after(gates, sums[g, True][0])
+            gates = after(gates, sums[g, True][0][0])
         late, parts = bwd_layer(whole, gates, *layers[l], len(chunks), l == 0)
         acts[l].append(to_home(late, s))
         if l < group * depth and l % depth == 0:
@@ -537,12 +540,11 @@
     inners, others = [[], [], []], [[], [], []]
     sums[0, True] = grads_of(0, True, acts[0][2][0])
     for g in reversed(range(group)):
-        for i in (1, 0):
-            own, away = sums[g, i == 0]
-            settled = settle(starts[i], own, away, g > 0)
-            for j, inner in enumerate(settled, 2 * i):
-                inners[j].insert(0, inner)
-                others[j].insert(0, exchange(inner, g))
+        for j in (2, 0, 1):
+            own, away = sums[g, j < 2][j % 2]
+            inner = settle(starts[j // 2], j % 2, own, away, g > 0)
+            inners[j].insert(0, inner)
+            others[j].insert(0, exchange(inner, g))
 
     info = jnp.stack([core, lax.dynamic_index_in_dim(fragment, section, 0, keepdims=False)])
 

time: 491 us -> 472 us (0.961)
  local copies, waits for them, and re-layouts: 31.9 us -> 22.6 us
  starting transfers between devices: 111 us -> 106 us
    ppermute x24, waiting for transfers between devices: 65.4 us -> 81.7 us  [spread(): lax.ppermute(value, 'tp', [(i, (i + k) % tp) for i in range(tp)])]
    unnamed x136 -> x98, local copies, waits for them, and re-layouts: 18.9 us -> 9.65 us
    ppermute x5, waiting for transfers between devices: 38.3 us -> 30.5 us  [shift(): return lax.ppermute(value, 'section', pairs)]
    ppermute x12, waiting for transfers between devices: 31.2 us -> 23.9 us  [to_home(): out.append(lax.ppermute(value, 'section', pairs))]
    ppermute x12, starting transfers between devices: 31.5 us -> 24.6 us  [to_home(): out.append(lax.ppermute(value, 'section', pairs))]
    ppermute x4 -> x6, starting transfers between devices: 7.49 us -> 11.8 us  [to_member(): return lax.ppermute(value, 'section', pairs)]
    pallas_call x24 -> x26, Pallas kernels: 34 us -> 34.4 us  [call(): pl.pallas_call(body, out_shape=outs, in_specs=[VMEM] * len(args), out_spe...]
  transfers between devices with their start and end apart: 80 -> 82, of which waited for: 41 -> 44; matrix products, arithmetic and copies ran while one was open for 5% -> 5% of each run, Pallas kernels for 10% -> 10%
where the time goes in v3:
time: 472 us; the launch traced here: 471 us
  waiting for transfers between devices  261 us (55%)
  starting transfers between devices  106 us (22%)
  Pallas kernels  64.1 us (14%)
  local copies, waits for them, and re-layouts  22.6 us (5%)
  other arithmetic  15.4 us (3%)
    ppermute x24, waiting for transfers between devices, spread(): lax.ppermute(value, 'tp', [(i, (i + k) % tp) for i in range(tp)])  81.7 us
    ppermute x18, waiting for transfers between devices, collect(): lax.ppermute(parts[k], 'tp', [(i, (i - k) % tp) for i in range(tp)])  66.5 us
    ppermute x6, waiting for transfers between devices, exchange(): return lax.ppermute(inner, ('section', 'rep'), ring)  56 us
    pallas_call x26, Pallas kernels, call(): pl.pallas_call(body, out_shape=outs, in_specs=[VMEM] * len(args), out_spe...  34.4 us
    ppermute x5, waiting for transfers between devices, shift(): return lax.ppermute(value, 'section', pairs)  30.5 us
    ppermute x12, starting transfers between devices, to_home(): out.append(lax.ppermute(value, 'section', pairs))  24.6 us
    pallas_call x3, Pallas kernels, update(): pl.pallas_call(functools.partial(update_body, replicas, group), out_shape...  24.5 us
    ppermute x12, waiting for transfers between devices, to_home(): out.append(lax.ppermute(value, 'section', pairs))  23.9 us
  transfers between devices with their start and end apart: 82, of which 44 were waited for; matrix products, arithmetic and copies ran while one was open for 5% of the time, Pallas kernels for 10%

profile of v3, /device:TPU:0, one launch (start us, length us, event | category | flops | bytes accessed | tf_op | source)
XLA Modules:
  0.0 470.7 jit_solution(12802013849857154489)
XLA Ops:
  9.3 2.9 collective-permute-start.6
  12.2 6.0 %gather_fusion = bf16[256,1024]{1,0:T(8,128)(2,1)S(1)} fusion(bf16[4096,1024]{1,0:T(8,128)(2,1)} %param.11, s32[1024]{0:T(1024)S(1)} %pad_clamp_fusion), kind=kCustom, calls=%fused_computation | custom fusion | bytes 1049600 | tf_op jit(solution)/shard_map/jit(_take)/gather | solution.py:441
  26.0 20.8 %collective-permute-done.2.refs_1_ = bf16[64,1024]{1,0:T(8,128)(2,1)S(1)} collective-permute-done((bf16[64,1024]{1,0:T(8,128)(2,1)S(1)}, bf16[64,1024]{1,0:T(8,128)(2,1)S(1)}, u32[]{:S(2)}, u32[]{:S(2)}) %collective-permute-start.2) | collective-permute-done | bytes 131104 | tf_op jit(solution)/shard_map/ppermute | solution.py:390
  50.4 3.8 collective-permute-start.5
  58.4 8.1 %collective-permute-done.4.refs_2_ = bf16[64,1024]{1,0:T(8,128)(2,1)S(1)} collective-permute-done((bf16[64,1024]{1,0:T(8,128)(2,1)S(1)}, bf16[64,1024]{1,0:T(8,128)(2,1)S(1)}, u32[]{:S(2)}, u32[]{:S(2)}) %collective-permute-start.4) | collective-permute-done | bytes 131104 | tf_op jit(solution)/shard_map/ppermute | solution.py:345
  76.1 8.9 %collective-permute-done.12.refs_3_ = bf16[64,1024]{1,0:T(8,128)(2,1)S(1)} collective-permute-done((bf16[64,1024]{1,0:T(8,128)(2,1)S(1)}, bf16[64,1024]{1,0:T(8,128)(2,1)S(1)}, u32[]{:S(2)}, u32[]{:S(2)}) %collective-permute-start.12) | collective-permute-done | bytes 131104 | tf_op jit(solution)/shard_map/ppermute | solution.py:352
  93.1 6.7 %collective-permute-done.15.refs_2_ = bf16[64,1024]{1,0:T(8,128)(2,1)S(1)} collective-permute-done((bf16[64,1024]{1,0:T(8,128)(2,1)S(1)}, bf16[64,1024]{1,0:T(8,128)(2,1)S(1)}, u32[]{:S(2)}, u32[]{:S(2)}) %collective-permute-start.15) | collective-permute-done | bytes 131104 | tf_op jit(solution)/shard_map/ppermute | solution.py:345
  101.1 7.6 %collective-permute-done.19 = bf16[1,352,1024]{2,1,0:T(8,128)(2,1)S(1)} collective-permute-done((bf16[1,352,1024]{2,1,0:T(8,128)(2,1)S(1)}, bf16[1,352,1024]{2,1,0:T(8,128)(2,1)S(1)}, u32[]{:S(2)}, u32[]{:S(2)}) %collective-permute-start.19) | collective-permute-done | bytes 720928 | tf_op jit(solution)/shard_map/ppermute | solution.py:390
  112.5 4.2 shard_map.149
  117.9 4.1 collective-permute-start.21
  123.0 3.0 collective-permute-done.21.refs_2_
  126.0 8.0 %collective-permute-done.22.refs_3_ = bf16[64,1024]{1,0:T(8,128)(2,1)S(1)} collective-permute-done((bf16[64,1024]{1,0:T(8,128)(2,1)S(1)}, bf16[64,1024]{1,0:T(8,128)(2,1)S(1)}, u32[]{:S(2)}, u32[]{:S(2)}) %collective-permute-start.22) | collective-permute-done | bytes 131104 | tf_op jit(solution)/shard_map/ppermute | solution.py:352
  140.0 8.0 %collective-permute-done.25.refs_2_ = bf16[64,1024]{1,0:T(8,128)(2,1)S(1)} collective-permute-done((bf16[64,1024]{1,0:T(8,128)(2,1)S(1)}, bf16[64,1024]{1,0:T(8,128)(2,1)S(1)}, u32[]{:S(2)}, u32[]{:S(2)}) %collective-permute-start.25) | collective-permute-done | bytes 131104 | tf_op jit(solution)/shard_map/ppermute | solution.py:345
  157.8 3.0 collective-permute-done.29.refs_2_
  160.8 7.2 %collective-permute-done.30.refs_3_ = bf16[64,1024]{1,0:T(8,128)(2,1)S(1)} collective-permute-done((bf16[64,1024]{1,0:T(8,128)(2,1)S(1)}, bf16[64,1024]{1,0:T(8,128)(2,1)S(1)}, u32[]{:S(2)}, u32[]{:S(2)}) %collective-permute-start.30) | collective-permute-done | bytes 131104 | tf_op jit(solution)/shard_map/ppermute | solution.py:352
  173.6 8.4 %collective-permute-done.36.refs_2_ = bf16[64,1024]{1,0:T(8,128)(2,1)S(1)} collective-permute-done((bf16[64,1024]{1,0:T(8,128)(2,1)S(1)}, bf16[64,1024]{1,0:T(8,128)(2,1)S(1)}, u32[]{:S(2)}, u32[]{:S(2)}) %collective-permute-start.36) | collective-permute-done | bytes 131104 | tf_op jit(solution)/shard_map/ppermute | solution.py:345
  187.4 5.0 %collective-permute-done.34.refs_3_ = bf16[64,1024]{1,0:T(8,128)(2,1)S(1)} collective-permute-done((bf16[64,1024]{1,0:T(8,128)(2,1)S(1)}, bf16[64,1024]{1,0:T(8,128)(2,1)S(1)}, u32[]{:S(2)}, u32[]{:S(2)}) %collective-permute-start.34) | collective-permute-done | bytes 131104 | tf_op jit(solution)/shard_map/ppermute | solution.py:345
  192.4 5.6 %collective-permute-done.33.refs_2_ = bf16[64,1024]{1,0:T(8,128)(2,1)S(1)} collective-permute-done((bf16[64,1024]{1,0:T(8,128)(2,1)S(1)}, bf16[64,1024]{1,0:T(8,128)(2,1)S(1)}, u32[]{:S(2)}, u32[]{:S(2)}) %collective-permute-start.33) | collective-permute-done | bytes 131104 | tf_op jit(solution)/shard_map/ppermute | solution.py:345
  199.9 3.2 shard_map.154
  203.1 4.5 shard_map.155
  213.0 9.6 %collective-permute-done.41.refs_4_ = bf16[64,1024]{1,0:T(8,128)(2,1)S(1)} collective-permute-done((bf16[64,1024]{1,0:T(8,128)(2,1)S(1)}, bf16[64,1024]{1,0:T(8,128)(2,1)S(1)}, u32[]{:S(2)}, u32[]{:S(2)}) %collective-permute-start.41) | collective-permute-done | bytes 131104 | tf_op jit(solution)/shard_map/ppermute | solution.py:352
  228.5 4.3 collective-permute-start.54
  232.8 2.7 collective-permute-done.44.refs_2_
  235.6 3.5 collective-permute-start.55
  241.4 5.0 %collective-permute-done.46.refs_3_ = bf16[64,1024]{1,0:T(8,128)(2,1)S(1)} collective-permute-done((bf16[64,1024]{1,0:T(8,128)(2,1)S(1)}, bf16[64,1024]{1,0:T(8,128)(2,1)S(1)}, u32[]{:S(2)}, u32[]{:S(2)}) %collective-permute-start.46) | collective-permute-done | bytes 131104 | tf_op jit(solution)/shard_map/ppermute | solution.py:352
  246.3 6.6 %collective-permute-done.47.refs_4_ = bf16[64,1024]{1,0:T(8,128)(2,1)S(1)} collective-permute-done((bf16[64,1024]{1,0:T(8,128)(2,1)S(1)}, bf16[64,1024]{1,0:T(8,128)(2,1)S(1)}, u32[]{:S(2)}, u32[]{:S(2)}) %collective-permute-start.47) | collective-permute-done | bytes 131104 | tf_op jit(solution)/shard_map/ppermute | solution.py:352
  252.9 7.3 %collective-permute-done.48.refs_5_ = bf16[64,1024]{1,0:T(8,128)(2,1)S(1)} collective-permute-done((bf16[64,1024]{1,0:T(8,128)(2,1)S(1)}, bf16[64,1024]{1,0:T(8,128)(2,1)S(1)}, u32[]{:S(2)}, u32[]{:S(2)}) %collective-permute-start.48) | collective-permute-done | bytes 131104 | tf_op jit(solution)/shard_map/ppermute | solution.py:352
  260.8 4.6 collective-permute-done.51.refs_3_
  265.4 8.7 %collective-permute-done.50.refs_2_ = bf16[64,1024]{1,0:T(8,128)(2,1)S(1)} collective-permute-done((bf16[64,1024]{1,0:T(8,128)(2,1)S(1)}, bf16[64,1024]{1,0:T(8,128)(2,1)S(1)}, u32[]{:S(2)}, u32[]{:S(2)}) %collective-permute-start.50) | collective-permute-done | bytes 131104 | tf_op jit(solution)/shard_map/ppermute | solution.py:345
  274.1 6.9 %collective-permute-done.49.refs_1_ = bf16[64,1024]{1,0:T(8,128)(2,1)S(1)} collective-permute-done((bf16[64,1024]{1,0:T(8,128)(2,1)S(1)}, bf16[64,1024]{1,0:T(8,128)(2,1)S(1)}, u32[]{:S(2)}, u32[]{:S(2)}) %collective-permute-start.49) | collective-permute-done | bytes 131104 | tf_op jit(solution)/shard_map/ppermute | solution.py:345
  281.1 4.3 shard_map.161
  290.5 2.7 collective-permute-done.56.refs_3_
  298.0 6.3 %collective-permute-done.61.refs_3_ = bf16[64,1024]{1,0:T(8,128)(2,1)S(1)} collective-permute-done((bf16[64,1024]{1,0:T(8,128)(2,1)S(1)}, bf16[64,1024]{1,0:T(8,128)(2,1)S(1)}, u32[]{:S(2)}, u32[]{:S(2)}) %collective-permute-start.61) | collective-permute-done | bytes 131104 | tf_op jit(solution)/shard_map/ppermute | solution.py:345
  306.0 6.5 %collective-permute-done.59.refs_1_ = bf16[64,1024]{1,0:T(8,128)(2,1)S(1)} collective-permute-done((bf16[64,1024]{1,0:T(8,128)(2,1)S(1)}, bf16[64,1024]{1,0:T(8,128)(2,1)S(1)}, u32[]{:S(2)}, u32[]{:S(2)}) %collective-permute-start.59) | collective-permute-done | bytes 131104 | tf_op jit(solution)/shard_map/ppermute | solution.py:345
  312.4 4.6 collective-permute-start.71
  318.4 5.4 %collective-permute-done.73.refs_6_ = bf16[256,1024]{1,0:T(8,128)(2,1)S(1)} collective-permute-done((bf16[256,1024]{1,0:T(8,128)(2,1)S(1)}, bf16[256,1024]{1,0:T(8,128)(2,1)S(1)}, u32[]{:S(2)}, u32[]{:S(2)}) %collective-permute-start.73) | collective-permute-done | bytes 524320 | tf_op jit(solution)/shard_map/ppermute | solution.py:483
  334.8 3.1 collective-permute-start.79
  337.9 13.1 %collective-permute-done.65.refs_3_ = bf16[256,1536]{1,0:T(8,128)(2,1)S(1)} collective-permute-done((bf16[256,1536]{1,0:T(8,128)(2,1)S(1)}, bf16[256,1536]{1,0:T(8,128)(2,1)S(1)}, u32[]{:S(2)}, u32[]{:S(2)}) %collective-permute-start.65) | collective-permute-done | bytes 786464 | tf_op jit(solution)/shard_map/ppermute | solution.py:483
  351.0 4.7 %collective-permute-done.64.refs_2_ = bf16[256,1536]{1,0:T(8,128)(2,1)S(1)} collective-permute-done((bf16[256,1536]{1,0:T(8,128)(2,1)S(1)}, bf16[256,1536]{1,0:T(8,128)(2,1)S(1)}, u32[]{:S(2)}, u32[]{:S(2)}) %collective-permute-start.64) | collective-permute-done | bytes 786464 | tf_op jit(solution)/shard_map/ppermute | solution.py:483
  358.7 3.2 collective-permute-start.67
  366.7 3.5 collective-permute-start.76
  384.8 3.5 collective-permute-start.68
  390.2 13.2 %collective-permute-done.76.refs_2_ = bf16[1,704,1024]{2,1,0:T(8,128)(2,1)} collective-permute-done((bf16[1,704,1024]{2,1,0:T(8,128)(2,1)}, bf16[1,704,1024]{2,1,0:T(8,128)(2,1)}, u32[]{:S(2)}, u32[]{:S(2)}) %collective-permute-start.76) | collective-permute-done | bytes 1441824 | tf_op jit(solution)/shard_map/ppermute | solution.py:538
  403.3 8.2 %shard_map.173 = (bf16[1,1,704,1024]{3,2,1,0:T(8,128)(2,1)}, f32[1,1,704,1024]{3,2,1,0:T(8,128)}, f32[1,1,704,1024]{3,2,1,0:T(8,128)}) custom-call(s32[2]{0:T(128)} %pad_add_fusion.info, bf16[1,704,1024]{2,1,0:T(8,128)(2,1)} %shard_map.170.refs_0_, bf16[1,704,1024]{2,1,0:T(8,128)(2,1)} %copy-done.12, bf16[1,704,1024]{2,1,0:T(8,128)(2,1)} %collective-permute-done.76.refs_2_, ...), custom_call_target="tpu_custom_call" | custom-call | flops 7208960 | bytes 15859712 | tf_op jit(solution)/shard_map/pallas_call | solution.py:319
  411.5 22.7 %collective-permute-done.80.refs_2_ = bf16[1,704,1024]{2,1,0:T(8,128)(2,1)} collective-permute-done((bf16[1,704,1024]{2,1,0:T(8,128)(2,1)}, bf16[1,704,1024]{2,1,0:T(8,128)(2,1)}, u32[]{:S(2)}, u32[]{:S(2)}) %collective-permute-start.80) | collective-permute-done | bytes 1441824 | tf_op jit(solution)/shard_map/ppermute | solution.py:538
  434.2 8.2 %shard_map.176 = (bf16[1,2,704,1024]{3,2,1,0:T(8,128)(2,1)}, f32[1,2,704,1024]{3,2,1,0:T(8,128)}, f32[1,2,704,1024]{3,2,1,0:T(8,128)}) custom-call(s32[2]{0:T(128)} %pad_add_fusion.info, bf16[1,704,1024]{2,1,0:T(8,128)(2,1)} %shard_map.174.refs_0_, bf16[1,704,1024]{2,1,0:T(8,128)(2,1)} %shard_map.175.refs_1_, ...), custom_call_target="tpu_custom_call" | custom-call | flops 7208960 | bytes 15859712 | tf_op jit(solution)/shard_map/pallas_call | solution.py:319
  442.4 20.1 %collective-permute-done.68.refs_2_ = bf16[1,704,1024]{2,1,0:T(8,128)(2,1)} collective-permute-done((bf16[1,704,1024]{2,1,0:T(8,128)(2,1)}, bf16[1,704,1024]{2,1,0:T(8,128)(2,1)}, u32[]{:S(2)}, u32[]{:S(2)}) %collective-permute-start.68) | collective-permute-done | bytes 1441824 | tf_op jit(solution)/shard_map/ppermute | solution.py:538
  462.5 8.2 %shard_map.177 = (bf16[1,2,704,1024]{3,2,1,0:T(8,128)(2,1)}, f32[1,2,704,1024]{3,2,1,0:T(8,128)}, f32[1,2,704,1024]{3,2,1,0:T(8,128)}) custom-call(s32[2]{0:T(128)} %pad_add_fusion.info, bf16[1,704,1024]{2,1,0:T(8,128)(2,1)} %shard_map.167.refs_0_, ...), custom_call_target="tpu_custom_call", output_to_operand_aliasing={{0}: (7, {}), {1}: (8, {}), {2}: (9, {})} | custom-call | flops 7208960 | bytes 15859712 | tf_op jit(solution)/shard_map/pallas_call | solution.py:319
  (275 shorter events, 139.4 us)
Async XLA Ops:
  6.4 14.0 %collective-permute-start.8 = (bf16[1,352,1024]{2,1,0:T(8,128)(2,1)}, bf16[1,352,1024]{2,1,0:T(8,128)(2,1)}, u32[]{:S(2)}, u32[]{:S(2)}) collective-permute-start(bf16[1,352,1024]{2,1,0:T(8,128)(2,1)} %get-tuple-element.183), channel_id=1, source_target_pairs={{0,8},{8,0},{16,24},{24,16},{1,9},{9,1},{17,25},{25,17},{2,10},{10... | collective-permute-start | bytes 2162696 | tf_op jit(solution)/shard_map/ppermute | solution.py:386
  9.3 37.7 %collective-permute-start.6 = (bf16[1,2,352,1024]{3,2,1,0:T(8,128)(2,1)}, bf16[1,2,352,1024]{3,2,1,0:T(8,128)(2,1)}, u32[]{:S(2)}, u32[]{:S(2)}) collective-permute-start(bf16[1,2,352,1024]{3,2,1,0:T(8,128)(2,1)} %get-tuple-element.94), channel_id=1, source_target_pairs={{0,16},{8,24},{16,0},{24,8},{1,17},{9,25},{17,1},{25,9},{2,18},{10... | collective-permute-start | bytes 4325384 | tf_op jit(solution)/shard_map/ppermute | solution.py:390
  22.6 24.2 %collective-permute-start.2 = (bf16[64,1024]{1,0:T(8,128)(2,1)S(1)}, bf16[64,1024]{1,0:T(8,128)(2,1)S(1)}, u32[]{:S(2)}, u32[]{:S(2)}) collective-permute-start(bf16[64,1024]{1,0:T(8,128)(2,1)S(1)} %get-tuple-element.184), channel_id=1, source_target_pairs={{0,16},{8,24},{16,0},{24,8},{1,17},{9,25},{17,1},{25,9},{2,18},{10... | collective-permute-start | bytes 393224 | tf_op jit(solution)/shard_map/ppermute | solution.py:390
  24.2 42.3 %collective-permute-start.9 = (bf16[1,352,1024]{2,1,0:T(8,128)(2,1)S(1)}, bf16[1,352,1024]{2,1,0:T(8,128)(2,1)S(1)}, u32[]{:S(2)}, u32[]{:S(2)}) collective-permute-start(bf16[1,352,1024]{2,1,0:T(8,128)(2,1)S(1)} %get-tuple-element.99), channel_id=1, source_target_pairs={{0,16},{8,24},{16,0},{24,8},{1,17},{9,25},{17,1},{25,9},{2,18},{10... | collective-permute-start | bytes 2162696 | tf_op jit(solution)/shard_map/ppermute | solution.py:390
  48.6 18.1 %collective-permute-start.7 = (bf16[1,2,352,1024]{3,2,1,0:T(8,128)(2,1)S(1)}, bf16[1,2,352,1024]{3,2,1,0:T(8,128)(2,1)S(1)}, u32[]{:S(2)}, u32[]{:S(2)}) collective-permute-start(bf16[1,2,352,1024]{3,2,1,0:T(8,128)(2,1)S(1)} %broadcast_select_fusion.3), channel_id=1, source_target_pairs={{0,8},{8,0},{16,24},{24,16},{1,9},{9,1},{17,25},{25,17},{2,10},{10... | collective-permute-start | bytes 4325384 | tf_op jit(solution)/shard_map/ppermute | solution.py:386
  55.8 37.4 %collective-permute-start.17 = (bf16[1,2,352,1024]{3,2,1,0:T(8,128)(2,1)S(1)}, bf16[1,2,352,1024]{3,2,1,0:T(8,128)(2,1)S(1)}, u32[]{:S(2)}, u32[]{:S(2)}) collective-permute-start(bf16[1,2,352,1024]{3,2,1,0:T(8,128)(2,1)S(1)} %broadcast_select_fusion.4), channel_id=1, source_target_pairs={{0,16},{8,24},{16,0},{24,8},{1,17},{9,25},{17,1},{25,9},{2,18},{10... | collective-permute-start | bytes 4325384 | tf_op jit(solution)/shard_map/ppermute | solution.py:390
  72.2 12.8 %collective-permute-start.12 = (bf16[64,1024]{1,0:T(8,128)(2,1)S(1)}, bf16[64,1024]{1,0:T(8,128)(2,1)S(1)}, u32[]{:S(2)}, u32[]{:S(2)}) collective-permute-start(bf16[64,1024]{1,0:T(8,128)(2,1)S(1)} %get-tuple-element.103), channel_id=1, source_target_pairs={{0,2},{1,3},{2,0},{3,1},{4,6},{5,7},{6,4},{7,5},{8,10},{9,11},{10,... | collective-permute-start | bytes 393224 | tf_op jit(solution)/shard_map/ppermute | solution.py:352
  72.5 12.5 %collective-permute-start.13 = (bf16[64,1024]{1,0:T(8,128)(2,1)S(1)}, bf16[64,1024]{1,0:T(8,128)(2,1)S(1)}, u32[]{:S(2)}, u32[]{:S(2)}) collective-permute-start(bf16[64,1024]{1,0:T(8,128)(2,1)S(1)} %get-tuple-element.104), channel_id=1, source_target_pairs={{0,1},{1,2},{2,3},{3,0},{4,5},{5,6},{6,7},{7,4},{8,9},{9,10},{10,1... | collective-permute-start | bytes 393224 | tf_op jit(solution)/shard_map/ppermute | solution.py:352
  85.8 14.0 %collective-permute-start.15 = (bf16[64,1024]{1,0:T(8,128)(2,1)S(1)}, bf16[64,1024]{1,0:T(8,128)(2,1)S(1)}, u32[]{:S(2)}, u32[]{:S(2)}) collective-permute-start(bf16[64,1024]{1,0:T(8,128)(2,1)S(1)} %get-tuple-element.106.refs_0_), channel_id=1, source_target_pairs={{0,2},{1,3},{2,0},{3,1},{4,6},{5,7},{6,4},{7,5},{8,10},{9,11},{10,... | collective-permute-start | bytes 393224 | tf_op jit(solution)/shard_map/ppermute | solution.py:345
  89.7 19.0 %collective-permute-start.19 = (bf16[1,352,1024]{2,1,0:T(8,128)(2,1)S(1)}, bf16[1,352,1024]{2,1,0:T(8,128)(2,1)S(1)}, u32[]{:S(2)}, u32[]{:S(2)}) collective-permute-start(bf16[1,352,1024]{2,1,0:T(8,128)(2,1)S(1)} %get-tuple-element.111), channel_id=1, source_target_pairs={{0,16},{8,24},{16,0},{24,8},{1,17},{9,25},{17,1},{25,9},{2,18},{10... | collective-permute-start | bytes 2162696 | tf_op jit(solution)/shard_map/ppermute | solution.py:390
  111.9 38.1 %collective-permute-start.27 = (bf16[1,2,352,1024]{3,2,1,0:T(8,128)(2,1)S(1)}, bf16[1,2,352,1024]{3,2,1,0:T(8,128)(2,1)S(1)}, u32[]{:S(2)}, u32[]{:S(2)}) collective-permute-start(bf16[1,2,352,1024]{3,2,1,0:T(8,128)(2,1)S(1)} %broadcast_select_fusion.1), channel_id=1, source_target_pairs={{0,8},{8,0},{16,24},{24,16},{1,9},{9,1},{17,25},{25,17},{2,10},{10... | collective-permute-start | bytes 4325384 | tf_op jit(solution)/shard_map/ppermute | solution.py:386
  135.6 12.4 %collective-permute-start.25 = (bf16[64,1024]{1,0:T(8,128)(2,1)S(1)}, bf16[64,1024]{1,0:T(8,128)(2,1)S(1)}, u32[]{:S(2)}, u32[]{:S(2)}) collective-permute-start(bf16[64,1024]{1,0:T(8,128)(2,1)S(1)} %get-tuple-element.118.refs_0_), channel_id=1, source_target_pairs={{0,2},{1,3},{2,0},{3,1},{4,6},{5,7},{6,4},{7,5},{8,10},{9,11},{10,... | collective-permute-start | bytes 393224 | tf_op jit(solution)/shard_map/ppermute | solution.py:345
  149.5 48.6 %collective-permute-start.38 = (bf16[1,2,352,1024]{3,2,1,0:T(8,128)(2,1)}, bf16[1,2,352,1024]{3,2,1,0:T(8,128)(2,1)}, u32[]{:S(2)}, u32[]{:S(2)}) collective-permute-start(bf16[1,2,352,1024]{3,2,1,0:T(8,128)(2,1)} %broadcast_select_fusion), channel_id=1, source_target_pairs={{0,8},{8,0},{16,24},{24,16},{1,9},{9,1},{17,25},{25,17},{2,10},{10... | collective-permute-start | bytes 4325384 | tf_op jit(solution)/shard_map/ppermute | solution.py:386
  154.5 13.5 %collective-permute-start.30 = (bf16[64,1024]{1,0:T(8,128)(2,1)S(1)}, bf16[64,1024]{1,0:T(8,128)(2,1)S(1)}, u32[]{:S(2)}, u32[]{:S(2)}) collective-permute-start(bf16[64,1024]{1,0:T(8,128)(2,1)S(1)} %get-tuple-element.123), channel_id=1, source_target_pairs={{0,2},{1,3},{2,0},{3,1},{4,6},{5,7},{6,4},{7,5},{8,10},{9,11},{10,... | collective-permute-start | bytes 393224 | tf_op jit(solution)/shard_map/ppermute | solution.py:352
  155.8 12.2 %collective-permute-start.31 = (bf16[64,1024]{1,0:T(8,128)(2,1)S(1)}, bf16[64,1024]{1,0:T(8,128)(2,1)S(1)}, u32[]{:S(2)}, u32[]{:S(2)}) collective-permute-start(bf16[64,1024]{1,0:T(8,128)(2,1)S(1)} %get-tuple-element.124), channel_id=1, source_target_pairs={{0,1},{1,2},{2,3},{3,0},{4,5},{5,6},{6,7},{7,4},{8,9},{9,10},{10,1... | collective-permute-start | bytes 393224 | tf_op jit(solution)/shard_map/ppermute | solution.py:352
  168.3 13.7 %collective-permute-start.36 = (bf16[64,1024]{1,0:T(8,128)(2,1)S(1)}, bf16[64,1024]{1,0:T(8,128)(2,1)S(1)}, u32[]{:S(2)}, u32[]{:S(2)}) collective-permute-start(bf16[64,1024]{1,0:T(8,128)(2,1)S(1)} %get-tuple-element.126.refs_0_), channel_id=1, source_target_pairs={{0,2},{1,3},{2,0},{3,1},{4,6},{5,7},{6,4},{7,5},{8,10},{9,11},{10,... | collective-permute-start | bytes 393224 | tf_op jit(solution)/shard_map/ppermute | solution.py:345
  169.9 12.7 %collective-permute-start.35 = (bf16[64,1024]{1,0:T(8,128)(2,1)S(1)}, bf16[64,1024]{1,0:T(8,128)(2,1)S(1)}, u32[]{:S(2)}, u32[]{:S(2)}) collective-permute-start(bf16[64,1024]{1,0:T(8,128)(2,1)S(1)} %get-tuple-element.126.refs_0_), channel_id=1, source_target_pairs={{0,1},{1,2},{2,3},{3,0},{4,5},{5,6},{6,7},{7,4},{8,9},{9,10},{10,1... | collective-permute-start | bytes 393224 | tf_op jit(solution)/shard_map/ppermute | solution.py:345
  184.2 18.8 %collective-permute-start.39 = (bf16[1,352,1024]{2,1,0:T(8,128)(2,1)}, bf16[1,352,1024]{2,1,0:T(8,128)(2,1)}, u32[]{:S(2)}, u32[]{:S(2)}) collective-permute-start(bf16[1,352,1024]{2,1,0:T(8,128)(2,1)} %broadcast_select_fusion.6), channel_id=1, source_target_pairs={{0,8},{8,0},{16,24},{24,16},{1,9},{9,1},{17,25},{25,17},{2,10},{10... | collective-permute-start | bytes 2162696 | tf_op jit(solution)/shard_map/ppermute | solution.py:386
  185.2 12.8 %collective-permute-start.33 = (bf16[64,1024]{1,0:T(8,128)(2,1)S(1)}, bf16[64,1024]{1,0:T(8,128)(2,1)S(1)}, u32[]{:S(2)}, u32[]{:S(2)}) collective-permute-start(bf16[64,1024]{1,0:T(8,128)(2,1)S(1)} %constant_dynamic-slice_fusion.refs_0_), channel_id=1, source_target_pairs={{0,2},{1,3},{2,0},{3,1},{4,6},{5,7},{6,4},{7,5},{8,10},{9,11},{10,... | collective-permute-start | bytes 393224 | tf_op jit(solution)/shard_map/ppermute | solution.py:345
  185.5 12.5 %collective-permute-start.32 = (bf16[64,1024]{1,0:T(8,128)(2,1)S(1)}, bf16[64,1024]{1,0:T(8,128)(2,1)S(1)}, u32[]{:S(2)}, u32[]{:S(2)}) collective-permute-start(bf16[64,1024]{1,0:T(8,128)(2,1)S(1)} %constant_dynamic-slice_fusion.refs_0_), channel_id=1, source_target_pairs={{0,1},{1,2},{2,3},{3,0},{4,5},{5,6},{6,7},{7,4},{8,9},{9,10},{10,1... | collective-permute-start | bytes 393224 | tf_op jit(solution)/shard_map/ppermute | solution.py:345
  208.5 14.0 %collective-permute-start.41 = (bf16[64,1024]{1,0:T(8,128)(2,1)S(1)}, bf16[64,1024]{1,0:T(8,128)(2,1)S(1)}, u32[]{:S(2)}, u32[]{:S(2)}) collective-permute-start(bf16[64,1024]{1,0:T(8,128)(2,1)S(1)} %get-tuple-element.132), channel_id=1, source_target_pairs={{0,2},{1,3},{2,0},{3,1},{4,6},{5,7},{6,4},{7,5},{8,10},{9,11},{10,... | collective-permute-start | bytes 393224 | tf_op jit(solution)/shard_map/ppermute | solution.py:352
  210.5 12.1 %collective-permute-start.42 = (bf16[64,1024]{1,0:T(8,128)(2,1)S(1)}, bf16[64,1024]{1,0:T(8,128)(2,1)S(1)}, u32[]{:S(2)}, u32[]{:S(2)}) collective-permute-start(bf16[64,1024]{1,0:T(8,128)(2,1)S(1)} %get-tuple-element.133), channel_id=1, source_target_pairs={{0,1},{1,2},{2,3},{3,0},{4,5},{5,6},{6,7},{7,4},{8,9},{9,10},{10,1... | collective-permute-start | bytes 393224 | tf_op jit(solution)/shard_map/ppermute | solution.py:352
  222.8 12.8 %collective-permute-start.44 = (bf16[64,1024]{1,0:T(8,128)(2,1)S(1)}, bf16[64,1024]{1,0:T(8,128)(2,1)S(1)}, u32[]{:S(2)}, u32[]{:S(2)}) collective-permute-start(bf16[64,1024]{1,0:T(8,128)(2,1)S(1)} %shard_map.156.refs_0_), channel_id=1, source_target_pairs={{0,2},{1,3},{2,0},{3,1},{4,6},{5,7},{6,4},{7,5},{8,10},{9,11},{10,... | collective-permute-start | bytes 393224 | tf_op jit(solution)/shard_map/ppermute | solution.py:345
  223.6 15.5 %collective-permute-start.43 = (bf16[64,1024]{1,0:T(8,128)(2,1)S(1)}, bf16[64,1024]{1,0:T(8,128)(2,1)S(1)}, u32[]{:S(2)}, u32[]{:S(2)}) collective-permute-start(bf16[64,1024]{1,0:T(8,128)(2,1)S(1)} %shard_map.156.refs_0_), channel_id=1, source_target_pairs={{0,1},{1,2},{2,3},{3,0},{4,5},{5,6},{6,7},{7,4},{8,9},{9,10},{10,1... | collective-permute-start | bytes 393224 | tf_op jit(solution)/shard_map/ppermute | solution.py:345
  225.5 55.6 %collective-permute-start.52 = (bf16[256,1792]{1,0:T(8,128)(2,1)S(1)}, bf16[256,1792]{1,0:T(8,128)(2,1)S(1)}, u32[]{:S(2)}, u32[]{:S(2)}) collective-permute-start(bf16[256,1792]{1,0:T(8,128)(2,1)S(1)} %copy-done.5), channel_id=1, source_target_pairs={{16,0},{24,8},{17,1},{25,9},{18,2},{26,10},{19,3},{27,11},{20,4},{... | collective-permute-start | bytes 2752520 | tf_op jit(solution)/shard_map/ppermute | solution.py:483
  226.8 54.3 %collective-permute-start.53 = (bf16[256,1792]{1,0:T(8,128)(2,1)S(1)}, bf16[256,1792]{1,0:T(8,128)(2,1)S(1)}, u32[]{:S(2)}, u32[]{:S(2)}) collective-permute-start(bf16[256,1792]{1,0:T(8,128)(2,1)S(1)} %copy-done.14), channel_id=1, source_target_pairs={{16,0},{24,8},{17,1},{25,9},{18,2},{26,10},{19,3},{27,11},{20,4},{... | collective-permute-start | bytes 2752520 | tf_op jit(solution)/shard_map/ppermute | solution.py:483
  228.5 52.6 %collective-permute-start.54 = (bf16[256,1792]{1,0:T(8,128)(2,1)S(1)}, bf16[256,1792]{1,0:T(8,128)(2,1)S(1)}, u32[]{:S(2)}, u32[]{:S(2)}) collective-permute-start(bf16[256,1792]{1,0:T(8,128)(2,1)S(1)} %copy-done.16), channel_id=1, source_target_pairs={{0,16},{8,24},{1,17},{9,25},{2,18},{10,26},{3,19},{11,27},{4,20},{... | collective-permute-start | bytes 2752520 | tf_op jit(solution)/shard_map/ppermute | solution.py:483
  235.6 45.5 %collective-permute-start.55 = (bf16[256,1792]{1,0:T(8,128)(2,1)S(1)}, bf16[256,1792]{1,0:T(8,128)(2,1)S(1)}, u32[]{:S(2)}, u32[]{:S(2)}) collective-permute-start(bf16[256,1792]{1,0:T(8,128)(2,1)S(1)} %get-tuple-element.142.refs_5_.refs_1_), channel_id=1, source_target_pairs={{0,16},{8,24},{1,17},{9,25},{2,18},{10,26},{3,19},{11,27},{4,20},{... | collective-permute-start | bytes 2752520 | tf_op jit(solution)/shard_map/ppermute | solution.py:483
  285.5 31.6 %collective-permute-start.74 = (bf16[256,1024]{1,0:T(8,128)(2,1)S(1)}, bf16[256,1024]{1,0:T(8,128)(2,1)S(1)}, u32[]{:S(2)}, u32[]{:S(2)}) collective-permute-start(bf16[256,1024]{1,0:T(8,128)(2,1)S(1)} %shard_map.153.grad_ref.refs_5_), channel_id=1, source_target_pairs={{0,16},{8,24},{1,17},{9,25},{2,18},{10,26},{3,19},{11,27},{4,20},{... | collective-permute-start | bytes 1572872 | tf_op jit(solution)/shard_map/ppermute | solution.py:483
  289.0 29.4 %collective-permute-start.63 = (bf16[256,1536]{1,0:T(8,128)(2,1)S(1)}, bf16[256,1536]{1,0:T(8,128)(2,1)S(1)}, u32[]{:S(2)}, u32[]{:S(2)}) collective-permute-start(bf16[256,1536]{1,0:T(8,128)(2,1)S(1)} %get-tuple-element.150.refs_1_), channel_id=1, source_target_pairs={{0,16},{8,24},{1,17},{9,25},{2,18},{10,26},{3,19},{11,27},{4,20},{... | collective-permute-start | bytes 2359304 | tf_op jit(solution)/shard_map/ppermute | solution.py:483
  293.3 33.2 %collective-permute-start.62 = (bf16[256,1536]{1,0:T(8,128)(2,1)S(1)}, bf16[256,1536]{1,0:T(8,128)(2,1)S(1)}, u32[]{:S(2)}, u32[]{:S(2)}) collective-permute-start(bf16[256,1536]{1,0:T(8,128)(2,1)S(1)} %get-tuple-element.149.refs_0_), channel_id=1, source_target_pairs={{16,0},{24,8},{17,1},{25,9},{18,2},{26,10},{19,3},{27,11},{20,4},{... | collective-permute-start | bytes 2359304 | tf_op jit(solution)/shard_map/ppermute | solution.py:483
  304.3 19.5 %collective-permute-start.73 = (bf16[256,1024]{1,0:T(8,128)(2,1)S(1)}, bf16[256,1024]{1,0:T(8,128)(2,1)S(1)}, u32[]{:S(2)}, u32[]{:S(2)}) collective-permute-start(bf16[256,1024]{1,0:T(8,128)(2,1)S(1)} %shard_map.160.grad_ref.refs_4_), channel_id=1, source_target_pairs={{16,0},{24,8},{17,1},{25,9},{18,2},{26,10},{19,3},{27,11},{20,4},{... | collective-permute-start | bytes 1572872 | tf_op jit(solution)/shard_map/ppermute | solution.py:483
  312.4 16.5 %collective-permute-start.71 = (bf16[256,1024]{1,0:T(8,128)(2,1)S(1)}, bf16[256,1024]{1,0:T(8,128)(2,1)S(1)}, u32[]{:S(2)}, u32[]{:S(2)}) collective-permute-start(bf16[256,1024]{1,0:T(8,128)(2,1)S(1)} %shard_map.157.grad_ref.refs_5_), channel_id=1, source_target_pairs={{0,16},{8,24},{1,17},{9,25},{2,18},{10,26},{3,19},{11,27},{4,20},{... | collective-permute-start | bytes 1572872 | tf_op jit(solution)/shard_map/ppermute | solution.py:483
  317.1 12.5 %collective-permute-start.70 = (bf16[256,1024]{1,0:T(8,128)(2,1)S(1)}, bf16[256,1024]{1,0:T(8,128)(2,1)S(1)}, u32[]{:S(2)}, u32[]{:S(2)}) collective-permute-start(bf16[256,1024]{1,0:T(8,128)(2,1)S(1)} %shard_map.163.grad_ref.refs_4_), channel_id=1, source_target_pairs={{16,0},{24,8},{17,1},{25,9},{18,2},{26,10},{19,3},{27,11},{20,4},{... | collective-permute-start | bytes 1572872 | tf_op jit(solution)/shard_map/ppermute | solution.py:483
  324.8 37.2 %collective-permute-start.75 = (bf16[2,1,1,352,1024]{4,3,2,1,0:T(8,128)(2,1)S(1)}, bf16[2,1,1,352,1024]{4,3,2,1,0:T(8,128)(2,1)S(1)}, u32[]{:S(2)}, u32[]{:S(2)}) collective-permute-start(bf16[2,1,1,352,1024]{4,3,2,1,0:T(8,128)(2,1)S(1)} %bitcast.66), channel_id=1, source_target_pairs={{0,8},{16,24},{1,9},{17,25},{2,10},{18,26},{3,11},{19,27},{4,12},{... | collective-permute-start | bytes 4325384 | tf_op jit(solution)/shard_map/ppermute | solution.py:394
  330.6 33.5 %collective-permute-start.72 = (bf16[2,1,1,352,1024]{4,3,2,1,0:T(8,128)(2,1)S(1)}, bf16[2,1,1,352,1024]{4,3,2,1,0:T(8,128)(2,1)S(1)}, u32[]{:S(2)}, u32[]{:S(2)}) collective-permute-start(bf16[2,1,1,352,1024]{4,3,2,1,0:T(8,128)(2,1)S(1)} %bitcast.68), channel_id=1, source_target_pairs={{8,0},{24,16},{9,1},{25,17},{10,2},{26,18},{11,3},{27,19},{12,4},{... | collective-permute-start | bytes 4325384 | tf_op jit(solution)/shard_map/ppermute | solution.py:394
  331.9 19.1 %collective-permute-start.65 = (bf16[256,1536]{1,0:T(8,128)(2,1)S(1)}, bf16[256,1536]{1,0:T(8,128)(2,1)S(1)}, u32[]{:S(2)}, u32[]{:S(2)}) collective-permute-start(bf16[256,1536]{1,0:T(8,128)(2,1)S(1)} %get-tuple-element.155.refs_1_), channel_id=1, source_target_pairs={{0,16},{8,24},{1,17},{9,25},{2,18},{10,26},{3,19},{11,27},{4,20},{... | collective-permute-start | bytes 2359304 | tf_op jit(solution)/shard_map/ppermute | solution.py:483
  333.5 22.2 %collective-permute-start.64 = (bf16[256,1536]{1,0:T(8,128)(2,1)S(1)}, bf16[256,1536]{1,0:T(8,128)(2,1)S(1)}, u32[]{:S(2)}, u32[]{:S(2)}) collective-permute-start(bf16[256,1536]{1,0:T(8,128)(2,1)S(1)} %shard_map.165.refs_0_), channel_id=1, source_target_pairs={{16,0},{24,8},{17,1},{25,9},{18,2},{26,10},{19,3},{27,11},{20,4},{... | collective-permute-start | bytes 2359304 | tf_op jit(solution)/shard_map/ppermute | solution.py:483
  334.8 31.8 %collective-permute-start.79 = (bf16[2,1,1,352,1024]{4,3,2,1,0:T(8,128)(2,1)S(1)}, bf16[2,1,1,352,1024]{4,3,2,1,0:T(8,128)(2,1)S(1)}, u32[]{:S(2)}, u32[]{:S(2)}) collective-permute-start(bf16[2,1,1,352,1024]{4,3,2,1,0:T(8,128)(2,1)S(1)} %bitcast.77), channel_id=1, source_target_pairs={{0,8},{16,24},{1,9},{17,25},{2,10},{18,26},{3,11},{19,27},{4,12},{... | collective-permute-start | bytes 4325384 | tf_op jit(solution)/shard_map/ppermute | solution.py:394
  357.4 14.6 %collective-permute-start.78 = (bf16[2,1,1,352,1024]{4,3,2,1,0:T(8,128)(2,1)S(1)}, bf16[2,1,1,352,1024]{4,3,2,1,0:T(8,128)(2,1)S(1)}, u32[]{:S(2)}, u32[]{:S(2)}) collective-permute-start(bf16[2,1,1,352,1024]{4,3,2,1,0:T(8,128)(2,1)S(1)} %bitcast.81), channel_id=1, source_target_pairs={{8,0},{24,16},{9,1},{25,17},{10,2},{26,18},{11,3},{27,19},{12,4},{... | collective-permute-start | bytes 4325384 | tf_op jit(solution)/shard_map/ppermute | solution.py:394
  358.7 17.0 %collective-permute-start.67 = (bf16[2,1,1,352,1024]{4,3,2,1,0:T(8,128)(2,1)S(1)}, bf16[2,1,1,352,1024]{4,3,2,1,0:T(8,128)(2,1)S(1)}, u32[]{:S(2)}, u32[]{:S(2)}) collective-permute-start(bf16[2,1,1,352,1024]{4,3,2,1,0:T(8,128)(2,1)S(1)} %bitcast.75), channel_id=1, source_target_pairs={{0,8},{16,24},{1,9},{17,25},{2,10},{18,26},{3,11},{19,27},{4,12},{... | collective-permute-start | bytes 4325384 | tf_op jit(solution)/shard_map/ppermute | solution.py:394
  362.0 18.0 %collective-permute-start.66 = (bf16[2,1,1,352,1024]{4,3,2,1,0:T(8,128)(2,1)S(1)}, bf16[2,1,1,352,1024]{4,3,2,1,0:T(8,128)(2,1)S(1)}, u32[]{:S(2)}, u32[]{:S(2)}) collective-permute-start(bf16[2,1,1,352,1024]{4,3,2,1,0:T(8,128)(2,1)S(1)} %bitcast.79), channel_id=1, source_target_pairs={{8,0},{24,16},{9,1},{25,17},{10,2},{26,18},{11,3},{27,19},{12,4},{... | collective-permute-start | bytes 4325384 | tf_op jit(solution)/shard_map/ppermute | solution.py:394
  364.0 19.7 %collective-permute-start.77 = (bf16[1,704,1024]{2,1,0:T(8,128)(2,1)S(1)}, bf16[1,704,1024]{2,1,0:T(8,128)(2,1)S(1)}, u32[]{:S(2)}, u32[]{:S(2)}) collective-permute-start(bf16[1,704,1024]{2,1,0:T(8,128)(2,1)S(1)} %shard_map.172.refs_1_), channel_id=1, source_target_pairs={{8,12},{12,8},{24,28},{28,24},{9,13},{13,9},{25,29},{29,25},{10,14... | collective-permute-start | bytes 4325384 | tf_op jit(solution)/shard_map/ppermute | solution.py:538
  366.7 36.7 %collective-permute-start.76 = (bf16[1,704,1024]{2,1,0:T(8,128)(2,1)}, bf16[1,704,1024]{2,1,0:T(8,128)(2,1)}, u32[]{:S(2)}, u32[]{:S(2)}) collective-permute-start(bf16[1,704,1024]{2,1,0:T(8,128)(2,1)} %shard_map.170.refs_0_), channel_id=1, source_target_pairs={{0,4},{4,0},{16,20},{20,16},{1,5},{5,1},{17,21},{21,17},{2,6},{6,2... | collective-permute-start | bytes 4325384 | tf_op jit(solution)/shard_map/ppermute | solution.py:538
  372.0 39.5 %collective-permute-start.81 = (bf16[1,704,1024]{2,1,0:T(8,128)(2,1)}, bf16[1,704,1024]{2,1,0:T(8,128)(2,1)}, u32[]{:S(2)}, u32[]{:S(2)}) collective-permute-start(bf16[1,704,1024]{2,1,0:T(8,128)(2,1)} %shard_map.175.refs_1_), channel_id=1, source_target_pairs={{8,12},{12,8},{24,28},{28,24},{9,13},{13,9},{25,29},{29,25},{10,14... | collective-permute-start | bytes 4325384 | tf_op jit(solution)/shard_map/ppermute | solution.py:538
  375.8 58.4 %collective-permute-start.80 = (bf16[1,704,1024]{2,1,0:T(8,128)(2,1)}, bf16[1,704,1024]{2,1,0:T(8,128)(2,1)}, u32[]{:S(2)}, u32[]{:S(2)}) collective-permute-start(bf16[1,704,1024]{2,1,0:T(8,128)(2,1)} %shard_map.174.refs_0_), channel_id=1, source_target_pairs={{0,4},{4,0},{16,20},{20,16},{1,5},{5,1},{17,21},{21,17},{2,6},{6,2... | collective-permute-start | bytes 4325384 | tf_op jit(solution)/shard_map/ppermute | solution.py:538
  380.0 62.4 %collective-permute-start.69 = (bf16[1,704,1024]{2,1,0:T(8,128)(2,1)}, bf16[1,704,1024]{2,1,0:T(8,128)(2,1)}, u32[]{:S(2)}, u32[]{:S(2)}) collective-permute-start(bf16[1,704,1024]{2,1,0:T(8,128)(2,1)} %shard_map.168.refs_1_), channel_id=1, source_target_pairs={{8,12},{12,8},{24,28},{28,24},{9,13},{13,9},{25,29},{29,25},{10,14... | collective-permute-start | bytes 4325384 | tf_op jit(solution)/shard_map/ppermute | solution.py:538
  384.8 77.7 %collective-permute-start.68 = (bf16[1,704,1024]{2,1,0:T(8,128)(2,1)}, bf16[1,704,1024]{2,1,0:T(8,128)(2,1)}, u32[]{:S(2)}, u32[]{:S(2)}) collective-permute-start(bf16[1,704,1024]{2,1,0:T(8,128)(2,1)} %shard_map.167.refs_0_), channel_id=1, source_target_pairs={{0,4},{4,0},{16,20},{20,16},{1,5},{5,1},{17,21},{21,17},{2,6},{6,2... | collective-permute-start | bytes 4325384 | tf_op jit(solution)/shard_map/ppermute | solution.py:538
  (83 other events, 1068.4 us)
